TPU v7x, 128 devices: a whole 4x4x4 slice. The times are simulated.
128 devices in a mesh: attn: 4 (over x), expert: 32 (over z, y, core).
Axes of the slice: x: 4, y: 4, z: 4, core: 2. Of those that a mesh axis runs over, the one named last changes fastest.
Arguments:
- tokens: bfloat16 [4096, 2880], P(('attn', 'expert')), may hold values from -6 to 6
- expert_ids: int32 [4096, 4], P(('attn', 'expert')), may hold values from 0 to 31, all different within a row; in each aligned block of 32 rows (0 to 31, 32 to 63, ...) at most 12 rows name the same one
- gate_probs: float32 [4096, 4], P(('attn', 'expert')), may hold values from 0.05 to 0.6
- shed_blocks: int32 [32], replicated, may hold values from 0 to 4, as said below
- partner: int32 [32], replicated, may hold values from 0 to 31, as said below
- gate_weight: bfloat16 [32, 2880, 2880], P('expert', None, 'attn'), may hold values from -0.109375 to 0.109375
- up_weight: bfloat16 [32, 2880, 2880], P('expert', None, 'attn'), may hold values from -0.109375 to 0.109375
- down_weight: bfloat16 [32, 2880, 2880], P('expert', 'attn'), may hold values from -0.109375 to 0.109375
Outputs:
- moe_out: bfloat16 [4096, 2880], P(('attn', 'expert'))
Inputs may be any that keep to these rules, and one draw needn't show every extreme that they name: `expert_ids`: in the rows of one device, no expert is named by more than 12 rows; the 4 experts of a token differ. `shed_blocks`: some expert has exactly 4. partner pairs the experts: partner[partner[e]] = e and partner[e] != e.
All inputs are finite; a program needn't handle non-finite values.
Results may differ from a plain program's by a relative error of at most 0.0081.
Values may be sent and summed in bfloat16 or wider, within the bound.
No kernel may reach another device: no remote copies, remote signals or barrier semaphores. Data moves between devices by JAX's collectives and lax.ppermute only.
A program may use at most 128 MiB of HBM per device.

v0:
```python
import jax
import jax.numpy as jnp
from jax import lax
from jax.experimental import pallas as pl
from jax.experimental.pallas import tpu as pltpu
from jax.sharding import Mesh
from jax.sharding import PartitionSpec as P

SHED_MOST = 4
ATTN_EXPERT = ("attn", "expert_0", "expert_1", "expert_2")
EXPERT = ("expert_0", "expert_1", "expert_2")
SWISH_SCALE = 1.702
BF = jnp.bfloat16
F32 = jnp.float32


def iota(shape, dim):
    return lax.broadcasted_iota(jnp.int32, shape, dim)


def dot(a, b, dims=((1,), (0,))):
    return lax.dot_general(a, b, (dims, ((), ())), preferred_element_type=F32)


def half(n):
    return (n // 2 + 15) // 16 * 16


def hot(places, width, first=0):
    at = (iota((places.shape[0], width), 1) + first).astype(F32)
    return jnp.where(places == at, 1.0, 0.0)


def send_kernel(lay, x_ref, id_ref, s_ref, seen_ref):
    tok, experts, seats = x_ref.shape[0], lay.experts, lay.seats
    seen_ref[...] = jnp.zeros_like(seen_ref)
    ids = id_ref[...].astype(F32)
    expert = iota((experts, tok), 0).astype(F32)
    hits = jnp.zeros((experts, tok), F32)
    for k in range(ids.shape[0]):
        hits += jnp.where(ids[k : k + 1] == expert, 1.0, 0.0)
    earlier = (iota((tok, tok), 0) < iota((tok, tok), 1)).astype(BF)
    order = dot(hits.astype(BF), earlier)
    order = jnp.where(hits > 0.5, order, -1.0).astype(BF)
    rows = experts * seats
    spread = (iota((rows, experts), 0) // seats == iota((rows, experts), 1)).astype(BF)
    order = dot(spread, order)
    seat = iota((rows, tok), 0) % seats
    over = (seats + seat // 2).astype(F32)
    full = jnp.where(order == seat.astype(F32), 1.0, 0.0).astype(BF)
    part = jnp.where(order == over, 1.0, 0.0)
    even = jnp.where(seat % 2 == 0, part, 0.0).astype(BF)
    odd = jnp.where(seat % 2 == 1, part, 0.0).astype(BF)
    one, none = jnp.ones((tok, 1), BF), lambda n: jnp.zeros((tok, n), BF)
    second = jnp.concatenate([none(lay.width + 1), one, none(lay.low - lay.width - 2)], axis=1)
    flags = dot(part.astype(BF), second)
    for b in range(x_ref.shape[1] // lay.width):
        first = b * lay.width
        x = x_ref[:, first : first + lay.width]
        at = slice(b * rows, (b + 1) * rows)
        wide = jnp.concatenate([x, one, none(lay.low - lay.width - 1)], axis=1)
        s_ref[at, : lay.low] = (dot(full, wide) + flags).astype(BF)
        tail = jnp.concatenate([x[:, lay.point :], none(lay.short)], axis=1)
        s_ref[at, lay.low :] = (dot(even, x[:, : lay.point]) + dot(odd, tail)).astype(BF)


def gather_slots(lay, rows, x_ref, first, outs):
    slots = outs[0].shape[1]
    place = (iota((slots, x_ref.shape[0]), 0) + first).astype(F32)
    match = lambda row: jnp.where(row == place, 1.0, 0.0).astype(BF)
    got = dot(match(rows[0]), x_ref[:, : lay.width])
    rest = x_ref[:, lay.low :]
    left, right = dot(match(rows[1]), rest), dot(match(rows[2]), rest)
    extra = jnp.concatenate([left, right[:, : lay.width - lay.point]], axis=1)
    share_out((got + extra).astype(BF).T, outs)


def pick_more_kernel(lay, first, x_ref, row_ref, *outs):
    gather_slots(lay, [row_ref[k : k + 1] for k in range(3)], x_ref, first, outs)


def pick_kernel(lay, x_ref, par_ref, row_ref, col_ref, *outs):
    came, seats = x_ref.shape[0], lay.seats
    sources = came // seats
    bound = par_ref[0].astype(F32)
    start = lay.width // 128 * 128
    tail = x_ref[:, start : lay.low]
    choose = (iota((8, tail.shape[1]), 1) == iota((8, tail.shape[1]), 0) + lay.width - start)
    flags = dot(choose.astype(BF), tail, ((1,), (1,)))
    full, part = flags[0:1], flags[1:2]
    seat = iota((1, came), 1) % seats
    even = seat % 2 == 0
    owner = iota((sources, came), 0) == iota((sources, came), 1) // seats
    each = full + jnp.where(even, part, 0.0)
    counts = jnp.sum(jnp.where(owner, each, 0.0), axis=1, keepdims=True)
    counts = jnp.broadcast_to(counts, (sources, 128)).astype(BF)
    earlier = (iota((sources, sources), 1) < iota((sources, sources), 0)).astype(BF)
    before = dot(earlier, counts)[:, 0:1]
    base = jnp.sum(jnp.where(owner, before, 0.0), axis=0, keepdims=True)
    rank = base + seat.astype(F32)
    over = base + (seats + seat // 2).astype(F32)
    rank = jnp.where(jnp.logical_and(full > 0.5, rank < bound), rank, -1.0)
    over = jnp.where(jnp.logical_and(part > 0.5, over < bound), over, -1.0)
    evens, odds = jnp.where(even, over, -1.0), jnp.where(even, -1.0, over)
    nothing = jnp.full((5, came), -1.0, F32)
    every = jnp.concatenate([rank, evens, odds, nothing], axis=0)
    row_ref[...] = every
    col_ref[...] = every.T
    gather_slots(lay, (rank, evens, odds), x_ref, 0, outs)


def whole(*parts):
    return jnp.concatenate([part[...] for part in parts], axis=0)


def relay_kernel(seen_ref, g_ref, u_ref, d_ref, go_ref, uo_ref, do_ref):
    del seen_ref
    blocks, width = go_ref.shape[0], go_ref.shape[2]
    for b in range(blocks):
        at = slice(b * width, (b + 1) * width)
        go_ref[b] = g_ref[:, at]
        uo_ref[b] = u_ref[:, at]
        do_ref[b] = d_ref[:, at].T


def mid_kernel(at_ref, oh, ol, lh, ll, rh, rl, ga, gb, gc, ua, ub, uc, g_ref, u_ref):
    del at_ref
    gate = up = None
    for n, (x, g, u) in enumerate(
        ((whole(oh, ol), ga, ua), (whole(lh, ll), gb, ub), (whole(rh, rl), gc, uc))
    ):
        g, u = dot(g[0], x), dot(u[0], x)
        gate, up = (g, u) if n == 0 else (gate + g, up + u)
    g_ref[...] = gate
    u_ref[...] = up


def share_out(values, refs):
    first = 0
    for ref in refs:
        ref[...] = values[first : first + ref.shape[0]].astype(ref.dtype)
        first += ref.shape[0]


def far_kernel(at_ref, g_ref, u_ref, fh, fl, wg_ref, wu_ref, wd_ref, h_ref, *outs):
    del at_ref
    x = whole(fh, fl)
    gate = g_ref[...] + dot(wg_ref[0], x)
    up = u_ref[...] + dot(wu_ref[0], x)
    hidden = (gate * jax.nn.sigmoid(SWISH_SCALE * gate) * (up + 1.0)).astype(BF)
    h_ref[...] = hidden
    share_out(dot(wd_ref[0], hidden), outs)


def near_kernel(at_ref, h_ref, da, db, dc, *outs):
    del at_ref
    hidden = h_ref[...]
    share_out(dot(db[0], hidden), outs[0:2])
    share_out(dot(dc[0], hidden), outs[2:4])
    share_out(dot(da[0], hidden), outs[4:5])


def place_kernel(lay, slot_ref, *refs):
    ins, z_ref = refs[:-1], refs[-1]
    columns = []
    for own, lh, ll, rh, rl in (ins[:5], ins[5:]):
        total = own[...] + whole(lh, ll).astype(F32) + whole(rh, rl).astype(F32)
        columns.append(total.astype(BF))
    y = jnp.concatenate(columns, axis=1)
    slots, came = y.shape[1], z_ref.shape[0]
    at = lambda k: hot(slot_ref[:, k : k + 1], slots).astype(BF)
    none = lambda n: jnp.zeros((came, n), BF)
    rows = dot(at(0), y, ((1,), (1,))).astype(BF)
    z_ref[:, : lay.low] = jnp.concatenate([rows, none(lay.low - lay.width)], axis=1)
    left = dot(at(1), y[: lay.point], ((1,), (1,))).astype(BF)
    right = dot(at(2), y[lay.point :], ((1,), (1,))).astype(BF)
    z_ref[:, lay.low :] = left + jnp.concatenate([right, none(lay.short)], axis=1)


def mix_kernel(lay, b_ref, id_ref, p_ref, o_ref):
    tok, seats = o_ref.shape[0], lay.seats
    ids, prob = id_ref[...].astype(F32).T, p_ref[...].T
    top = ids.shape[1]
    lane = iota((tok, lay.experts), 1).astype(F32)
    named = [ids[:, k : k + 1] == lane for k in range(top)]
    hits = jnp.zeros((tok, lay.experts), F32)
    for k in range(top):
        hits += jnp.where(named[k], 1.0, 0.0)
    earlier = (iota((tok, tok), 1) < iota((tok, tok), 0)).astype(BF)
    order = dot(earlier, hits.astype(BF))
    rows = lay.experts * seats
    kinds = [jnp.zeros((tok, rows), F32) for _ in range(3)]
    for k in range(top):
        seat = jnp.sum(jnp.where(named[k], order, 0.0), axis=1, keepdims=True)
        base = ids[:, k : k + 1] * seats
        full = jnp.where(seat < seats, base + seat, -1.0)
        over = jnp.where(seat < seats, -1.0, base + 2.0 * (seat - seats))
        odd = jnp.where(seat < seats, -1.0, over + 1.0)
        for n, place in enumerate((full, over, odd)):
            kinds[n] += hot(place, rows) * prob[:, k : k + 1]
    weights = []
    for kind in kinds:
        high = kind.astype(BF)
        rest = kind - high.astype(F32)
        middle = rest.astype(BF)
        low = (rest - middle.astype(F32)).astype(BF)
        weights.append(jnp.concatenate([high, middle, low], axis=0))

    def weighted(n, block):
        three = dot(weights[n], block)
        return three[:tok] + three[tok : 2 * tok] + three[2 * tok :]

    for b in range(o_ref.shape[1] // lay.width):
        at = slice(b * rows, (b + 1) * rows)
        whole_rows = weighted(0, b_ref[at, : lay.width])
        rest = b_ref[at, lay.low :]
        left, right = weighted(1, rest), weighted(2, rest)
        extra = jnp.concatenate([left, right[:, : lay.width - lay.point]], axis=1)
        o_ref[:, b * lay.width : (b + 1) * lay.width] = (whole_rows + extra).astype(BF)


VMEM = pl.BlockSpec(memory_space=pltpu.VMEM)
SMEM = pl.BlockSpec(memory_space=pltpu.SMEM)
ANY = pl.BlockSpec(memory_space=pl.ANY)
shape = jax.ShapeDtypeStruct


class Layout:
    def __init__(self, width, experts, most):
        self.width, self.experts = width, experts
        self.seats = 8
        self.low = (width + 2 + 127) // 128 * 128
        self.point = (width // 2 + 127) // 128 * 128
        self.short = 2 * self.point - width
        self.lanes = self.low + self.point
        assert self.seats <= most <= self.seats * 3 // 2


def cost(flops, moved):
    return pl.CostEstimate(flops=flops, bytes_accessed=moved, transcendentals=0)


def grant(mebibytes):
    return pltpu.CompilerParams(vmem_limit_bytes=mebibytes << 20)


def run(kernel, ins, outs, work, scratch=(), mebibytes=24):
    return pl.pallas_call(
        kernel,
        out_shape=outs,
        in_specs=ins,
        out_specs=jax.tree.map(lambda _: VMEM, outs),
        scratch_shapes=scratch,
        cost_estimate=cost(*work),
        compiler_params=grant(mebibytes),
    )


def on_device(
    tokens, expert_ids, gate_probs, shed_blocks, partner, gate_weight, up_weight, down_weight
):
    tok, model = tokens.shape
    top = expert_ids.shape[1]
    experts = shed_blocks.shape[0]
    groups = lax.axis_size("attn")
    width = model // groups
    capacity = tok * top * groups
    block = capacity // 8
    slots = capacity + block * SHED_MOST
    units = gate_weight.shape[2]
    lay = Layout(width, experts, min(tok, 3 * tok * top // experts))
    cut = half(width)
    rest = width - cut
    devices = groups * experts
    came = devices * lay.seats
    me = lax.axis_index(EXPERT)
    bound = capacity - block * shed_blocks[partner[me]] + block * shed_blocks[me]
    par = bound.reshape(1).astype(jnp.int32)
    at = lax.axis_index("attn").astype(jnp.int32).reshape(1)

    def shifted(distance):
        pairs = [(i, (i + distance) % groups) for i in range(groups)]
        return lambda array: lax.ppermute(array, "attn", pairs)

    right, left = shifted(1), shifted(groups - 1)

    def exchange(rows):
        blocks = rows.reshape(devices, lay.seats, lay.lanes)
        moved = lax.all_to_all(blocks, ATTN_EXPERT, split_axis=0, concat_axis=0, tiled=True)
        return moved.reshape(came, lay.lanes)

    packed = shape((came, lay.lanes), BF)
    outgoing, seen = run(
        lambda *refs: send_kernel(lay, *refs),
        [VMEM] * 2,
        (packed, shape((8, 128), F32)),
        (2 * tok * came * width, 2 * came * width),
        mebibytes=60,
    )(tokens, expert_ids.T)
    arrived = exchange(outgoing)
    relaid = shape((groups, units, width), BF)
    step = 128
    rows_in = pl.BlockSpec((step, model), lambda i: (i, 0))
    rows_out = pl.BlockSpec((groups, step, width), lambda i: (0, i, 0))
    wg, wu, wd = pl.pallas_call(
        relay_kernel,
        grid=(pl.cdiv(units, step),),
        out_shape=(relaid, relaid, shape((groups, width, units), BF)),
        in_specs=[ANY] + [rows_in] * 3,
        out_specs=(rows_out, rows_out, pl.BlockSpec((groups, width, step), lambda i: (0, 0, i))),
        cost_estimate=cost(12 * slots * width * units, 12 * model * units),
        compiler_params=grant(60),
        name="relay",
    )(seen, gate_weight[0].T, up_weight[0].T, down_weight[0])
    arrived, wg, wu, wd = lax.optimization_barrier((arrived, wg, wu, wd))

    tile = 256
    parts = (tile, slots - tile)
    gather_work = (2 * slots * came * width, 2 * came * width)
    pieces = [tuple(shape((n, p), BF) for n in (cut, rest)) for p in parts]
    places, slot, *own = run(
        lambda *refs: pick_kernel(lay, *refs),
        [VMEM, SMEM],
        (shape((8, came), F32), shape((came, 8), F32), *pieces[0]),
        gather_work,
    )(arrived, par)
    more = run(
        lambda *refs: pick_more_kernel(lay, parts[0], *refs), [VMEM] * 2, pieces[1], gather_work
    )(arrived, places)
    lane = lambda rows: pl.BlockSpec((rows, tile), lambda i, p: (0, i))

    def weight(rows, columns, ahead):
        return pl.BlockSpec((1, rows, columns), lambda i, p: (lax.rem(p[0] + ahead, groups), 0, 0))

    def staged(kernel, ins, outs, flops, moved):
        return pl.pallas_call(
            kernel,
            grid_spec=pltpu.PrefetchScalarGridSpec(
                num_scalar_prefetch=1,
                grid=(outs[0].shape[1] // tile,),
                in_specs=ins,
                out_specs=tuple(lane(out.shape[0]) for out in outs),
            ),
            out_shape=outs,
            cost_estimate=cost(flops, moved),
            compiler_params=grant(32),
        )

    before, after, across = groups - 1, 1, groups // 2
    halves = [lane(cut), lane(rest)]
    opposite = weight(units, width, across)
    area = width * units

    def ring(part, oh, ol):
        rows = lambda n, kind: shape((n, part), kind)
        ll, rh = right(ol), left(oh)
        lh, rl = right(oh), left(ol)
        fl, fh = right(ll), left(rh)
        gate, up = staged(
            mid_kernel,
            halves * 3 + [weight(units, width, d) for d in (0, before, after)] * 2,
            (rows(units, F32), rows(units, F32)),
            12 * part * area,
            12 * area,
        )(at, oh, ol, lh, ll, rh, rl, wg, wg, wg, wu, wu, wu)
        return gate, up, fh, fl

    def far(part, gate, up, fh, fl):
        rows = lambda n, kind: shape((n, part), kind)
        return staged(
            far_kernel,
            [lane(units)] * 2 + halves + [opposite, opposite, weight(width, units, across)],
            (rows(units, BF), rows(cut, BF), rows(rest, BF)),
            6 * part * area,
            6 * area,
        )(at, gate, up, fh, fl, wg, wu, wd)

    def near(part, hidden):
        rows = lambda n, kind: shape((n, part), kind)
        return staged(
            near_kernel,
            [lane(units)] + [weight(width, units, d) for d in (0, before, after)],
            (rows(cut, F32), rows(rest, BF), rows(cut, BF), rows(rest, F32), rows(width, F32)),
            6 * part * area,
            6 * area,
        )(at, hidden, wd, wd, wd)

    def add(mine, came):
        return (mine + came.astype(F32)).astype(BF)

    first = ring(parts[0], *own)
    second = ring(parts[1], *more)
    first, ready = lax.optimization_barrier((first, second[:2]))
    second = (*ready, *second[2:])
    hidden_a, high_a, low_a = far(parts[0], *first)
    to_right_a, to_left_a = right(low_a), left(high_a)
    lha, lla, rha, rla, own_a = near(parts[0], hidden_a)
    straight_a = right(rha), left(lla)
    hidden_b, high_b, low_b = far(parts[1], *second)
    to_right_b, to_left_b = right(low_b), left(high_b)
    sum_right, sum_left = add(rla, to_right_a), add(lha, to_left_a)
    added_a = right(sum_right), left(sum_left)
    sums_a = own_a, straight_a[0], *added_a, straight_a[1]
    lhb, llb, rhb, rlb, own_b = near(parts[1], hidden_b)
    straight_b = right(rhb), left(llb)
    sums_b = (
        own_b,
        straight_b[0],
        right(add(rlb, to_right_b)),
        left(add(lhb, to_left_b)),
        straight_b[1],
    )
    sums = sums_a + sums_b
    answers = run(
        lambda *refs: place_kernel(lay, *refs), [VMEM] * 11, packed, gather_work
    )(slot, *sums)
    return run(
        lambda *refs: mix_kernel(lay, *refs),
        [VMEM] * 3,
        shape((tok, model), BF),
        (6 * tok * came * width, 2 * came * width),
    )(exchange(answers), expert_ids.T, gate_probs.T)


def solution(mesh):
    split = Mesh(
        mesh.devices.reshape(mesh.shape["attn"], 4, 4, 2),
        ("attn", "expert_0", "expert_1", "expert_2"),
    )
    return jax.shard_map(
        on_device,
        mesh=split,
        in_specs=(
            P(ATTN_EXPERT, None),
            P(ATTN_EXPERT, None),
            P(ATTN_EXPERT, None),
            P(),
            P(),
            P(EXPERT, None, "attn"),
            P(EXPERT, None, "attn"),
            P(EXPERT, "attn", None),
        ),
        out_specs=P(ATTN_EXPERT, None),
        check_vma=False,
    )
```

profile of v0, /device:TPU:0, one launch (start us, length us, event | category | flops | bytes accessed | tf_op | source)
XLA Modules:
  0.0 190.4 jit_solution(16977121887836702931)
XLA Ops:
  0.0 3.6 %shard_map.82 = (bf16[1024,1152]{1,0:T(8,128)(2,1)}, f32[8,128]{1,0:T(8,128)}) custom-call(bf16[32,2880]{1,0:T(8,128)(2,1)} %refs_0_.1, s32[4,32]{1,0:T(4,128)} %bitcast.23), custom_call_target="tpu_custom_call" | custom-call | flops 47185920 | bytes 1474560 | tf_op jit(solution)/shard_map/pallas_call | solution.py:293
  3.6 11.2 %all-to-all-start = ((bf16[128,8,1152]{2,1,0:T(8,128)(2,1)}), bf16[128,8,1152]{2,1,0:T(8,128)(2,1)S(1)}, u32[]{:S(2)}, u32[]{:S(2)}) async-start(bf16[128,8,1152]{2,1,0:T(8,128)(2,1)} %bitcast.26), calls=%async_computation | async-start | bytes 4718592 | tf_op jit(solution)/shard_map/all_to_all | solution.py:289
  14.8 0.6 dynamic_slice.9
  17.3 0.7 fusion
  19.3 13.3 %relay.1 = (bf16[4,720,720]{2,1,0:T(8,128)(2,1)}, bf16[4,720,720]{2,1,0:T(8,128)(2,1)}, bf16[4,720,720]{2,1,0:T(8,128)(2,1)}) custom-call(f32[8,128]{1,0:T(8,128)} %get-tuple-element.47.seen_ref, bf16[720,2880]{1,0:T(8,128)(2,1)} %bitcast.27, bf16[720,2880]{1,0:T(8,128)(2,1)} %bitcast.28, bf16[720,2880]{1,0:T(8,128)(2,1)} %bitcast.29), custom_call_target="tpu_custom_call" | custom-call | flops 4777574400 | bytes 24883200 | tf_op jit(solution)/shard_map/relay/pallas_call | solution.py:305
  32.6 15.4 %all-to-all-done = bf16[128,8,1152]{2,1,0:T(8,128)(2,1)S(1)} async-done(((bf16[128,8,1152]{2,1,0:T(8,128)(2,1)}), bf16[128,8,1152]{2,1,0:T(8,128)(2,1)S(1)}, u32[]{:S(2)}, u32[]{:S(2)}) %all-to-all-start) | async-done | bytes 2359328 | tf_op jit(solution)/shard_map/all_to_all | solution.py:289
  48.0 2.3 %shard_map.83 = (f32[8,1024]{1,0:T(8,128)S(1)}, f32[1024,8]{1,0:T(8,128)S(1)}, bf16[368,256]{1,0:T(8,128)(2,1)}, bf16[352,256]{1,0:T(8,128)(2,1)S(1)}) custom-call(bf16[1024,1152]{1,0:T(8,128)(2,1)S(1)} %bitcast.21, s32[1]{0:T(128)S(6)} %add.33.refs_1_), custom_call_target="tpu_custom_call" | custom-call | flops 1132462080 | bytes 1474560 | tf_op jit(solution)/shard_map/pallas_call | solution.py:321
  50.3 0.5 collective-permute-start.1
  50.8 2.7 %collective-permute-start.3 = (bf16[352,256]{1,0:T(8,128)(2,1)S(1)}, bf16[352,256]{1,0:T(8,128)(2,1)S(1)}, u32[]{:S(2)}, u32[]{:S(2)}) collective-permute-start(bf16[352,256]{1,0:T(8,128)(2,1)S(1)} %get-tuple-element.54.ol), channel_id=1, source_target_pairs={{0,96},{32,0},{64,32},{96,64},{1,97},{33,1},{65,33},{97,65},{2,98}... | collective-permute-start | bytes 540680 | tf_op jit(solution)/shard_map/ppermute | solution.py:283
  53.5 2.9 %shard_map.85 = (bf16[368,512]{1,0:T(8,128)(2,1)S(1)}, bf16[352,512]{1,0:T(8,128)(2,1)}) custom-call(bf16[1024,1152]{1,0:T(8,128)(2,1)S(1)} %bitcast.22, f32[8,1024]{1,0:T(8,128)S(1)} %get-tuple-element.59.refs_1_), custom_call_target="tpu_custom_call" | custom-call | flops 1132462080 | bytes 1474560 | tf_op jit(solution)/shard_map/pallas_call | solution.py:327
  56.4 3.2 %collective-permute-start.8 = (bf16[368,512]{1,0:T(8,128)(2,1)S(1)}, bf16[368,512]{1,0:T(8,128)(2,1)S(1)}, u32[]{:S(2)}, u32[]{:S(2)}) collective-permute-start(bf16[368,512]{1,0:T(8,128)(2,1)S(1)} %get-tuple-element.60.oh), channel_id=1, source_target_pairs={{0,96},{32,0},{64,32},{96,64},{1,97},{33,1},{65,33},{97,65},{2,98}... | collective-permute-start | bytes 1130504 | tf_op jit(solution)/shard_map/ppermute | solution.py:283
  59.6 0.0 collective-permute-start.6
  59.6 0.0 collective-permute-done.1.ll
  59.7 0.7 copy-done.8
  60.3 3.2 %collective-permute-start.9 = (bf16[352,512]{1,0:T(8,128)(2,1)}, bf16[352,512]{1,0:T(8,128)(2,1)S(1)}, u32[]{:S(2)}, u32[]{:S(2)}) collective-permute-start(bf16[352,512]{1,0:T(8,128)(2,1)} %get-tuple-element.61.ol), channel_id=1, source_target_pairs={{0,96},{32,0},{64,32},{96,64},{1,97},{33,1},{65,33},{97,65},{2,98}... | collective-permute-start | bytes 1081352 | tf_op jit(solution)/shard_map/ppermute | solution.py:283
  63.6 0.0 collective-permute-done.lh
  63.6 0.7 copy-done.4
  64.2 2.0 %collective-permute-start.2 = (bf16[368,256]{1,0:T(8,128)(2,1)}, bf16[368,256]{1,0:T(8,128)(2,1)S(1)}, u32[]{:S(2)}, u32[]{:S(2)}) collective-permute-start(bf16[368,256]{1,0:T(8,128)(2,1)} %get-tuple-element.53.oh), channel_id=1, source_target_pairs={{0,96},{32,0},{64,32},{96,64},{1,97},{33,1},{65,33},{97,65},{2,98}... | collective-permute-start | bytes 565256 | tf_op jit(solution)/shard_map/ppermute | solution.py:283
  66.2 11.9 %collective-permute-done.2.rh = bf16[368,256]{1,0:T(8,128)(2,1)S(1)} collective-permute-done((bf16[368,256]{1,0:T(8,128)(2,1)}, bf16[368,256]{1,0:T(8,128)(2,1)S(1)}, u32[]{:S(2)}, u32[]{:S(2)}) %collective-permute-start.2) | collective-permute-done | bytes 188448 | tf_op jit(solution)/shard_map/ppermute | solution.py:283
  78.1 0.0 collective-permute-start.5
  78.1 2.3 %copy-done = bf16[4,720,720]{2,1,0:T(8,128)(2,1)S(1)} copy-done((bf16[4,720,720]{2,1,0:T(8,128)(2,1)S(1)}, bf16[4,720,720]{2,1,0:T(8,128)(2,1)}, u32[]{:S(2)}) %copy-start) | copy-done | bytes 4147224
  80.4 2.3 %copy-done.1 = bf16[4,720,720]{2,1,0:T(8,128)(2,1)S(1)} copy-done((bf16[4,720,720]{2,1,0:T(8,128)(2,1)S(1)}, bf16[4,720,720]{2,1,0:T(8,128)(2,1)}, u32[]{:S(2)}) %copy-start.1) | copy-done | bytes 4147224
  82.6 0.9 copy-done.5
  83.6 0.9 copy-done.7
  84.5 0.9 copy-done.9
  85.4 3.0 %shard_map.84 = (f32[720,256]{1,0:T(8,128)S(1)}, f32[720,256]{1,0:T(8,128)S(1)}) custom-call(s32[1]{0:T(128)} %bitcast.9.at_ref, bf16[368,256]{1,0:T(8,128)(2,1)} %get-tuple-element.53.oh, bf16[352,256]{1,0:T(8,128)(2,1)S(1)} %copy-done.7, bf16[368,256]{1,0:T(8,128)(2,1)S(1)} %copy-done.5, bf16[352,256]{1,0:T(8,128)(2,1)} %collective-permute-done.1.ll, ...), custom_call_target="tpu_custom_call" | custom-call | flops 1592524800 | bytes 6220800 | tf_op jit(solution)/shard_map/pallas_call | solution.py:359
  88.5 3.7 %collective-permute-start.4 = (bf16[368,256]{1,0:T(8,128)(2,1)S(1)}, bf16[368,256]{1,0:T(8,128)(2,1)S(1)}, u32[]{:S(2)}, u32[]{:S(2)}) collective-permute-start(bf16[368,256]{1,0:T(8,128)(2,1)S(1)} %collective-permute-done.2.rh), channel_id=1, source_target_pairs={{0,96},{32,0},{64,32},{96,64},{1,97},{33,1},{65,33},{97,65},{2,98}... | collective-permute-start | bytes 565256 | tf_op jit(solution)/shard_map/ppermute | solution.py:283
  92.1 0.0 collective-permute-done.9.rl
  92.1 0.0 collective-permute-start.17
  92.1 0.0 collective-permute-done.8.rh
  92.1 3.2 %collective-permute-start.16 = (bf16[368,512]{1,0:T(8,128)(2,1)S(1)}, bf16[368,512]{1,0:T(8,128)(2,1)S(1)}, u32[]{:S(2)}, u32[]{:S(2)}) collective-permute-start(bf16[368,512]{1,0:T(8,128)(2,1)S(1)} %collective-permute-done.8.rh), channel_id=1, source_target_pairs={{0,96},{32,0},{64,32},{96,64},{1,97},{33,1},{65,33},{97,65},{2,98}... | collective-permute-start | bytes 1130504 | tf_op jit(solution)/shard_map/ppermute | solution.py:283
  95.4 2.2 %copy-done.2 = bf16[4,720,720]{2,1,0:T(8,128)(2,1)S(1)} copy-done((bf16[4,720,720]{2,1,0:T(8,128)(2,1)S(1)}, bf16[4,720,720]{2,1,0:T(8,128)(2,1)}, u32[]{:S(2)}) %copy-start.2) | copy-done | bytes 4147224
  97.6 4.9 %shard_map.86 = (f32[720,512]{1,0:T(8,128)S(1)}, f32[720,512]{1,0:T(8,128)S(1)}) custom-call(s32[1]{0:T(128)} %bitcast.9.at_ref, bf16[368,512]{1,0:T(8,128)(2,1)S(1)} %get-tuple-element.60.oh, bf16[352,512]{1,0:T(8,128)(2,1)} %get-tuple-element.61.ol, bf16[368,512]{1,0:T(8,128)(2,1)S(1)} %collective-permute-done.6.lh, ...), custom_call_target="tpu_custom_call" | custom-call | flops 3185049600 | bytes 6220800 | tf_op jit(solution)/shard_map/pallas_call | solution.py:359
  102.6 0.0 collective-permute-done.5.fl
  102.6 2.2 %copy-done.3 = bf16[4,720,720]{2,1,0:T(8,128)(2,1)S(1)} copy-done((bf16[4,720,720]{2,1,0:T(8,128)(2,1)S(1)}, bf16[4,720,720]{2,1,0:T(8,128)(2,1)}, u32[]{:S(2)}) %copy-start.3) | copy-done | bytes 4147224
  104.9 1.6 shard_map.87
  106.5 0.1 collective-permute-start.11
  106.6 1.0 shard_map.88
  107.6 0.3 collective-permute-start.10
  107.9 3.0 %collective-permute-start.13 = (bf16[368,256]{1,0:T(8,128)(2,1)S(1)}, bf16[368,256]{1,0:T(8,128)(2,1)S(1)}, u32[]{:S(2)}, u32[]{:S(2)}) collective-permute-start(bf16[368,256]{1,0:T(8,128)(2,1)S(1)} %get-tuple-element.75), channel_id=1, source_target_pairs={{0,96},{32,0},{64,32},{96,64},{1,97},{33,1},{65,33},{97,65},{2,98}... | collective-permute-start | bytes 565256 | tf_op jit(solution)/shard_map/ppermute | solution.py:283
  111.0 0.0 collective-permute-done.17.fl
  111.0 1.9 %collective-permute-start.15 = (bf16[352,256]{1,0:T(8,128)(2,1)S(1)}, bf16[352,256]{1,0:T(8,128)(2,1)S(1)}, u32[]{:S(2)}, u32[]{:S(2)}) collective-permute-start(bf16[352,256]{1,0:T(8,128)(2,1)S(1)} %get-tuple-element.76), channel_id=1, source_target_pairs={{0,96},{32,0},{64,32},{96,64},{1,97},{33,1},{65,33},{97,65},{2,98}... | collective-permute-start | bytes 540680 | tf_op jit(solution)/shard_map/ppermute | solution.py:283
  112.9 3.6 %shard_map.89 = (bf16[720,512]{1,0:T(8,128)(2,1)S(1)}, bf16[368,512]{1,0:T(8,128)(2,1)S(1)}, bf16[352,512]{1,0:T(8,128)(2,1)S(1)}) custom-call(s32[1]{0:T(128)} %bitcast.9.at_ref, f32[720,512]{1,0:T(8,128)S(1)} %get-tuple-element.77.g_ref, f32[720,512]{1,0:T(8,128)S(1)} %get-tuple-element.78.u_ref, bf16[368,512]{1,0:T(8,128)(2,1)S(1)} %collective-permute-done.16.fh, ...), custom_call_target="tpu_custom_call" | custom-call | flops 1592524800 | bytes 3110400 | tf_op jit(solution)/shard_map/pallas_call | solution.py:370
  116.5 0.2 collective-permute-start.19
  116.7 3.2 %collective-permute-start.21 = (bf16[368,512]{1,0:T(8,128)(2,1)S(1)}, bf16[368,512]{1,0:T(8,128)(2,1)S(1)}, u32[]{:S(2)}, u32[]{:S(2)}) collective-permute-start(bf16[368,512]{1,0:T(8,128)(2,1)S(1)} %get-tuple-element.85), channel_id=1, source_target_pairs={{0,96},{32,0},{64,32},{96,64},{1,97},{33,1},{65,33},{97,65},{2,98}... | collective-permute-start | bytes 1130504 | tf_op jit(solution)/shard_map/ppermute | solution.py:283
  119.9 2.4 %shard_map.90 = (f32[368,512]{1,0:T(8,128)S(1)}, bf16[352,512]{1,0:T(8,128)(2,1)S(1)}, bf16[368,512]{1,0:T(8,128)(2,1)S(1)}, f32[352,512]{1,0:T(8,128)S(1)}, f32[720,512]{1,0:T(8,128)S(1)}) custom-call(s32[1]{0:T(128)} %bitcast.9.at_ref, bf16[720,512]{1,0:T(8,128)(2,1)S(1)} %get-tuple-element.79.h_ref, bf16[4,720,720]{2,1,0:T(8,128)(2,1)S(1)} %bitcast.16, ...), custom_call_target="tpu_custom_call" | custom-call | flops 1592524800 | bytes 3110400 | tf_op jit(solution)/shard_map/pallas_call | solution.py:380
  122.3 4.6 %collective-permute-done.19 = bf16[352,512]{1,0:T(8,128)(2,1)S(1)} collective-permute-done((bf16[352,512]{1,0:T(8,128)(2,1)S(1)}, bf16[352,512]{1,0:T(8,128)(2,1)S(1)}, u32[]{:S(2)}, u32[]{:S(2)}) %collective-permute-start.19) | collective-permute-done | bytes 360480 | tf_op jit(solution)/shard_map/ppermute | solution.py:283
  126.9 0.0 collective-permute-start.12
  126.9 0.1 add_convert_fusion.1
  127.0 0.1 collective-permute-start.18
  127.1 0.1 add_convert_fusion
  127.3 3.3 %collective-permute-start.23 = (bf16[352,512]{1,0:T(8,128)(2,1)S(1)}, bf16[352,512]{1,0:T(8,128)(2,1)S(1)}, u32[]{:S(2)}, u32[]{:S(2)}) collective-permute-start(bf16[352,512]{1,0:T(8,128)(2,1)S(1)} %get-tuple-element.86), channel_id=1, source_target_pairs={{0,96},{32,0},{64,32},{96,64},{1,97},{33,1},{65,33},{97,65},{2,98}... | collective-permute-start | bytes 1081352 | tf_op jit(solution)/shard_map/ppermute | solution.py:283
  130.6 0.0 collective-permute-done.10.refs_2_
  130.6 0.0 collective-permute-start.20
  130.6 3.2 %collective-permute-start.22 = (bf16[368,512]{1,0:T(8,128)(2,1)S(1)}, bf16[368,512]{1,0:T(8,128)(2,1)S(1)}, u32[]{:S(2)}, u32[]{:S(2)}) collective-permute-start(bf16[368,512]{1,0:T(8,128)(2,1)S(1)} %add_convert_fusion), channel_id=1, source_target_pairs={{0,96},{32,0},{64,32},{96,64},{1,97},{33,1},{65,33},{97,65},{2,98}... | collective-permute-start | bytes 1130504 | tf_op jit(solution)/shard_map/ppermute | solution.py:283
  133.8 0.1 add_convert_fusion.2
  133.9 1.7 collective-permute-done.12.refs_3_
  135.5 0.0 collective-permute-start.14
  135.5 10.2 %collective-permute-done.14.refs_4_ = bf16[368,256]{1,0:T(8,128)(2,1)S(1)} collective-permute-done((bf16[368,256]{1,0:T(8,128)(2,1)S(1)}, bf16[368,256]{1,0:T(8,128)(2,1)S(1)}, u32[]{:S(2)}, u32[]{:S(2)}) %collective-permute-start.14) | collective-permute-done | bytes 188448 | tf_op jit(solution)/shard_map/ppermute | solution.py:283
  145.8 3.1 %shard_map.91 = bf16[1024,1152]{1,0:T(8,128)(2,1)S(1)} custom-call(f32[1024,8]{1,0:T(8,128)S(1)} %get-tuple-element.52.refs_0_, f32[720,256]{1,0:T(8,128)S(1)} %get-tuple-element.70.refs_1_, bf16[368,256]{1,0:T(8,128)(2,1)S(1)} %collective-permute-done.10.refs_2_, bf16[352,256]{1,0:T(8,128)(2,1)S(1)} %collective-permute-done.12.refs_3_, ...), custom_call_target="tpu_custom_call" | custom-call | flops 1132462080 | bytes 1474560 | tf_op jit(solution)/shard_map/pallas_call | solution.py:414
  148.9 0.0 copy-start.10
  149.0 0.0 copy-start.11
  149.0 39.5 %all_to_all.10 = bf16[128,8,1152]{2,1,0:T(8,128)(2,1)S(1)} all-to-all(bf16[128,8,1152]{2,1,0:T(8,128)(2,1)S(1)} %bitcast.19), channel_id=1, replica_groups=mesh['attn'=4,'expert_0'=4,'expert_1'=4,'expert_2'=2] {'attn','expert_0'..., dimensions={0} | all-to-all | bytes 4718592 | tf_op jit(solution)/shard_map/all_to_all | solution.py:289
  188.4 1.9 %shard_map.92 = bf16[32,2880]{1,0:T(8,128)(2,1)} custom-call(bf16[1024,1152]{1,0:T(8,128)(2,1)S(1)} %bitcast.20, s32[4,32]{1,0:T(4,128)S(1)} %bitcast.24, f32[4,32]{1,0:T(4,128)S(1)} %bitcast.25), custom_call_target="tpu_custom_call" | custom-call | flops 141557760 | bytes 1474560 | tf_op jit(solution)/shard_map/pallas_call | solution.py:417
  (43 shorter events, 0.1 us)
Async XLA Ops:
  3.6 11.2 %copy-start.13 = (s32[32]{0:T(128)S(1)}, s32[32]{0:T(128)}, u32[]{:S(2)}) copy-start(s32[32]{0:T(128)} %param.12) | copy-start | bytes 388
  3.6 13.7 %copy-start.12 = (s32[32]{0:T(128)S(1)}, s32[32]{0:T(128)}, u32[]{:S(2)}) copy-start(s32[32]{0:T(128)} %param.11) | copy-start | bytes 388
  3.6 44.4 %all-to-all-start = ((bf16[128,8,1152]{2,1,0:T(8,128)(2,1)}), bf16[128,8,1152]{2,1,0:T(8,128)(2,1)S(1)}, u32[]{:S(2)}, u32[]{:S(2)}) async-start(bf16[128,8,1152]{2,1,0:T(8,128)(2,1)} %bitcast.26), calls=%async_computation | async-start | bytes 4718592 | tf_op jit(solution)/shard_map/all_to_all | solution.py:289
  50.3 13.3 %copy-start.6 = (bf16[352,256]{1,0:T(8,128)(2,1)}, bf16[352,256]{1,0:T(8,128)(2,1)S(1)}, u32[]{:S(2)}) copy-start(bf16[352,256]{1,0:T(8,128)(2,1)S(1)} %get-tuple-element.54.ol) | copy-start | bytes 540676
  50.3 9.4 %collective-permute-start.1 = (bf16[352,256]{1,0:T(8,128)(2,1)S(1)}, bf16[352,256]{1,0:T(8,128)(2,1)}, u32[]{:S(2)}, u32[]{:S(2)}) collective-permute-start(bf16[352,256]{1,0:T(8,128)(2,1)S(1)} %get-tuple-element.54.ol), channel_id=1, source_target_pairs={{0,32},{32,64},{64,96},{96,0},{1,33},{33,65},{65,97},{97,1},{2,34}... | collective-permute-start | bytes 540680 | tf_op jit(solution)/shard_map/ppermute | solution.py:283
  50.8 8.8 %collective-permute-start.3 = (bf16[352,256]{1,0:T(8,128)(2,1)S(1)}, bf16[352,256]{1,0:T(8,128)(2,1)S(1)}, u32[]{:S(2)}, u32[]{:S(2)}) collective-permute-start(bf16[352,256]{1,0:T(8,128)(2,1)S(1)} %get-tuple-element.54.ol), channel_id=1, source_target_pairs={{0,96},{32,0},{64,32},{96,64},{1,97},{33,1},{65,33},{97,65},{2,98}... | collective-permute-start | bytes 540680 | tf_op jit(solution)/shard_map/ppermute | solution.py:283
  53.5 10.0 %collective-permute-start = (bf16[368,256]{1,0:T(8,128)(2,1)}, bf16[368,256]{1,0:T(8,128)(2,1)S(1)}, u32[]{:S(2)}, u32[]{:S(2)}) collective-permute-start(bf16[368,256]{1,0:T(8,128)(2,1)} %get-tuple-element.53.oh), channel_id=1, source_target_pairs={{0,32},{32,64},{64,96},{96,0},{1,33},{33,65},{65,97},{97,1},{2,34}... | collective-permute-start | bytes 565256 | tf_op jit(solution)/shard_map/ppermute | solution.py:283
  53.5 41.8 %slice-start.2 = ((s8[4423680]{0:T(1024)(128)(4,1)}), s8[229376]{0:T(1024)(128)(4,1)S(1)}, s32[]{:S(2)}) async-start(s8[4423680]{0:T(1024)(128)(4,1)} %bitcast.17), calls=%async_computation.4 | async-start | bytes 458752
  56.4 35.7 %collective-permute-start.8 = (bf16[368,512]{1,0:T(8,128)(2,1)S(1)}, bf16[368,512]{1,0:T(8,128)(2,1)S(1)}, u32[]{:S(2)}, u32[]{:S(2)}) collective-permute-start(bf16[368,512]{1,0:T(8,128)(2,1)S(1)} %get-tuple-element.60.oh), channel_id=1, source_target_pairs={{0,96},{32,0},{64,32},{96,64},{1,97},{33,1},{65,33},{97,65},{2,98}... | collective-permute-start | bytes 1130504 | tf_op jit(solution)/shard_map/ppermute | solution.py:283
  59.6 35.7 %collective-permute-start.6 = (bf16[368,512]{1,0:T(8,128)(2,1)S(1)}, bf16[368,512]{1,0:T(8,128)(2,1)S(1)}, u32[]{:S(2)}, u32[]{:S(2)}) collective-permute-start(bf16[368,512]{1,0:T(8,128)(2,1)S(1)} %get-tuple-element.60.oh), channel_id=1, source_target_pairs={{0,32},{32,64},{64,96},{96,0},{1,33},{33,65},{65,97},{97,1},{2,34}... | collective-permute-start | bytes 1130504 | tf_op jit(solution)/shard_map/ppermute | solution.py:283
  59.6 28.8 %collective-permute-start.7 = (bf16[352,512]{1,0:T(8,128)(2,1)}, bf16[352,512]{1,0:T(8,128)(2,1)S(1)}, u32[]{:S(2)}, u32[]{:S(2)}) collective-permute-start(bf16[352,512]{1,0:T(8,128)(2,1)} %get-tuple-element.61.ol), channel_id=1, source_target_pairs={{0,32},{32,64},{64,96},{96,0},{1,33},{33,65},{65,97},{97,1},{2,34}... | collective-permute-start | bytes 1081352 | tf_op jit(solution)/shard_map/ppermute | solution.py:283
  59.7 0.7 copy-start.8
  60.3 31.8 %collective-permute-start.9 = (bf16[352,512]{1,0:T(8,128)(2,1)}, bf16[352,512]{1,0:T(8,128)(2,1)S(1)}, u32[]{:S(2)}, u32[]{:S(2)}) collective-permute-start(bf16[352,512]{1,0:T(8,128)(2,1)} %get-tuple-element.61.ol), channel_id=1, source_target_pairs={{0,96},{32,0},{64,32},{96,64},{1,97},{33,1},{65,33},{97,65},{2,98}... | collective-permute-start | bytes 1081352 | tf_op jit(solution)/shard_map/ppermute | solution.py:283
  63.6 0.7 copy-start.4
  64.2 13.9 %collective-permute-start.2 = (bf16[368,256]{1,0:T(8,128)(2,1)}, bf16[368,256]{1,0:T(8,128)(2,1)S(1)}, u32[]{:S(2)}, u32[]{:S(2)}) collective-permute-start(bf16[368,256]{1,0:T(8,128)(2,1)} %get-tuple-element.53.oh), channel_id=1, source_target_pairs={{0,96},{32,0},{64,32},{96,64},{1,97},{33,1},{65,33},{97,65},{2,98}... | collective-permute-start | bytes 565256 | tf_op jit(solution)/shard_map/ppermute | solution.py:283
  78.1 24.4 %collective-permute-start.5 = (bf16[352,256]{1,0:T(8,128)(2,1)}, bf16[352,256]{1,0:T(8,128)(2,1)S(1)}, u32[]{:S(2)}, u32[]{:S(2)}) collective-permute-start(bf16[352,256]{1,0:T(8,128)(2,1)} %collective-permute-done.1.ll), channel_id=1, source_target_pairs={{0,32},{32,64},{64,96},{96,0},{1,33},{33,65},{65,97},{97,1},{2,34}... | collective-permute-start | bytes 540680 | tf_op jit(solution)/shard_map/ppermute | solution.py:283
  78.1 2.3 %copy-start = (bf16[4,720,720]{2,1,0:T(8,128)(2,1)S(1)}, bf16[4,720,720]{2,1,0:T(8,128)(2,1)}, u32[]{:S(2)}) copy-start(bf16[4,720,720]{2,1,0:T(8,128)(2,1)} %get-tuple-element.55.ga.gb.gc.wg_ref) | copy-start | bytes 12441604
  80.4 2.3 %copy-start.1 = (bf16[4,720,720]{2,1,0:T(8,128)(2,1)S(1)}, bf16[4,720,720]{2,1,0:T(8,128)(2,1)}, u32[]{:S(2)}) copy-start(bf16[4,720,720]{2,1,0:T(8,128)(2,1)} %get-tuple-element.56.ua.ub.uc.wu_ref) | copy-start | bytes 12441604
  82.6 0.9 copy-start.5
  83.6 0.9 copy-start.7
  84.5 0.9 copy-start.9
  85.4 10.0 %slice-start.3 = ((s8[4423680]{0:T(1024)(128)(4,1)}), s8[4194304]{0:T(1024)(128)(4,1)S(1)}, s32[]{:S(2)}) async-start(s8[4423680]{0:T(1024)(128)(4,1)} %bitcast.17), calls=%async_computation.5 | async-start | bytes 8388608
  85.4 17.2 %slice-start = ((s8[4423680]{0:T(1024)(128)(4,1)}), s8[4194304]{0:T(1024)(128)(4,1)S(1)}, s32[]{:S(2)}) async-start(s8[4423680]{0:T(1024)(128)(4,1)} %bitcast.15), calls=%async_computation.2 | async-start | bytes 8388608
  88.4 14.1 %slice-start.1 = ((s8[4423680]{0:T(1024)(128)(4,1)}), s8[229376]{0:T(1024)(128)(4,1)S(1)}, s32[]{:S(2)}) async-start(s8[4423680]{0:T(1024)(128)(4,1)} %bitcast.15), calls=%async_computation.3 | async-start | bytes 458752
  88.5 14.1 %collective-permute-start.4 = (bf16[368,256]{1,0:T(8,128)(2,1)S(1)}, bf16[368,256]{1,0:T(8,128)(2,1)S(1)}, u32[]{:S(2)}, u32[]{:S(2)}) collective-permute-start(bf16[368,256]{1,0:T(8,128)(2,1)S(1)} %collective-permute-done.2.rh), channel_id=1, source_target_pairs={{0,96},{32,0},{64,32},{96,64},{1,97},{33,1},{65,33},{97,65},{2,98}... | collective-permute-start | bytes 565256 | tf_op jit(solution)/shard_map/ppermute | solution.py:283
  92.1 18.8 %collective-permute-start.17 = (bf16[352,512]{1,0:T(8,128)(2,1)S(1)}, bf16[352,512]{1,0:T(8,128)(2,1)S(1)}, u32[]{:S(2)}, u32[]{:S(2)}) collective-permute-start(bf16[352,512]{1,0:T(8,128)(2,1)S(1)} %collective-permute-done.7.ll), channel_id=1, source_target_pairs={{0,32},{32,64},{64,96},{96,0},{1,33},{33,65},{65,97},{97,1},{2,34}... | collective-permute-start | bytes 1081352 | tf_op jit(solution)/shard_map/ppermute | solution.py:283
  92.1 20.8 %collective-permute-start.16 = (bf16[368,512]{1,0:T(8,128)(2,1)S(1)}, bf16[368,512]{1,0:T(8,128)(2,1)S(1)}, u32[]{:S(2)}, u32[]{:S(2)}) collective-permute-start(bf16[368,512]{1,0:T(8,128)(2,1)S(1)} %collective-permute-done.8.rh), channel_id=1, source_target_pairs={{0,96},{32,0},{64,32},{96,64},{1,97},{33,1},{65,33},{97,65},{2,98}... | collective-permute-start | bytes 1130504 | tf_op jit(solution)/shard_map/ppermute | solution.py:283
  95.4 2.3 %copy-start.2 = (bf16[4,720,720]{2,1,0:T(8,128)(2,1)S(1)}, bf16[4,720,720]{2,1,0:T(8,128)(2,1)}, u32[]{:S(2)}) copy-start(bf16[4,720,720]{2,1,0:T(8,128)(2,1)} %get-tuple-element.56.ua.ub.uc.wu_ref) | copy-start | bytes 12441604
  102.6 2.3 %copy-start.3 = (bf16[4,720,720]{2,1,0:T(8,128)(2,1)S(1)}, bf16[4,720,720]{2,1,0:T(8,128)(2,1)}, u32[]{:S(2)}) copy-start(bf16[4,720,720]{2,1,0:T(8,128)(2,1)} %get-tuple-element.56.ua.ub.uc.wu_ref) | copy-start | bytes 12441604
  106.5 10.2 %collective-permute-start.11 = (bf16[352,256]{1,0:T(8,128)(2,1)S(1)}, bf16[352,256]{1,0:T(8,128)(2,1)S(1)}, u32[]{:S(2)}, u32[]{:S(2)}) collective-permute-start(bf16[352,256]{1,0:T(8,128)(2,1)S(1)} %get-tuple-element.73), channel_id=1, source_target_pairs={{0,32},{32,64},{64,96},{96,0},{1,33},{33,65},{65,97},{97,1},{2,34}... | collective-permute-start | bytes 540680 | tf_op jit(solution)/shard_map/ppermute | solution.py:283
  107.6 23.0 %collective-permute-start.10 = (bf16[368,256]{1,0:T(8,128)(2,1)S(1)}, bf16[368,256]{1,0:T(8,128)(2,1)S(1)}, u32[]{:S(2)}, u32[]{:S(2)}) collective-permute-start(bf16[368,256]{1,0:T(8,128)(2,1)S(1)} %get-tuple-element.71), channel_id=1, source_target_pairs={{0,32},{32,64},{64,96},{96,0},{1,33},{33,65},{65,97},{97,1},{2,34}... | collective-permute-start | bytes 565256 | tf_op jit(solution)/shard_map/ppermute | solution.py:283
  107.9 22.6 %collective-permute-start.13 = (bf16[368,256]{1,0:T(8,128)(2,1)S(1)}, bf16[368,256]{1,0:T(8,128)(2,1)S(1)}, u32[]{:S(2)}, u32[]{:S(2)}) collective-permute-start(bf16[368,256]{1,0:T(8,128)(2,1)S(1)} %get-tuple-element.75), channel_id=1, source_target_pairs={{0,96},{32,0},{64,32},{96,64},{1,97},{33,1},{65,33},{97,65},{2,98}... | collective-permute-start | bytes 565256 | tf_op jit(solution)/shard_map/ppermute | solution.py:283
  111.0 16.3 %collective-permute-start.15 = (bf16[352,256]{1,0:T(8,128)(2,1)S(1)}, bf16[352,256]{1,0:T(8,128)(2,1)S(1)}, u32[]{:S(2)}, u32[]{:S(2)}) collective-permute-start(bf16[352,256]{1,0:T(8,128)(2,1)S(1)} %get-tuple-element.76), channel_id=1, source_target_pairs={{0,96},{32,0},{64,32},{96,64},{1,97},{33,1},{65,33},{97,65},{2,98}... | collective-permute-start | bytes 540680 | tf_op jit(solution)/shard_map/ppermute | solution.py:283
  116.5 10.4 %collective-permute-start.19 = (bf16[352,512]{1,0:T(8,128)(2,1)S(1)}, bf16[352,512]{1,0:T(8,128)(2,1)S(1)}, u32[]{:S(2)}, u32[]{:S(2)}) collective-permute-start(bf16[352,512]{1,0:T(8,128)(2,1)S(1)} %get-tuple-element.83), channel_id=1, source_target_pairs={{0,32},{32,64},{64,96},{96,0},{1,33},{33,65},{65,97},{97,1},{2,34}... | collective-permute-start | bytes 1081352 | tf_op jit(solution)/shard_map/ppermute | solution.py:283
  116.7 10.3 %collective-permute-start.21 = (bf16[368,512]{1,0:T(8,128)(2,1)S(1)}, bf16[368,512]{1,0:T(8,128)(2,1)S(1)}, u32[]{:S(2)}, u32[]{:S(2)}) collective-permute-start(bf16[368,512]{1,0:T(8,128)(2,1)S(1)} %get-tuple-element.85), channel_id=1, source_target_pairs={{0,96},{32,0},{64,32},{96,64},{1,97},{33,1},{65,33},{97,65},{2,98}... | collective-permute-start | bytes 1130504 | tf_op jit(solution)/shard_map/ppermute | solution.py:283
  126.9 8.6 %collective-permute-start.12 = (bf16[352,256]{1,0:T(8,128)(2,1)S(1)}, bf16[352,256]{1,0:T(8,128)(2,1)S(1)}, u32[]{:S(2)}, u32[]{:S(2)}) collective-permute-start(bf16[352,256]{1,0:T(8,128)(2,1)S(1)} %add_convert_fusion.3), channel_id=1, source_target_pairs={{0,32},{32,64},{64,96},{96,0},{1,33},{33,65},{65,97},{97,1},{2,34}... | collective-permute-start | bytes 540680 | tf_op jit(solution)/shard_map/ppermute | solution.py:283
  127.0 18.7 %collective-permute-start.18 = (bf16[368,512]{1,0:T(8,128)(2,1)S(1)}, bf16[368,512]{1,0:T(8,128)(2,1)S(1)}, u32[]{:S(2)}, u32[]{:S(2)}) collective-permute-start(bf16[368,512]{1,0:T(8,128)(2,1)S(1)} %get-tuple-element.81), channel_id=1, source_target_pairs={{0,32},{32,64},{64,96},{96,0},{1,33},{33,65},{65,97},{97,1},{2,34}... | collective-permute-start | bytes 1130504 | tf_op jit(solution)/shard_map/ppermute | solution.py:283
  127.3 18.5 %collective-permute-start.23 = (bf16[352,512]{1,0:T(8,128)(2,1)S(1)}, bf16[352,512]{1,0:T(8,128)(2,1)S(1)}, u32[]{:S(2)}, u32[]{:S(2)}) collective-permute-start(bf16[352,512]{1,0:T(8,128)(2,1)S(1)} %get-tuple-element.86), channel_id=1, source_target_pairs={{0,96},{32,0},{64,32},{96,64},{1,97},{33,1},{65,33},{97,65},{2,98}... | collective-permute-start | bytes 1081352 | tf_op jit(solution)/shard_map/ppermute | solution.py:283
  130.6 15.2 %collective-permute-start.20 = (bf16[352,512]{1,0:T(8,128)(2,1)S(1)}, bf16[352,512]{1,0:T(8,128)(2,1)S(1)}, u32[]{:S(2)}, u32[]{:S(2)}) collective-permute-start(bf16[352,512]{1,0:T(8,128)(2,1)S(1)} %add_convert_fusion.1), channel_id=1, source_target_pairs={{0,32},{32,64},{64,96},{96,0},{1,33},{33,65},{65,97},{97,1},{2,34}... | collective-permute-start | bytes 1081352 | tf_op jit(solution)/shard_map/ppermute | solution.py:283
  130.6 15.2 %collective-permute-start.22 = (bf16[368,512]{1,0:T(8,128)(2,1)S(1)}, bf16[368,512]{1,0:T(8,128)(2,1)S(1)}, u32[]{:S(2)}, u32[]{:S(2)}) collective-permute-start(bf16[368,512]{1,0:T(8,128)(2,1)S(1)} %add_convert_fusion), channel_id=1, source_target_pairs={{0,96},{32,0},{64,32},{96,64},{1,97},{33,1},{65,33},{97,65},{2,98}... | collective-permute-start | bytes 1130504 | tf_op jit(solution)/shard_map/ppermute | solution.py:283
  135.5 10.2 %collective-permute-start.14 = (bf16[368,256]{1,0:T(8,128)(2,1)S(1)}, bf16[368,256]{1,0:T(8,128)(2,1)S(1)}, u32[]{:S(2)}, u32[]{:S(2)}) collective-permute-start(bf16[368,256]{1,0:T(8,128)(2,1)S(1)} %add_convert_fusion.2), channel_id=1, source_target_pairs={{0,96},{32,0},{64,32},{96,64},{1,97},{33,1},{65,33},{97,65},{2,98}... | collective-permute-start | bytes 565256 | tf_op jit(solution)/shard_map/ppermute | solution.py:283
  148.9 39.5 %copy-start.10 = (s32[32,4]{0,1:T(4,128)S(1)}, s32[32,4]{0,1:T(4,128)}, u32[]{:S(2)}) copy-start(s32[32,4]{0,1:T(4,128)} %param.9) | copy-start | bytes 1540
  149.0 39.5 %copy-start.11 = (f32[32,4]{0,1:T(4,128)S(1)}, f32[32,4]{0,1:T(4,128)}, u32[]{:S(2)}) copy-start(f32[32,4]{0,1:T(4,128)} %param.10) | copy-start | bytes 1540
where the time goes:
time: 191 us; the launch traced here: 190 us
  starting transfers between devices  45.2 us (24%)
  waiting for transfers between devices  43.8 us (23%)
  Pallas kernels  43.7 us (23%)
  blocking collectives  39.5 us (21%)
  local copies, waits for them, and re-layouts  14.4 us (8%)
  between operations  3.52 us (2%)
    all_to_all x1, blocking collectives, exchange(): lax.all_to_all(blocks, ATTN_EXPERT, split_axis=0, concat_axis=0, tiled=True)  39.5 us
    ppermute x24, starting transfers between devices, shifted(): return lambda array: lax.ppermute(array, 'attn', pairs)  34 us
    ppermute x24, waiting for transfers between devices, shifted(): return lambda array: lax.ppermute(array, 'attn', pairs)  28.4 us
    all_to_all x1, waiting for transfers between devices, exchange(): lax.all_to_all(blocks, ATTN_EXPERT, split_axis=0, concat_axis=0, tiled=True)  15.4 us
    pallas_call x1, Pallas kernels, on_device(): pl.pallas_call(relay_kernel, grid=(pl.cdiv(units, step),), out_shape=(rel...  13.3 us
    unnamed x36, local copies, waits for them, and re-layouts  13.1 us
    all_to_all x1, starting transfers between devices, exchange(): lax.all_to_all(blocks, ATTN_EXPERT, split_axis=0, concat_axis=0, tiled=True)  11.2 us
    pallas_call x2, Pallas kernels, ring(): staged(mid_kernel, halves * 3 + [weight(units, width, d) for d in (0, bef...  7.93 us
  transfers between devices with their start and end apart: 25, of which 5 were waited for; matrix products, arithmetic and copies ran while one was open for 1% of the time, Pallas kernels for 17%

commit v1 on v0

--- a/solution.py
+++ b/solution.py
@@ -20,10 +20,6 @@
 
 def dot(a, b, dims=((1,), (0,))):
     return lax.dot_general(a, b, (dims, ((), ())), preferred_element_type=F32)
-
-
-def half(n):
-    return (n // 2 + 15) // 16 * 16
 
 
 def hot(places, width, first=0):
@@ -64,22 +60,22 @@
         s_ref[at, lay.low :] = (dot(even, x[:, : lay.point]) + dot(odd, tail)).astype(BF)
 
 
-def gather_slots(lay, rows, x_ref, first, outs):
-    slots = outs[0].shape[1]
+def gather_slots(lay, rows, x_ref, first, out):
+    slots = out.shape[1]
     place = (iota((slots, x_ref.shape[0]), 0) + first).astype(F32)
     match = lambda row: jnp.where(row == place, 1.0, 0.0).astype(BF)
     got = dot(match(rows[0]), x_ref[:, : lay.width])
     rest = x_ref[:, lay.low :]
     left, right = dot(match(rows[1]), rest), dot(match(rows[2]), rest)
     extra = jnp.concatenate([left, right[:, : lay.width - lay.point]], axis=1)
-    share_out((got + extra).astype(BF).T, outs)
-
-
-def pick_more_kernel(lay, first, x_ref, row_ref, *outs):
-    gather_slots(lay, [row_ref[k : k + 1] for k in range(3)], x_ref, first, outs)
-
-
-def pick_kernel(lay, x_ref, par_ref, row_ref, col_ref, *outs):
+    out[...] = (got + extra).astype(BF).T
+
+
+def pick_more_kernel(lay, first, x_ref, row_ref, out):
+    gather_slots(lay, [row_ref[k : k + 1] for k in range(3)], x_ref, first, out)
+
+
+def pick_kernel(lay, x_ref, par_ref, row_ref, col_ref, out):
     came, seats = x_ref.shape[0], lay.seats
     sources = came // seats
     bound = par_ref[0].astype(F32)
@@ -106,11 +102,7 @@
     every = jnp.concatenate([rank, evens, odds, nothing], axis=0)
     row_ref[...] = every
     col_ref[...] = every.T
-    gather_slots(lay, (rank, evens, odds), x_ref, 0, outs)
-
-
-def whole(*parts):
-    return jnp.concatenate([part[...] for part in parts], axis=0)
+    gather_slots(lay, (rank, evens, odds), x_ref, 0, out)
 
 
 def relay_kernel(seen_ref, g_ref, u_ref, d_ref, go_ref, uo_ref, do_ref):
@@ -123,48 +115,42 @@
         do_ref[b] = d_ref[:, at].T
 
 
-def mid_kernel(at_ref, oh, ol, lh, ll, rh, rl, ga, gb, gc, ua, ub, uc, g_ref, u_ref):
+def gate_up(refs):
+    count = len(refs) // 3
+    gate = up = None
+    for x, wg, wu in zip(refs[:count], refs[count : 2 * count], refs[2 * count :]):
+        g, u = dot(wg[0], x[...]), dot(wu[0], x[...])
+        gate, up = (g, u) if gate is None else (gate + g, up + u)
+    return gate, up
+
+
+def mid_kernel(at_ref, *refs):
     del at_ref
-    gate = up = None
-    for n, (x, g, u) in enumerate(
-        ((whole(oh, ol), ga, ua), (whole(lh, ll), gb, ub), (whole(rh, rl), gc, uc))
-    ):
-        g, u = dot(g[0], x), dot(u[0], x)
-        gate, up = (g, u) if n == 0 else (gate + g, up + u)
-    g_ref[...] = gate
-    u_ref[...] = up
-
-
-def share_out(values, refs):
-    first = 0
-    for ref in refs:
-        ref[...] = values[first : first + ref.shape[0]].astype(ref.dtype)
-        first += ref.shape[0]
-
-
-def far_kernel(at_ref, g_ref, u_ref, fh, fl, wg_ref, wu_ref, wd_ref, h_ref, *outs):
+    refs[-2][...], refs[-1][...] = gate_up(refs[:-2])
+
+
+def far_kernel(at_ref, g_ref, u_ref, wd_ref, *refs):
     del at_ref
-    x = whole(fh, fl)
-    gate = g_ref[...] + dot(wg_ref[0], x)
-    up = u_ref[...] + dot(wu_ref[0], x)
+    gate, up = gate_up(refs[:-2])
+    h_ref, o_ref = refs[-2:]
+    gate, up = gate + g_ref[...], up + u_ref[...]
     hidden = (gate * jax.nn.sigmoid(SWISH_SCALE * gate) * (up + 1.0)).astype(BF)
     h_ref[...] = hidden
-    share_out(dot(wd_ref[0], hidden), outs)
-
-
-def near_kernel(at_ref, h_ref, da, db, dc, *outs):
+    o_ref[...] = dot(wd_ref[0], hidden).astype(BF)
+
+
+def near_kernel(at_ref, h_ref, *refs):
     del at_ref
     hidden = h_ref[...]
-    share_out(dot(db[0], hidden), outs[0:2])
-    share_out(dot(dc[0], hidden), outs[2:4])
-    share_out(dot(da[0], hidden), outs[4:5])
+    for weight, out in zip(refs[:3], refs[3:]):
+        out[...] = dot(weight[0], hidden).astype(out.dtype)
 
 
 def place_kernel(lay, slot_ref, *refs):
     ins, z_ref = refs[:-1], refs[-1]
     columns = []
-    for own, lh, ll, rh, rl in (ins[:5], ins[5:]):
-        total = own[...] + whole(lh, ll).astype(F32) + whole(rh, rl).astype(F32)
+    for own, left, right in (ins[:3], ins[3:]):
+        total = own[...] + left[...].astype(F32) + right[...].astype(F32)
         columns.append(total.astype(BF))
     y = jnp.concatenate(columns, axis=1)
     slots, came = y.shape[1], z_ref.shape[0]
@@ -269,8 +255,6 @@
     slots = capacity + block * SHED_MOST
     units = gate_weight.shape[2]
     lay = Layout(width, experts, min(tok, 3 * tok * top // experts))
-    cut = half(width)
-    rest = width - cut
     devices = groups * experts
     came = devices * lay.seats
     me = lax.axis_index(EXPERT)
@@ -314,20 +298,19 @@
     )(seen, gate_weight[0].T, up_weight[0].T, down_weight[0])
     arrived, wg, wu, wd = lax.optimization_barrier((arrived, wg, wu, wd))
 
-    tile = 256
-    parts = (tile, slots - tile)
+    part = slots // 2
+    columns = shape((width, part), BF)
     gather_work = (2 * slots * came * width, 2 * came * width)
-    pieces = [tuple(shape((n, p), BF) for n in (cut, rest)) for p in parts]
-    places, slot, *own = run(
+    places, slot, own_a = run(
         lambda *refs: pick_kernel(lay, *refs),
         [VMEM, SMEM],
-        (shape((8, came), F32), shape((came, 8), F32), *pieces[0]),
+        (shape((8, came), F32), shape((came, 8), F32), columns),
         gather_work,
     )(arrived, par)
-    more = run(
-        lambda *refs: pick_more_kernel(lay, parts[0], *refs), [VMEM] * 2, pieces[1], gather_work
+    own_b = run(
+        lambda *refs: pick_more_kernel(lay, part, *refs), [VMEM] * 2, columns, gather_work
     )(arrived, places)
-    lane = lambda rows: pl.BlockSpec((rows, tile), lambda i, p: (0, i))
+    lane = lambda rows: pl.BlockSpec((rows, part), lambda i, p: (0, 0))
 
     def weight(rows, columns, ahead):
         return pl.BlockSpec((1, rows, columns), lambda i, p: (lax.rem(p[0] + ahead, groups), 0, 0))
@@ -337,7 +320,7 @@
             kernel,
             grid_spec=pltpu.PrefetchScalarGridSpec(
                 num_scalar_prefetch=1,
-                grid=(outs[0].shape[1] // tile,),
+                grid=(1,),
                 in_specs=ins,
                 out_specs=tuple(lane(out.shape[0]) for out in outs),
             ),
@@ -347,40 +330,37 @@
         )
 
     before, after, across = groups - 1, 1, groups // 2
-    halves = [lane(cut), lane(rest)]
-    opposite = weight(units, width, across)
     area = width * units
-
-    def ring(part, oh, ol):
-        rows = lambda n, kind: shape((n, part), kind)
-        ll, rh = right(ol), left(oh)
-        lh, rl = right(oh), left(ol)
-        fl, fh = right(ll), left(rh)
-        gate, up = staged(
+    rows = lambda n, kind: shape((n, part), kind)
+
+    def mid(blocks, ahead):
+        count = len(blocks)
+        return staged(
             mid_kernel,
-            halves * 3 + [weight(units, width, d) for d in (0, before, after)] * 2,
+            [lane(width)] * count + [weight(units, width, d) for d in ahead] * 2,
             (rows(units, F32), rows(units, F32)),
-            12 * part * area,
-            12 * area,
-        )(at, oh, ol, lh, ll, rh, rl, wg, wg, wg, wu, wu, wu)
-        return gate, up, fh, fl
-
-    def far(part, gate, up, fh, fl):
-        rows = lambda n, kind: shape((n, part), kind)
+            4 * count * part * area,
+            4 * count * area,
+        )(at, *blocks, *[wg] * count, *[wu] * count)
+
+    def far(sums, blocks, ahead):
+        count = len(blocks)
         return staged(
             far_kernel,
-            [lane(units)] * 2 + halves + [opposite, opposite, weight(width, units, across)],
-            (rows(units, BF), rows(cut, BF), rows(rest, BF)),
-            6 * part * area,
-            6 * area,
-        )(at, gate, up, fh, fl, wg, wu, wd)
-
-    def near(part, hidden):
-        rows = lambda n, kind: shape((n, part), kind)
+            [lane(units)] * 2
+            + [weight(width, units, across)]
+            + [lane(width)] * count
+            + [weight(units, width, d) for d in ahead] * 2,
+            (rows(units, BF), rows(width, BF)),
+            (4 * count + 2) * part * area,
+            (4 * count + 2) * area,
+        )(at, *sums, wd, *blocks, *[wg] * count, *[wu] * count)
+
+    def near(hidden, kinds):
         return staged(
             near_kernel,
             [lane(units)] + [weight(width, units, d) for d in (0, before, after)],
-            (rows(cut, F32), rows(rest, BF), rows(cut, BF), rows(rest, F32), rows(width, F32)),
+            tuple(rows(width, kind) for kind in kinds),
             6 * part * area,
             6 * area,
         )(at, hidden, wd, wd, wd)
@@ -388,31 +368,27 @@
     def add(mine, came):
         return (mine + came.astype(F32)).astype(BF)
 
-    first = ring(parts[0], *own)
-    second = ring(parts[1], *more)
-    first, ready = lax.optimization_barrier((first, second[:2]))
-    second = (*ready, *second[2:])
-    hidden_a, high_a, low_a = far(parts[0], *first)
-    to_right_a, to_left_a = right(low_a), left(high_a)
-    lha, lla, rha, rla, own_a = near(parts[0], hidden_a)
-    straight_a = right(rha), left(lla)
-    hidden_b, high_b, low_b = far(parts[1], *second)
-    to_right_b, to_left_b = right(low_b), left(high_b)
-    sum_right, sum_left = add(rla, to_right_a), add(lha, to_left_a)
-    added_a = right(sum_right), left(sum_left)
-    sums_a = own_a, straight_a[0], *added_a, straight_a[1]
-    lhb, llb, rhb, rlb, own_b = near(parts[1], hidden_b)
-    straight_b = right(rhb), left(llb)
-    sums_b = (
-        own_b,
-        straight_b[0],
-        right(add(rlb, to_right_b)),
-        left(add(lhb, to_left_b)),
-        straight_b[1],
-    )
-    sums = sums_a + sums_b
+    below_a, above_a = right(own_a), left(own_a)
+    above_b = left(own_b)
+    far_a = right(below_a)
+    below_b = right(own_b)
+    far_b = left(above_b)
+    sums_a = mid((own_a, below_a, above_a), (0, before, after))
+    hidden_a, share_a = far(sums_a, (far_a,), (across,))
+    crossed_a = right(share_a)
+    mine_a, left_a, right_a = near(hidden_a, (F32, BF, F32))
+    from_right_a = left(left_a)
+    sums_b = mid((own_b, above_b), (0, after))
+    hidden_b, share_b = far(sums_b, (below_b, far_b), (before, across))
+    crossed_b = left(share_b)
+    mine_b, left_b, right_b = near(hidden_b, (F32, F32, BF))
+    from_left_b = right(right_b)
+    added_a, added_b = add(right_a, crossed_a), add(left_b, crossed_b)
+    from_left_a = right(added_a)
+    from_right_b = left(added_b)
+    sums = (mine_a, from_left_a, from_right_a, mine_b, from_left_b, from_right_b)
     answers = run(
-        lambda *refs: place_kernel(lay, *refs), [VMEM] * 11, packed, gather_work
+        lambda *refs: place_kernel(lay, *refs), [VMEM] * 7, packed, gather_work
     )(slot, *sums)
     return run(
         lambda *refs: mix_kernel(lay, *refs),

time: 191 us -> 183 us (0.958)
  starting transfers between devices: 45.2 us -> 26.1 us
  waiting for transfers between devices: 43.8 us -> 62.4 us
  local copies, waits for them, and re-layouts: 14.4 us -> 6.93 us
    ppermute x24 -> x12, starting transfers between devices: 34 us -> 15 us  [shifted(): return lambda array: lax.ppermute(array, 'attn', pairs)]
    ppermute x24 -> x12, waiting for transfers between devices: 28.4 us -> 46.9 us  [shifted(): return lambda array: lax.ppermute(array, 'attn', pairs)]
    unnamed x36 -> x24, local copies, waits for them, and re-layouts: 13.1 us -> 5.68 us
    pallas_call x6, Pallas kernels: 19.1 us -> 17.1 us  [the longest x2 7.11 us: mid(): staged(mid_kernel, [lane(width)] * count + [weight(units, width, d) for d...]
  transfers between devices with their start and end apart: 25 -> 13, of which waited for: 5 -> 8; matrix products, arithmetic and copies ran while one was open for 1% -> 1% of each run, Pallas kernels for 17% -> 16%
where the time goes in v1:
time: 183 us; the launch traced here: 182 us
  waiting for transfers between devices  62.4 us (34%)
  Pallas kernels  41.9 us (23%)
  blocking collectives  41.2 us (23%)
  starting transfers between devices  26.1 us (14%)
  local copies, waits for them, and re-layouts  6.93 us (4%)
  between operations  3.31 us (2%)
    ppermute x12, waiting for transfers between devices, shifted(): return lambda array: lax.ppermute(array, 'attn', pairs)  46.9 us
    all_to_all x1, blocking collectives, exchange(): lax.all_to_all(blocks, ATTN_EXPERT, split_axis=0, concat_axis=0, tiled=True)  41.2 us
    all_to_all x1, waiting for transfers between devices, exchange(): lax.all_to_all(blocks, ATTN_EXPERT, split_axis=0, concat_axis=0, tiled=True)  15.6 us
    ppermute x12, starting transfers between devices, shifted(): return lambda array: lax.ppermute(array, 'attn', pairs)  15 us
    pallas_call x1, Pallas kernels, on_device(): pl.pallas_call(relay_kernel, grid=(pl.cdiv(units, step),), out_shape=(rel...  13.3 us
    all_to_all x1, starting transfers between devices, exchange(): lax.all_to_all(blocks, ATTN_EXPERT, split_axis=0, concat_axis=0, tiled=True)  11.2 us
    pallas_call x2, Pallas kernels, mid(): staged(mid_kernel, [lane(width)] * count + [weight(units, width, d) for d...  7.11 us
    unnamed x24, local copies, waits for them, and re-layouts  5.68 us
  transfers between devices with their start and end apart: 13, of which 8 were waited for; matrix products, arithmetic and copies ran while one was open for 1% of the time, Pallas kernels for 16%

profile of v1, /device:TPU:0, one launch (start us, length us, event | category | flops | bytes accessed | tf_op | source)
XLA Modules:
  0.0 182.2 jit_solution(9835845064046450064)
XLA Ops:
  0.0 3.6 %shard_map.82 = (bf16[1024,1152]{1,0:T(8,128)(2,1)}, f32[8,128]{1,0:T(8,128)}) custom-call(bf16[32,2880]{1,0:T(8,128)(2,1)} %refs_0_.1, s32[4,32]{1,0:T(4,128)} %bitcast.23), custom_call_target="tpu_custom_call" | custom-call | flops 47185920 | bytes 1474560 | tf_op jit(solution)/shard_map/pallas_call | solution.py:277
  3.6 0.0 copy-start.7
  3.6 0.0 copy-start.6
  3.6 11.2 %all-to-all-start = ((bf16[128,8,1152]{2,1,0:T(8,128)(2,1)}), bf16[128,8,1152]{2,1,0:T(8,128)(2,1)S(1)}, u32[]{:S(2)}, u32[]{:S(2)}) async-start(bf16[128,8,1152]{2,1,0:T(8,128)(2,1)} %bitcast.26), calls=%async_computation | async-start | bytes 4718592 | tf_op jit(solution)/shard_map/all_to_all | solution.py:273
  14.8 0.0 copy-done.7
  14.8 0.6 dynamic_slice.9
  17.3 0.0 copy-done.6
  17.3 0.6 fusion
  19.2 13.3 %relay.1 = (bf16[4,720,720]{2,1,0:T(8,128)(2,1)}, bf16[4,720,720]{2,1,0:T(8,128)(2,1)}, bf16[4,720,720]{2,1,0:T(8,128)(2,1)}) custom-call(f32[8,128]{1,0:T(8,128)} %get-tuple-element.32.seen_ref, bf16[720,2880]{1,0:T(8,128)(2,1)} %bitcast.27, bf16[720,2880]{1,0:T(8,128)(2,1)} %bitcast.28, bf16[720,2880]{1,0:T(8,128)(2,1)} %bitcast.29), custom_call_target="tpu_custom_call" | custom-call | flops 4777574400 | bytes 24883200 | tf_op jit(solution)/shard_map/relay/pallas_call | solution.py:289
  32.5 15.6 %all-to-all-done = bf16[128,8,1152]{2,1,0:T(8,128)(2,1)S(1)} async-done(((bf16[128,8,1152]{2,1,0:T(8,128)(2,1)}), bf16[128,8,1152]{2,1,0:T(8,128)(2,1)S(1)}, u32[]{:S(2)}, u32[]{:S(2)}) %all-to-all-start) | async-done | bytes 2359328 | tf_op jit(solution)/shard_map/all_to_all | solution.py:273
  48.0 2.2 %shard_map.83 = (f32[8,1024]{1,0:T(8,128)S(1)}, f32[1024,8]{1,0:T(8,128)S(1)}, bf16[720,384]{1,0:T(8,128)(2,1)S(1)}) custom-call(bf16[1024,1152]{1,0:T(8,128)(2,1)S(1)} %bitcast.21, s32[1]{0:T(128)S(6)} %add.27.refs_1_), custom_call_target="tpu_custom_call" | custom-call | flops 1132462080 | bytes 1474560 | tf_op jit(solution)/shard_map/pallas_call | solution.py:304
  50.2 0.0 copy-start.2
  50.2 0.8 copy-done.2
  51.0 1.7 shard_map.87.refs_0_
  52.7 1.2 collective-permute-start.6
  53.8 0.9 collective-permute-start
  54.8 0.5 collective-permute-start.7
  55.3 11.1 %collective-permute-done.6.refs_1_ = bf16[720,384]{1,0:T(8,128)(2,1)S(1)} collective-permute-done((bf16[720,384]{1,0:T(8,128)(2,1)S(1)}, bf16[720,384]{1,0:T(8,128)(2,1)S(1)}, u32[]{:S(2)}, u32[]{:S(2)}) %collective-permute-start.6) | collective-permute-done | bytes 552992 | tf_op jit(solution)/shard_map/ppermute | solution.py:267
  66.4 2.4 %collective-permute-start.8 = (bf16[720,384]{1,0:T(8,128)(2,1)S(1)}, bf16[720,384]{1,0:T(8,128)(2,1)S(1)}, u32[]{:S(2)}, u32[]{:S(2)}) collective-permute-start(bf16[720,384]{1,0:T(8,128)(2,1)S(1)} %collective-permute-done.6.refs_1_), channel_id=1, source_target_pairs={{0,96},{32,0},{64,32},{96,64},{1,97},{33,1},{65,33},{97,65},{2,98}... | collective-permute-start | bytes 1658888 | tf_op jit(solution)/shard_map/ppermute | solution.py:267
  68.9 0.0 collective-permute-start.1
  68.9 1.6 collective-permute-done.refs_1_
  70.5 0.4 collective-permute-start.2
  70.9 0.0 slice-start
  70.9 0.0 copy-start
  70.9 2.4 %copy-done = bf16[4,720,720]{2,1,0:T(8,128)(2,1)S(1)} copy-done((bf16[4,720,720]{2,1,0:T(8,128)(2,1)S(1)}, bf16[4,720,720]{2,1,0:T(8,128)(2,1)}, u32[]{:S(2)}) %copy-start) | copy-done | bytes 4147224
  73.3 0.0 copy-start.1
  73.3 2.4 %copy-done.1 = bf16[4,720,720]{2,1,0:T(8,128)(2,1)S(1)} copy-done((bf16[4,720,720]{2,1,0:T(8,128)(2,1)S(1)}, bf16[4,720,720]{2,1,0:T(8,128)(2,1)}, u32[]{:S(2)}) %copy-start.1) | copy-done | bytes 4147224
  75.7 2.5 %shard_map.88 = (f32[720,384]{1,0:T(8,128)S(1)}, f32[720,384]{1,0:T(8,128)S(1)}) custom-call(s32[1]{0:T(128)} %bitcast.9.at_ref, bf16[720,384]{1,0:T(8,128)(2,1)S(1)} %shard_map.87.refs_0_, bf16[720,384]{1,0:T(8,128)(2,1)S(1)} %collective-permute-done.6.refs_1_, bf16[4,720,720]{2,1,0:T(8,128)(2,1)S(1)} %copy-done, bf16[4,720,720]{2,1,0:T(8,128)(2,1)S(1)} %copy-done, ...), custom_call_target="tpu_custom_call" | custom-call | flops 1592524800 | bytes 4147200 | tf_op jit(solution)/shard_map/pallas_call | solution.py:338
  78.2 4.1 %collective-permute-done.7.refs_0_ = bf16[720,384]{1,0:T(8,128)(2,1)S(1)} collective-permute-done((bf16[720,384]{1,0:T(8,128)(2,1)S(1)}, bf16[720,384]{1,0:T(8,128)(2,1)S(1)}, u32[]{:S(2)}, u32[]{:S(2)}) %collective-permute-start.7) | collective-permute-done | bytes 552992 | tf_op jit(solution)/shard_map/ppermute | solution.py:267
  82.3 0.0 collective-permute-done.8.refs_1_
  82.3 0.0 slice-done
  82.3 0.0 slice-done.1
  82.3 0.0 slice-start.3
  82.4 3.2 %shard_map.89 = (bf16[720,384]{1,0:T(8,128)(2,1)S(1)}, bf16[720,384]{1,0:T(8,128)(2,1)S(1)}) custom-call(s32[1]{0:T(128)} %bitcast.9.at_ref, f32[720,384]{1,0:T(8,128)S(1)} %get-tuple-element.50.g_ref, f32[720,384]{1,0:T(8,128)S(1)} %get-tuple-element.51.u_ref, bf16[4,720,720]{2,1,0:T(8,128)(2,1)S(1)} %bitcast.16, ...), custom_call_target="tpu_custom_call" | custom-call | flops 1990656000 | bytes 5184000 | tf_op jit(solution)/shard_map/pallas_call | solution.py:348
  85.6 3.2 %collective-permute-start.10 = (bf16[720,384]{1,0:T(8,128)(2,1)S(1)}, bf16[720,384]{1,0:T(8,128)(2,1)S(1)}, u32[]{:S(2)}, u32[]{:S(2)}) collective-permute-start(bf16[720,384]{1,0:T(8,128)(2,1)S(1)} %get-tuple-element.56), channel_id=1, source_target_pairs={{0,96},{32,0},{64,32},{96,64},{1,97},{33,1},{65,33},{97,65},{2,98}... | collective-permute-start | bytes 1658888 | tf_op jit(solution)/shard_map/ppermute | solution.py:267
  88.8 5.0 %collective-permute-done.1.refs_2_ = bf16[720,384]{1,0:T(8,128)(2,1)} collective-permute-done((bf16[720,384]{1,0:T(8,128)(2,1)S(1)}, bf16[720,384]{1,0:T(8,128)(2,1)}, u32[]{:S(2)}, u32[]{:S(2)}) %collective-permute-start.1) | collective-permute-done | bytes 552992 | tf_op jit(solution)/shard_map/ppermute | solution.py:267
  93.8 0.0 slice-done.2
  93.8 0.0 slice-done.3
  93.8 4.7 %shard_map.84 = (f32[720,384]{1,0:T(8,128)S(1)}, f32[720,384]{1,0:T(8,128)S(1)}) custom-call(s32[1]{0:T(128)} %bitcast.9.at_ref, bf16[720,384]{1,0:T(8,128)(2,1)S(1)} %get-tuple-element.38.refs_0_, bf16[720,384]{1,0:T(8,128)(2,1)S(1)} %collective-permute-done.refs_1_, bf16[720,384]{1,0:T(8,128)(2,1)} %collective-permute-done.1.refs_2_, ...), custom_call_target="tpu_custom_call" | custom-call | flops 2388787200 | bytes 6220800 | tf_op jit(solution)/shard_map/pallas_call | solution.py:338
  98.5 0.0 collective-permute-done.2.refs_0_
  98.5 2.0 %shard_map.85 = (bf16[720,384]{1,0:T(8,128)(2,1)S(1)}, bf16[720,384]{1,0:T(8,128)(2,1)S(1)}) custom-call(s32[1]{0:T(128)} %bitcast.9.at_ref, f32[720,384]{1,0:T(8,128)S(1)} %get-tuple-element.41.g_ref, f32[720,384]{1,0:T(8,128)S(1)} %get-tuple-element.42.u_ref, bf16[4,720,720]{2,1,0:T(8,128)(2,1)S(1)} %bitcast.16, ...), custom_call_target="tpu_custom_call" | custom-call | flops 1194393600 | bytes 3110400 | tf_op jit(solution)/shard_map/pallas_call | solution.py:348
  100.4 0.6 collective-permute-start.3
  101.1 1.9 %shard_map.90 = (f32[720,384]{1,0:T(8,128)S(1)}, f32[720,384]{1,0:T(8,128)S(1)}, bf16[720,384]{1,0:T(8,128)(2,1)S(1)}) custom-call(s32[1]{0:T(128)} %bitcast.9.at_ref, bf16[720,384]{1,0:T(8,128)(2,1)S(1)} %get-tuple-element.52.h_ref, bf16[4,720,720]{2,1,0:T(8,128)(2,1)S(1)} %bitcast.16, bf16[4,720,720]{2,1,0:T(8,128)(2,1)S(1)} %bitcast.16, ...), custom_call_target="tpu_custom_call" | custom-call | flops 1194393600 | bytes 3110400 | tf_op jit(solution)/shard_map/pallas_call | solution.py:360
  102.9 1.4 collective-permute-start.9
  104.3 1.9 %shard_map.86 = (f32[720,384]{1,0:T(8,128)S(1)}, bf16[720,384]{1,0:T(8,128)(2,1)S(1)}, f32[720,384]{1,0:T(8,128)S(1)}) custom-call(s32[1]{0:T(128)} %bitcast.9.at_ref, bf16[720,384]{1,0:T(8,128)(2,1)S(1)} %get-tuple-element.44.h_ref, bf16[4,720,720]{2,1,0:T(8,128)(2,1)S(1)} %bitcast.16, bf16[4,720,720]{2,1,0:T(8,128)(2,1)S(1)} %bitcast.16, ...), custom_call_target="tpu_custom_call" | custom-call | flops 1194393600 | bytes 3110400 | tf_op jit(solution)/shard_map/pallas_call | solution.py:360
  106.2 2.0 %collective-permute-start.5 = (bf16[720,384]{1,0:T(8,128)(2,1)S(1)}, bf16[720,384]{1,0:T(8,128)(2,1)S(1)}, u32[]{:S(2)}, u32[]{:S(2)}) collective-permute-start(bf16[720,384]{1,0:T(8,128)(2,1)S(1)} %get-tuple-element.48), channel_id=1, source_target_pairs={{0,96},{32,0},{64,32},{96,64},{1,97},{33,1},{65,33},{97,65},{2,98}... | collective-permute-start | bytes 1658888 | tf_op jit(solution)/shard_map/ppermute | solution.py:267
  108.2 0.0 collective-permute-done.10
  108.2 0.1 add_convert_fusion
  108.3 2.2 %collective-permute-start.11 = (bf16[720,384]{1,0:T(8,128)(2,1)S(1)}, bf16[720,384]{1,0:T(8,128)(2,1)S(1)}, u32[]{:S(2)}, u32[]{:S(2)}) collective-permute-start(bf16[720,384]{1,0:T(8,128)(2,1)S(1)} %add_convert_fusion), channel_id=1, source_target_pairs={{0,96},{32,0},{64,32},{96,64},{1,97},{33,1},{65,33},{97,65},{2,98}... | collective-permute-start | bytes 1658888 | tf_op jit(solution)/shard_map/ppermute | solution.py:267
  110.5 7.0 %collective-permute-done.3 = bf16[720,384]{1,0:T(8,128)(2,1)S(1)} collective-permute-done((bf16[720,384]{1,0:T(8,128)(2,1)S(1)}, bf16[720,384]{1,0:T(8,128)(2,1)S(1)}, u32[]{:S(2)}, u32[]{:S(2)}) %collective-permute-start.3) | collective-permute-done | bytes 552992 | tf_op jit(solution)/shard_map/ppermute | solution.py:267
  117.5 0.1 add_convert_fusion.1
  117.7 0.1 collective-permute-start.4
  117.8 11.6 %collective-permute-done.9.refs_5_ = bf16[720,384]{1,0:T(8,128)(2,1)S(1)} collective-permute-done((bf16[720,384]{1,0:T(8,128)(2,1)S(1)}, bf16[720,384]{1,0:T(8,128)(2,1)S(1)}, u32[]{:S(2)}, u32[]{:S(2)}) %collective-permute-start.9) | collective-permute-done | bytes 552992 | tf_op jit(solution)/shard_map/ppermute | solution.py:267
  129.4 0.0 collective-permute-done.5.refs_3_
  129.4 0.0 collective-permute-done.11.refs_6_
  129.4 6.4 %collective-permute-done.4.refs_2_ = bf16[720,384]{1,0:T(8,128)(2,1)S(1)} collective-permute-done((bf16[720,384]{1,0:T(8,128)(2,1)S(1)}, bf16[720,384]{1,0:T(8,128)(2,1)S(1)}, u32[]{:S(2)}, u32[]{:S(2)}) %collective-permute-start.4) | collective-permute-done | bytes 552992 | tf_op jit(solution)/shard_map/ppermute | solution.py:267
  135.8 0.0 copy-done.3
  135.8 3.2 %shard_map.91 = bf16[1024,1152]{1,0:T(8,128)(2,1)S(1)} custom-call(f32[1024,8]{1,0:T(8,128)S(1)} %copy-done.3, f32[720,384]{1,0:T(8,128)S(1)} %get-tuple-element.45.refs_1_, bf16[720,384]{1,0:T(8,128)(2,1)S(1)} %collective-permute-done.4.refs_2_, bf16[720,384]{1,0:T(8,128)(2,1)S(1)} %collective-permute-done.5.refs_3_, ...), custom_call_target="tpu_custom_call" | custom-call | flops 1132462080 | bytes 1474560 | tf_op jit(solution)/shard_map/pallas_call | solution.py:390
  139.0 0.0 copy-start.4
  139.0 0.0 copy-start.5
  139.0 41.2 %all_to_all.10 = bf16[128,8,1152]{2,1,0:T(8,128)(2,1)S(1)} all-to-all(bf16[128,8,1152]{2,1,0:T(8,128)(2,1)S(1)} %bitcast.19), channel_id=1, replica_groups=mesh['attn'=4,'expert_0'=4,'expert_1'=4,'expert_2'=2] {'attn','expert_0'..., dimensions={0} | all-to-all | bytes 4718592 | tf_op jit(solution)/shard_map/all_to_all | solution.py:273
  180.2 0.0 copy-done.4
  180.3 0.0 copy-done.5
  180.3 1.9 %shard_map.92 = bf16[32,2880]{1,0:T(8,128)(2,1)} custom-call(bf16[1024,1152]{1,0:T(8,128)(2,1)S(1)} %bitcast.20, s32[4,32]{1,0:T(4,128)S(1)} %bitcast.24, f32[4,32]{1,0:T(4,128)S(1)} %bitcast.25), custom_call_target="tpu_custom_call" | custom-call | flops 141557760 | bytes 1474560 | tf_op jit(solution)/shard_map/pallas_call | solution.py:393
  (5 shorter events, 0.0 us)
Async XLA Ops:
  3.6 11.2 %copy-start.7 = (s32[32]{0:T(128)S(1)}, s32[32]{0:T(128)}, u32[]{:S(2)}) copy-start(s32[32]{0:T(128)} %param.12) | copy-start | bytes 388
  3.6 13.7 %copy-start.6 = (s32[32]{0:T(128)S(1)}, s32[32]{0:T(128)}, u32[]{:S(2)}) copy-start(s32[32]{0:T(128)} %param.11) | copy-start | bytes 388
  3.6 44.4 %all-to-all-start = ((bf16[128,8,1152]{2,1,0:T(8,128)(2,1)}), bf16[128,8,1152]{2,1,0:T(8,128)(2,1)S(1)}, u32[]{:S(2)}, u32[]{:S(2)}) async-start(bf16[128,8,1152]{2,1,0:T(8,128)(2,1)} %bitcast.26), calls=%async_computation | async-start | bytes 4718592 | tf_op jit(solution)/shard_map/all_to_all | solution.py:273
  50.2 0.8 copy-start.2
  52.7 13.8 %collective-permute-start.6 = (bf16[720,384]{1,0:T(8,128)(2,1)S(1)}, bf16[720,384]{1,0:T(8,128)(2,1)S(1)}, u32[]{:S(2)}, u32[]{:S(2)}) collective-permute-start(bf16[720,384]{1,0:T(8,128)(2,1)S(1)} %shard_map.87.refs_0_), channel_id=1, source_target_pairs={{0,96},{32,0},{64,32},{96,64},{1,97},{33,1},{65,33},{97,65},{2,98}... | collective-permute-start | bytes 1658888 | tf_op jit(solution)/shard_map/ppermute | solution.py:267
  53.8 16.6 %collective-permute-start = (bf16[720,384]{1,0:T(8,128)(2,1)S(1)}, bf16[720,384]{1,0:T(8,128)(2,1)S(1)}, u32[]{:S(2)}, u32[]{:S(2)}) collective-permute-start(bf16[720,384]{1,0:T(8,128)(2,1)S(1)} %get-tuple-element.38.refs_0_), channel_id=1, source_target_pairs={{0,32},{32,64},{64,96},{96,0},{1,33},{33,65},{65,97},{97,1},{2,34}... | collective-permute-start | bytes 1658888 | tf_op jit(solution)/shard_map/ppermute | solution.py:267
  54.8 27.6 %collective-permute-start.7 = (bf16[720,384]{1,0:T(8,128)(2,1)S(1)}, bf16[720,384]{1,0:T(8,128)(2,1)S(1)}, u32[]{:S(2)}, u32[]{:S(2)}) collective-permute-start(bf16[720,384]{1,0:T(8,128)(2,1)S(1)} %shard_map.87.refs_0_), channel_id=1, source_target_pairs={{0,32},{32,64},{64,96},{96,0},{1,33},{33,65},{65,97},{97,1},{2,34}... | collective-permute-start | bytes 1658888 | tf_op jit(solution)/shard_map/ppermute | solution.py:267
  66.4 15.9 %collective-permute-start.8 = (bf16[720,384]{1,0:T(8,128)(2,1)S(1)}, bf16[720,384]{1,0:T(8,128)(2,1)S(1)}, u32[]{:S(2)}, u32[]{:S(2)}) collective-permute-start(bf16[720,384]{1,0:T(8,128)(2,1)S(1)} %collective-permute-done.6.refs_1_), channel_id=1, source_target_pairs={{0,96},{32,0},{64,32},{96,64},{1,97},{33,1},{65,33},{97,65},{2,98}... | collective-permute-start | bytes 1658888 | tf_op jit(solution)/shard_map/ppermute | solution.py:267
  68.9 24.9 %collective-permute-start.1 = (bf16[720,384]{1,0:T(8,128)(2,1)S(1)}, bf16[720,384]{1,0:T(8,128)(2,1)}, u32[]{:S(2)}, u32[]{:S(2)}) collective-permute-start(bf16[720,384]{1,0:T(8,128)(2,1)S(1)} %get-tuple-element.38.refs_0_), channel_id=1, source_target_pairs={{0,96},{32,0},{64,32},{96,64},{1,97},{33,1},{65,33},{97,65},{2,98}... | collective-permute-start | bytes 1658888 | tf_op jit(solution)/shard_map/ppermute | solution.py:267
  70.5 28.0 %collective-permute-start.2 = (bf16[720,384]{1,0:T(8,128)(2,1)S(1)}, bf16[720,384]{1,0:T(8,128)(2,1)S(1)}, u32[]{:S(2)}, u32[]{:S(2)}) collective-permute-start(bf16[720,384]{1,0:T(8,128)(2,1)S(1)} %collective-permute-done.refs_1_), channel_id=1, source_target_pairs={{0,32},{32,64},{64,96},{96,0},{1,33},{33,65},{65,97},{97,1},{2,34}... | collective-permute-start | bytes 1658888 | tf_op jit(solution)/shard_map/ppermute | solution.py:267
  70.9 11.4 %slice-start = ((s8[4423680]{0:T(1024)(128)(4,1)}), s8[4194304]{0:T(1024)(128)(4,1)S(1)}, s32[]{:S(2)}) async-start(s8[4423680]{0:T(1024)(128)(4,1)} %bitcast.15), calls=%async_computation.2 | async-start | bytes 8388608
  70.9 2.4 %copy-start = (bf16[4,720,720]{2,1,0:T(8,128)(2,1)S(1)}, bf16[4,720,720]{2,1,0:T(8,128)(2,1)}, u32[]{:S(2)}) copy-start(bf16[4,720,720]{2,1,0:T(8,128)(2,1)} %get-tuple-element.39.refs_3_.refs_4_.refs_5_.refs_1_.refs_2_) | copy-start | bytes 12441604
  73.3 2.4 %copy-start.1 = (bf16[4,720,720]{2,1,0:T(8,128)(2,1)S(1)}, bf16[4,720,720]{2,1,0:T(8,128)(2,1)}, u32[]{:S(2)}) copy-start(bf16[4,720,720]{2,1,0:T(8,128)(2,1)} %get-tuple-element.40.refs_6_.refs_7_.refs_8_.refs_2_.refs_4_.refs_5_) | copy-start | bytes 12441604
  75.7 6.6 %slice-start.1 = ((s8[4423680]{0:T(1024)(128)(4,1)}), s8[229376]{0:T(1024)(128)(4,1)S(1)}, s32[]{:S(2)}) async-start(s8[4423680]{0:T(1024)(128)(4,1)} %bitcast.15), calls=%async_computation.3 | async-start | bytes 458752
  82.3 11.5 %slice-start.2 = ((s8[4423680]{0:T(1024)(128)(4,1)}), s8[4194304]{0:T(1024)(128)(4,1)S(1)}, s32[]{:S(2)}) async-start(s8[4423680]{0:T(1024)(128)(4,1)} %bitcast.17), calls=%async_computation.4 | async-start | bytes 8388608
  82.3 11.5 %slice-start.3 = ((s8[4423680]{0:T(1024)(128)(4,1)}), s8[229376]{0:T(1024)(128)(4,1)S(1)}, s32[]{:S(2)}) async-start(s8[4423680]{0:T(1024)(128)(4,1)} %bitcast.17), calls=%async_computation.5 | async-start | bytes 458752
  85.6 22.6 %collective-permute-start.10 = (bf16[720,384]{1,0:T(8,128)(2,1)S(1)}, bf16[720,384]{1,0:T(8,128)(2,1)S(1)}, u32[]{:S(2)}, u32[]{:S(2)}) collective-permute-start(bf16[720,384]{1,0:T(8,128)(2,1)S(1)} %get-tuple-element.56), channel_id=1, source_target_pairs={{0,96},{32,0},{64,32},{96,64},{1,97},{33,1},{65,33},{97,65},{2,98}... | collective-permute-start | bytes 1658888 | tf_op jit(solution)/shard_map/ppermute | solution.py:267
  100.4 17.1 %collective-permute-start.3 = (bf16[720,384]{1,0:T(8,128)(2,1)S(1)}, bf16[720,384]{1,0:T(8,128)(2,1)S(1)}, u32[]{:S(2)}, u32[]{:S(2)}) collective-permute-start(bf16[720,384]{1,0:T(8,128)(2,1)S(1)} %get-tuple-element.47), channel_id=1, source_target_pairs={{0,32},{32,64},{64,96},{96,0},{1,33},{33,65},{65,97},{97,1},{2,34}... | collective-permute-start | bytes 1658888 | tf_op jit(solution)/shard_map/ppermute | solution.py:267
  102.9 26.5 %collective-permute-start.9 = (bf16[720,384]{1,0:T(8,128)(2,1)S(1)}, bf16[720,384]{1,0:T(8,128)(2,1)S(1)}, u32[]{:S(2)}, u32[]{:S(2)}) collective-permute-start(bf16[720,384]{1,0:T(8,128)(2,1)S(1)} %get-tuple-element.54), channel_id=1, source_target_pairs={{0,32},{32,64},{64,96},{96,0},{1,33},{33,65},{65,97},{97,1},{2,34}... | collective-permute-start | bytes 1658888 | tf_op jit(solution)/shard_map/ppermute | solution.py:267
  106.2 23.2 %collective-permute-start.5 = (bf16[720,384]{1,0:T(8,128)(2,1)S(1)}, bf16[720,384]{1,0:T(8,128)(2,1)S(1)}, u32[]{:S(2)}, u32[]{:S(2)}) collective-permute-start(bf16[720,384]{1,0:T(8,128)(2,1)S(1)} %get-tuple-element.48), channel_id=1, source_target_pairs={{0,96},{32,0},{64,32},{96,64},{1,97},{33,1},{65,33},{97,65},{2,98}... | collective-permute-start | bytes 1658888 | tf_op jit(solution)/shard_map/ppermute | solution.py:267
  108.3 21.1 %collective-permute-start.11 = (bf16[720,384]{1,0:T(8,128)(2,1)S(1)}, bf16[720,384]{1,0:T(8,128)(2,1)S(1)}, u32[]{:S(2)}, u32[]{:S(2)}) collective-permute-start(bf16[720,384]{1,0:T(8,128)(2,1)S(1)} %add_convert_fusion), channel_id=1, source_target_pairs={{0,96},{32,0},{64,32},{96,64},{1,97},{33,1},{65,33},{97,65},{2,98}... | collective-permute-start | bytes 1658888 | tf_op jit(solution)/shard_map/ppermute | solution.py:267
  117.5 18.2 %copy-start.3 = (f32[1024,8]{1,0:T(8,128)S(1)}, f32[1024,8]{1,0:T(8,128)}, u32[]{:S(2)}) copy-start(f32[1024,8]{1,0:T(8,128)} %copy-done.2) | copy-start | bytes 98308
  117.7 18.1 %collective-permute-start.4 = (bf16[720,384]{1,0:T(8,128)(2,1)S(1)}, bf16[720,384]{1,0:T(8,128)(2,1)S(1)}, u32[]{:S(2)}, u32[]{:S(2)}) collective-permute-start(bf16[720,384]{1,0:T(8,128)(2,1)S(1)} %add_convert_fusion.1), channel_id=1, source_target_pairs={{0,32},{32,64},{64,96},{96,0},{1,33},{33,65},{65,97},{97,1},{2,34}... | collective-permute-start | bytes 1658888 | tf_op jit(solution)/shard_map/ppermute | solution.py:267
  139.0 41.3 %copy-start.4 = (s32[32,4]{0,1:T(4,128)S(1)}, s32[32,4]{0,1:T(4,128)}, u32[]{:S(2)}) copy-start(s32[32,4]{0,1:T(4,128)} %param.9) | copy-start | bytes 1540
  139.0 41.3 %copy-start.5 = (f32[32,4]{0,1:T(4,128)S(1)}, f32[32,4]{0,1:T(4,128)}, u32[]{:S(2)}) copy-start(f32[32,4]{0,1:T(4,128)} %param.10) | copy-start | bytes 1540

commit v2 on v1

--- a/solution.py
+++ b/solution.py
@@ -115,35 +115,36 @@
         do_ref[b] = d_ref[:, at].T
 
 
-def gate_up(refs):
-    count = len(refs) // 3
+def gate_up(at, ahead, wg_ref, wu_ref, blocks):
     gate = up = None
-    for x, wg, wu in zip(refs[:count], refs[count : 2 * count], refs[2 * count :]):
-        g, u = dot(wg[0], x[...]), dot(wu[0], x[...])
+    for distance, x in zip(ahead, blocks):
+        block = lax.rem(at + distance, wg_ref.shape[0])
+        g, u = dot(wg_ref[block], x[...]), dot(wu_ref[block], x[...])
         gate, up = (g, u) if gate is None else (gate + g, up + u)
     return gate, up
 
 
-def mid_kernel(at_ref, *refs):
-    del at_ref
-    refs[-2][...], refs[-1][...] = gate_up(refs[:-2])
-
-
-def far_kernel(at_ref, g_ref, u_ref, wd_ref, *refs):
-    del at_ref
-    gate, up = gate_up(refs[:-2])
+def mid_kernel(ahead, at_ref, wg_ref, wu_ref, *refs):
+    refs[-2][...], refs[-1][...] = gate_up(at_ref[0], ahead, wg_ref, wu_ref, refs[:-2])
+
+
+def far_kernel(ahead, at_ref, wg_ref, wu_ref, wd_ref, g_ref, u_ref, *refs):
+    gate, up = gate_up(at_ref[0], ahead, wg_ref, wu_ref, refs[:-2])
     h_ref, o_ref = refs[-2:]
     gate, up = gate + g_ref[...], up + u_ref[...]
     hidden = (gate * jax.nn.sigmoid(SWISH_SCALE * gate) * (up + 1.0)).astype(BF)
     h_ref[...] = hidden
-    o_ref[...] = dot(wd_ref[0], hidden).astype(BF)
-
-
-def near_kernel(at_ref, h_ref, *refs):
-    del at_ref
+    groups = wd_ref.shape[0]
+    across = lax.rem(at_ref[0] + groups // 2, groups)
+    o_ref[...] = dot(wd_ref[across], hidden).astype(BF)
+
+
+def near_kernel(at_ref, h_ref, wd_ref, *outs):
     hidden = h_ref[...]
-    for weight, out in zip(refs[:3], refs[3:]):
-        out[...] = dot(weight[0], hidden).astype(out.dtype)
+    groups = wd_ref.shape[0]
+    for distance, out in zip((0, groups - 1, 1), outs):
+        block = lax.rem(at_ref[0] + distance, groups)
+        out[...] = dot(wd_ref[block], hidden).astype(out.dtype)
 
 
 def place_kernel(lay, slot_ref, *refs):
@@ -230,7 +231,7 @@
     return pltpu.CompilerParams(vmem_limit_bytes=mebibytes << 20)
 
 
-def run(kernel, ins, outs, work, scratch=(), mebibytes=24):
+def run(kernel, ins, outs, work, scratch=(), mebibytes=12):
     return pl.pallas_call(
         kernel,
         out_shape=outs,
@@ -310,60 +311,34 @@
     own_b = run(
         lambda *refs: pick_more_kernel(lay, part, *refs), [VMEM] * 2, columns, gather_work
     )(arrived, places)
-    lane = lambda rows: pl.BlockSpec((rows, part), lambda i, p: (0, 0))
-
-    def weight(rows, columns, ahead):
-        return pl.BlockSpec((1, rows, columns), lambda i, p: (lax.rem(p[0] + ahead, groups), 0, 0))
-
-    def staged(kernel, ins, outs, flops, moved):
-        return pl.pallas_call(
-            kernel,
-            grid_spec=pltpu.PrefetchScalarGridSpec(
-                num_scalar_prefetch=1,
-                grid=(1,),
-                in_specs=ins,
-                out_specs=tuple(lane(out.shape[0]) for out in outs),
-            ),
-            out_shape=outs,
-            cost_estimate=cost(flops, moved),
-            compiler_params=grant(32),
-        )
-
     before, after, across = groups - 1, 1, groups // 2
     area = width * units
     rows = lambda n, kind: shape((n, part), kind)
 
     def mid(blocks, ahead):
-        count = len(blocks)
-        return staged(
-            mid_kernel,
-            [lane(width)] * count + [weight(units, width, d) for d in ahead] * 2,
+        return run(
+            lambda *refs: mid_kernel(ahead, *refs),
+            [SMEM] + [VMEM] * (2 + len(blocks)),
             (rows(units, F32), rows(units, F32)),
-            4 * count * part * area,
-            4 * count * area,
-        )(at, *blocks, *[wg] * count, *[wu] * count)
+            (4 * len(blocks) * part * area, 4 * len(blocks) * area),
+        )(at, wg, wu, *blocks)
 
     def far(sums, blocks, ahead):
-        count = len(blocks)
-        return staged(
-            far_kernel,
-            [lane(units)] * 2
-            + [weight(width, units, across)]
-            + [lane(width)] * count
-            + [weight(units, width, d) for d in ahead] * 2,
+        count = 4 * len(blocks) + 2
+        return run(
+            lambda *refs: far_kernel(ahead, *refs),
+            [SMEM] + [VMEM] * (5 + len(blocks)),
             (rows(units, BF), rows(width, BF)),
-            (4 * count + 2) * part * area,
-            (4 * count + 2) * area,
-        )(at, *sums, wd, *blocks, *[wg] * count, *[wu] * count)
+            (count * part * area, count * area),
+        )(at, wg, wu, wd, *sums, *blocks)
 
     def near(hidden, kinds):
-        return staged(
+        return run(
             near_kernel,
-            [lane(units)] + [weight(width, units, d) for d in (0, before, after)],
+            [SMEM] + [VMEM] * 2,
             tuple(rows(width, kind) for kind in kinds),
-            6 * part * area,
-            6 * area,
-        )(at, hidden, wd, wd, wd)
+            (6 * part * area, 6 * area),
+        )(at, hidden, wd)
 
     def add(mine, came):
         return (mine + came.astype(F32)).astype(BF)

time: 183 us -> 182 us (level)
  transfers between devices with their start and end apart: 13 -> 13, of which waited for: 8 -> 9; matrix products, arithmetic and copies ran while one was open for 1% -> 1% of each run, Pallas kernels for 16% -> 16%
where the time goes in v2:
time: 182 us
  waiting for transfers between devices  61.1 us (34%)
  Pallas kernels  43 us (24%)
  blocking collectives  41.3 us (23%)
  starting transfers between devices  26.9 us (15%)
  local copies, waits for them, and re-layouts  5.8 us (3%)
  between operations  3.29 us (2%)
    ppermute x12, waiting for transfers between devices, shifted(): return lambda array: lax.ppermute(array, 'attn', pairs)  45.5 us
    all_to_all x1, blocking collectives, exchange(): lax.all_to_all(blocks, ATTN_EXPERT, split_axis=0, concat_axis=0, tiled=True)  41.3 us
    ppermute x12, starting transfers between devices, shifted(): return lambda array: lax.ppermute(array, 'attn', pairs)  15.7 us
    all_to_all x1, waiting for transfers between devices, exchange(): lax.all_to_all(blocks, ATTN_EXPERT, split_axis=0, concat_axis=0, tiled=True)  15.6 us
    pallas_call x1, Pallas kernels, on_device(): pl.pallas_call(relay_kernel, grid=(pl.cdiv(units, step),), out_shape=(rel...  13.2 us
    all_to_all x1, starting transfers between devices, exchange(): lax.all_to_all(blocks, ATTN_EXPERT, split_axis=0, concat_axis=0, tiled=True)  11.2 us
    pallas_call x2, Pallas kernels, mid(): run(lambda *refs: mid_kernel(ahead, *refs), [SMEM] + [VMEM] * (2 + len(bl...  7.44 us
    pallas_call x2, Pallas kernels, far(): run(lambda *refs: far_kernel(ahead, *refs), [SMEM] + [VMEM] * (5 + len(bl...  5.15 us
  transfers between devices with their start and end apart: 13, of which 9 were waited for; matrix products, arithmetic and copies ran while one was open for 1% of the time, Pallas kernels for 16%

profile of v2, /device:TPU:0, one launch (start us, length us, event | category | flops | bytes accessed | tf_op | source)
XLA Modules:
  0.0 181.6 jit_solution(8225073763493754697)
XLA Ops:
  0.0 3.6 %shard_map.82 = (bf16[1024,1152]{1,0:T(8,128)(2,1)}, f32[8,128]{1,0:T(8,128)}) custom-call(bf16[32,2880]{1,0:T(8,128)(2,1)} %refs_0_.1, s32[4,32]{1,0:T(4,128)} %bitcast.23), custom_call_target="tpu_custom_call" | custom-call | flops 47185920 | bytes 1474560 | tf_op jit(solution)/shard_map/pallas_call | solution.py:278
  3.6 0.0 copy-start.7
  3.6 0.0 copy-start.6
  3.6 11.2 %all-to-all-start = ((bf16[128,8,1152]{2,1,0:T(8,128)(2,1)}), bf16[128,8,1152]{2,1,0:T(8,128)(2,1)S(1)}, u32[]{:S(2)}, u32[]{:S(2)}) async-start(bf16[128,8,1152]{2,1,0:T(8,128)(2,1)} %bitcast.26), calls=%async_computation | async-start | bytes 4718592 | tf_op jit(solution)/shard_map/all_to_all | solution.py:274
  14.8 0.0 copy-done.7
  14.8 0.6 dynamic_slice.9
  17.3 0.0 copy-done.6
  17.3 0.6 fusion
  19.2 13.2 %relay.1 = (bf16[4,720,720]{2,1,0:T(8,128)(2,1)}, bf16[4,720,720]{2,1,0:T(8,128)(2,1)}, bf16[4,720,720]{2,1,0:T(8,128)(2,1)}) custom-call(f32[8,128]{1,0:T(8,128)} %get-tuple-element.32.seen_ref, bf16[720,2880]{1,0:T(8,128)(2,1)} %bitcast.27, bf16[720,2880]{1,0:T(8,128)(2,1)} %bitcast.28, bf16[720,2880]{1,0:T(8,128)(2,1)} %bitcast.29), custom_call_target="tpu_custom_call" | custom-call | flops 4777574400 | bytes 24883200 | tf_op jit(solution)/shard_map/relay/pallas_call | solution.py:290
  32.4 15.6 %all-to-all-done = bf16[128,8,1152]{2,1,0:T(8,128)(2,1)S(1)} async-done(((bf16[128,8,1152]{2,1,0:T(8,128)(2,1)}), bf16[128,8,1152]{2,1,0:T(8,128)(2,1)S(1)}, u32[]{:S(2)}, u32[]{:S(2)}) %all-to-all-start) | async-done | bytes 2359328 | tf_op jit(solution)/shard_map/all_to_all | solution.py:274
  48.0 2.2 %shard_map.83 = (f32[8,1024]{1,0:T(8,128)S(1)}, f32[1024,8]{1,0:T(8,128)S(1)}, bf16[720,384]{1,0:T(8,128)(2,1)S(1)}) custom-call(bf16[1024,1152]{1,0:T(8,128)(2,1)S(1)} %bitcast.21, s32[1]{0:T(128)S(6)} %add.27.refs_1_), custom_call_target="tpu_custom_call" | custom-call | flops 1132462080 | bytes 1474560 | tf_op jit(solution)/shard_map/pallas_call | solution.py:305
  50.2 0.0 copy-start.2
  50.2 0.0 slice-start.2
  50.2 2.5 %shard_map.87.refs_3_ = bf16[720,384]{1,0:T(8,128)(2,1)} custom-call(bf16[1024,1152]{1,0:T(8,128)(2,1)S(1)} %bitcast.22, f32[8,1024]{1,0:T(8,128)S(1)} %get-tuple-element.49.refs_1_), custom_call_target="tpu_custom_call" | custom-call | flops 1132462080 | bytes 1474560 | tf_op jit(solution)/shard_map/pallas_call | solution.py:311
  52.7 0.0 copy-done.2
  52.7 1.1 collective-permute-start.6
  53.8 0.9 collective-permute-start
  54.7 0.5 collective-permute-start.7
  55.3 11.5 %collective-permute-done.6.refs_4_ = bf16[720,384]{1,0:T(8,128)(2,1)} collective-permute-done((bf16[720,384]{1,0:T(8,128)(2,1)}, bf16[720,384]{1,0:T(8,128)(2,1)}, u32[]{:S(2)}, u32[]{:S(2)}) %collective-permute-start.6) | collective-permute-done | bytes 552992 | tf_op jit(solution)/shard_map/ppermute | solution.py:268
  66.7 2.4 %collective-permute-start.8 = (bf16[720,384]{1,0:T(8,128)(2,1)}, bf16[720,384]{1,0:T(8,128)(2,1)S(1)}, u32[]{:S(2)}, u32[]{:S(2)}) collective-permute-start(bf16[720,384]{1,0:T(8,128)(2,1)} %collective-permute-done.6.refs_4_), channel_id=1, source_target_pairs={{0,96},{32,0},{64,32},{96,64},{1,97},{33,1},{65,33},{97,65},{2,98}... | collective-permute-start | bytes 1658888 | tf_op jit(solution)/shard_map/ppermute | solution.py:268
  69.2 0.0 collective-permute-start.1
  69.2 1.3 collective-permute-done.refs_4_
  70.4 0.8 collective-permute-start.2
  71.2 0.0 copy-start
  71.2 2.3 %copy-done = bf16[4,720,720]{2,1,0:T(8,128)(2,1)S(1)} copy-done((bf16[4,720,720]{2,1,0:T(8,128)(2,1)S(1)}, bf16[4,720,720]{2,1,0:T(8,128)(2,1)}, u32[]{:S(2)}) %copy-start) | copy-done | bytes 4147224
  73.5 0.0 copy-start.1
  73.5 2.3 %copy-done.1 = bf16[4,720,720]{2,1,0:T(8,128)(2,1)S(1)} copy-done((bf16[4,720,720]{2,1,0:T(8,128)(2,1)S(1)}, bf16[4,720,720]{2,1,0:T(8,128)(2,1)}, u32[]{:S(2)}) %copy-start.1) | copy-done | bytes 4147224
  75.7 0.0 slice-start.3
  75.7 3.8 %shard_map.88 = (f32[720,384]{1,0:T(8,128)S(1)}, f32[720,384]{1,0:T(8,128)S(1)}) custom-call(s32[1]{0:T(128)} %bitcast.9.refs_0_.at_ref, bf16[4,720,720]{2,1,0:T(8,128)(2,1)S(1)} %copy-done, bf16[4,720,720]{2,1,0:T(8,128)(2,1)S(1)} %copy-done.1, bf16[720,384]{1,0:T(8,128)(2,1)} %shard_map.87.refs_3_, bf16[720,384]{1,0:T(8,128)(2,1)} %collective-permute-done.6.refs_4_), custom_call_target="tpu_custom_call" | custom-call | flops 1592524800 | bytes 4147200 | tf_op jit(solution)/shard_map/pallas_call | solution.py:319
  79.5 2.8 %collective-permute-done.7.refs_6_ = bf16[720,384]{1,0:T(8,128)(2,1)S(1)} collective-permute-done((bf16[720,384]{1,0:T(8,128)(2,1)}, bf16[720,384]{1,0:T(8,128)(2,1)S(1)}, u32[]{:S(2)}, u32[]{:S(2)}) %collective-permute-start.7) | collective-permute-done | bytes 552992 | tf_op jit(solution)/shard_map/ppermute | solution.py:268
  82.3 0.1 collective-permute-done.8.refs_7_
  82.4 0.0 slice-done.2
  82.4 0.0 slice-done.3
  82.4 3.2 %shard_map.89 = (bf16[720,384]{1,0:T(8,128)(2,1)S(1)}, bf16[720,384]{1,0:T(8,128)(2,1)S(1)}) custom-call(s32[1]{0:T(128)} %bitcast.9.refs_0_.at_ref, bf16[4,720,720]{2,1,0:T(8,128)(2,1)S(1)} %copy-done, bf16[4,720,720]{2,1,0:T(8,128)(2,1)S(1)} %copy-done.1, bf16[4,720,720]{2,1,0:T(8,128)(2,1)S(1)} %bitcast.18, f32[720,384]{1,0:T(8,128)S(1)} %get-tuple-element.50.refs_4_, ...), custom_call_target="tpu_custom_call" | custom-call | flops 1990656000 | bytes 5184000 | tf_op jit(solution)/shard_map/pallas_call | solution.py:328
  85.6 3.7 %collective-permute-start.10 = (bf16[720,384]{1,0:T(8,128)(2,1)S(1)}, bf16[720,384]{1,0:T(8,128)(2,1)S(1)}, u32[]{:S(2)}, u32[]{:S(2)}) collective-permute-start(bf16[720,384]{1,0:T(8,128)(2,1)S(1)} %get-tuple-element.56), channel_id=1, source_target_pairs={{0,96},{32,0},{64,32},{96,64},{1,97},{33,1},{65,33},{97,65},{2,98}... | collective-permute-start | bytes 1658888 | tf_op jit(solution)/shard_map/ppermute | solution.py:268
  89.3 4.9 %collective-permute-done.1.refs_5_ = bf16[720,384]{1,0:T(8,128)(2,1)S(1)} collective-permute-done((bf16[720,384]{1,0:T(8,128)(2,1)S(1)}, bf16[720,384]{1,0:T(8,128)(2,1)S(1)}, u32[]{:S(2)}, u32[]{:S(2)}) %collective-permute-start.1) | collective-permute-done | bytes 552992 | tf_op jit(solution)/shard_map/ppermute | solution.py:268
  94.2 0.0 slice-done
  94.2 0.0 slice-done.1
  94.2 3.6 %shard_map.84 = (f32[720,384]{1,0:T(8,128)S(1)}, f32[720,384]{1,0:T(8,128)S(1)}) custom-call(s32[1]{0:T(128)} %bitcast.9.refs_0_.at_ref, bf16[4,720,720]{2,1,0:T(8,128)(2,1)S(1)} %bitcast.16, bf16[4,720,720]{2,1,0:T(8,128)(2,1)S(1)} %copy-done.1, bf16[720,384]{1,0:T(8,128)(2,1)S(1)} %get-tuple-element.41.refs_3_, ...), custom_call_target="tpu_custom_call" | custom-call | flops 2388787200 | bytes 6220800 | tf_op jit(solution)/shard_map/pallas_call | solution.py:319
  97.8 0.0 collective-permute-done.2.refs_6_
  97.9 1.9 %shard_map.85 = (bf16[720,384]{1,0:T(8,128)(2,1)S(1)}, bf16[720,384]{1,0:T(8,128)(2,1)S(1)}) custom-call(s32[1]{0:T(128)} %bitcast.9.refs_0_.at_ref, bf16[4,720,720]{2,1,0:T(8,128)(2,1)S(1)} %bitcast.16, bf16[4,720,720]{2,1,0:T(8,128)(2,1)S(1)} %copy-done.1, bf16[4,720,720]{2,1,0:T(8,128)(2,1)S(1)} %bitcast.18, f32[720,384]{1,0:T(8,128)S(1)} %get-tuple-element.42.refs_4_, ...), custom_call_target="tpu_custom_call" | custom-call | flops 1194393600 | bytes 3110400 | tf_op jit(solution)/shard_map/pallas_call | solution.py:328
  99.8 0.6 collective-permute-start.3
  100.4 1.9 %shard_map.90 = (f32[720,384]{1,0:T(8,128)S(1)}, f32[720,384]{1,0:T(8,128)S(1)}, bf16[720,384]{1,0:T(8,128)(2,1)S(1)}) custom-call(s32[1]{0:T(128)} %bitcast.9.refs_0_.at_ref, bf16[720,384]{1,0:T(8,128)(2,1)S(1)} %get-tuple-element.52.h_ref, bf16[4,720,720]{2,1,0:T(8,128)(2,1)S(1)} %bitcast.18), custom_call_target="tpu_custom_call" | custom-call | flops 1194393600 | bytes 3110400 | tf_op jit(solution)/shard_map/pallas_call | solution.py:336
  102.3 1.3 collective-permute-start.9
  103.7 1.9 %shard_map.86 = (f32[720,384]{1,0:T(8,128)S(1)}, bf16[720,384]{1,0:T(8,128)(2,1)S(1)}, f32[720,384]{1,0:T(8,128)S(1)}) custom-call(s32[1]{0:T(128)} %bitcast.9.refs_0_.at_ref, bf16[720,384]{1,0:T(8,128)(2,1)S(1)} %get-tuple-element.44.h_ref, bf16[4,720,720]{2,1,0:T(8,128)(2,1)S(1)} %bitcast.18), custom_call_target="tpu_custom_call" | custom-call | flops 1194393600 | bytes 3110400 | tf_op jit(solution)/shard_map/pallas_call | solution.py:336
  105.6 2.0 %collective-permute-start.5 = (bf16[720,384]{1,0:T(8,128)(2,1)S(1)}, bf16[720,384]{1,0:T(8,128)(2,1)S(1)}, u32[]{:S(2)}, u32[]{:S(2)}) collective-permute-start(bf16[720,384]{1,0:T(8,128)(2,1)S(1)} %get-tuple-element.48), channel_id=1, source_target_pairs={{0,96},{32,0},{64,32},{96,64},{1,97},{33,1},{65,33},{97,65},{2,98}... | collective-permute-start | bytes 1658888 | tf_op jit(solution)/shard_map/ppermute | solution.py:268
  107.6 0.0 collective-permute-done.10
  107.6 0.1 add_convert_fusion
  107.7 2.2 %collective-permute-start.11 = (bf16[720,384]{1,0:T(8,128)(2,1)S(1)}, bf16[720,384]{1,0:T(8,128)(2,1)S(1)}, u32[]{:S(2)}, u32[]{:S(2)}) collective-permute-start(bf16[720,384]{1,0:T(8,128)(2,1)S(1)} %add_convert_fusion), channel_id=1, source_target_pairs={{0,96},{32,0},{64,32},{96,64},{1,97},{33,1},{65,33},{97,65},{2,98}... | collective-permute-start | bytes 1658888 | tf_op jit(solution)/shard_map/ppermute | solution.py:268
  109.9 7.0 %collective-permute-done.3 = bf16[720,384]{1,0:T(8,128)(2,1)S(1)} collective-permute-done((bf16[720,384]{1,0:T(8,128)(2,1)S(1)}, bf16[720,384]{1,0:T(8,128)(2,1)S(1)}, u32[]{:S(2)}, u32[]{:S(2)}) %collective-permute-start.3) | collective-permute-done | bytes 552992 | tf_op jit(solution)/shard_map/ppermute | solution.py:268
  116.9 0.1 add_convert_fusion.1
  117.1 0.1 collective-permute-start.4
  117.1 11.7 %collective-permute-done.9.refs_5_ = bf16[720,384]{1,0:T(8,128)(2,1)S(1)} collective-permute-done((bf16[720,384]{1,0:T(8,128)(2,1)S(1)}, bf16[720,384]{1,0:T(8,128)(2,1)S(1)}, u32[]{:S(2)}, u32[]{:S(2)}) %collective-permute-start.9) | collective-permute-done | bytes 552992 | tf_op jit(solution)/shard_map/ppermute | solution.py:268
  128.8 0.0 collective-permute-done.5.refs_3_
  128.8 0.0 collective-permute-done.11.refs_6_
  128.8 6.4 %collective-permute-done.4.refs_2_ = bf16[720,384]{1,0:T(8,128)(2,1)S(1)} collective-permute-done((bf16[720,384]{1,0:T(8,128)(2,1)S(1)}, bf16[720,384]{1,0:T(8,128)(2,1)S(1)}, u32[]{:S(2)}, u32[]{:S(2)}) %collective-permute-start.4) | collective-permute-done | bytes 552992 | tf_op jit(solution)/shard_map/ppermute | solution.py:268
  135.2 0.0 copy-done.3
  135.2 3.2 %shard_map.91 = bf16[1024,1152]{1,0:T(8,128)(2,1)S(1)} custom-call(f32[1024,8]{1,0:T(8,128)S(1)} %copy-done.3, f32[720,384]{1,0:T(8,128)S(1)} %get-tuple-element.45.refs_1_, bf16[720,384]{1,0:T(8,128)(2,1)S(1)} %collective-permute-done.4.refs_2_, bf16[720,384]{1,0:T(8,128)(2,1)S(1)} %collective-permute-done.5.refs_3_, ...), custom_call_target="tpu_custom_call" | custom-call | flops 1132462080 | bytes 1474560 | tf_op jit(solution)/shard_map/pallas_call | solution.py:365
  138.4 0.0 copy-start.4
  138.4 0.0 copy-start.5
  138.4 41.3 %all_to_all.10 = bf16[128,8,1152]{2,1,0:T(8,128)(2,1)S(1)} all-to-all(bf16[128,8,1152]{2,1,0:T(8,128)(2,1)S(1)} %bitcast.19), channel_id=1, replica_groups=mesh['attn'=4,'expert_0'=4,'expert_1'=4,'expert_2'=2] {'attn','expert_0'..., dimensions={0} | all-to-all | bytes 4718592 | tf_op jit(solution)/shard_map/all_to_all | solution.py:274
  179.7 0.0 copy-done.4
  179.7 0.0 copy-done.5
  179.7 1.9 %shard_map.92 = bf16[32,2880]{1,0:T(8,128)(2,1)} custom-call(bf16[1024,1152]{1,0:T(8,128)(2,1)S(1)} %bitcast.20, s32[4,32]{1,0:T(4,128)S(1)} %bitcast.24, f32[4,32]{1,0:T(4,128)S(1)} %bitcast.25), custom_call_target="tpu_custom_call" | custom-call | flops 141557760 | bytes 1474560 | tf_op jit(solution)/shard_map/pallas_call | solution.py:368
  (5 shorter events, 0.0 us)
Async XLA Ops:
  3.6 11.2 %copy-start.7 = (s32[32]{0:T(128)S(1)}, s32[32]{0:T(128)}, u32[]{:S(2)}) copy-start(s32[32]{0:T(128)} %param.12) | copy-start | bytes 388
  3.6 13.7 %copy-start.6 = (s32[32]{0:T(128)S(1)}, s32[32]{0:T(128)}, u32[]{:S(2)}) copy-start(s32[32]{0:T(128)} %param.11) | copy-start | bytes 388
  3.6 44.4 %all-to-all-start = ((bf16[128,8,1152]{2,1,0:T(8,128)(2,1)}), bf16[128,8,1152]{2,1,0:T(8,128)(2,1)S(1)}, u32[]{:S(2)}, u32[]{:S(2)}) async-start(bf16[128,8,1152]{2,1,0:T(8,128)(2,1)} %bitcast.26), calls=%async_computation | async-start | bytes 4718592 | tf_op jit(solution)/shard_map/all_to_all | solution.py:274
  50.2 2.5 %copy-start.2 = (f32[1024,8]{1,0:T(8,128)}, f32[1024,8]{1,0:T(8,128)S(1)}, u32[]{:S(2)}) copy-start(f32[1024,8]{1,0:T(8,128)S(1)} %get-tuple-element.37.refs_0_) | copy-start | bytes 98308
  50.2 32.2 %slice-start.2 = ((s8[4423680]{0:T(1024)(128)(4,1)}), s8[229376]{0:T(1024)(128)(4,1)S(1)}, s32[]{:S(2)}) async-start(s8[4423680]{0:T(1024)(128)(4,1)} %bitcast.17), calls=%async_computation.4 | async-start | bytes 458752
  52.7 14.0 %collective-permute-start.6 = (bf16[720,384]{1,0:T(8,128)(2,1)}, bf16[720,384]{1,0:T(8,128)(2,1)}, u32[]{:S(2)}, u32[]{:S(2)}) collective-permute-start(bf16[720,384]{1,0:T(8,128)(2,1)} %shard_map.87.refs_3_), channel_id=1, source_target_pairs={{0,96},{32,0},{64,32},{96,64},{1,97},{33,1},{65,33},{97,65},{2,98}... | collective-permute-start | bytes 1658888 | tf_op jit(solution)/shard_map/ppermute | solution.py:268
  53.8 16.6 %collective-permute-start = (bf16[720,384]{1,0:T(8,128)(2,1)S(1)}, bf16[720,384]{1,0:T(8,128)(2,1)S(1)}, u32[]{:S(2)}, u32[]{:S(2)}) collective-permute-start(bf16[720,384]{1,0:T(8,128)(2,1)S(1)} %get-tuple-element.41.refs_3_), channel_id=1, source_target_pairs={{0,32},{32,64},{64,96},{96,0},{1,33},{33,65},{65,97},{97,1},{2,34}... | collective-permute-start | bytes 1658888 | tf_op jit(solution)/shard_map/ppermute | solution.py:268
  54.7 27.6 %collective-permute-start.7 = (bf16[720,384]{1,0:T(8,128)(2,1)}, bf16[720,384]{1,0:T(8,128)(2,1)S(1)}, u32[]{:S(2)}, u32[]{:S(2)}) collective-permute-start(bf16[720,384]{1,0:T(8,128)(2,1)} %shard_map.87.refs_3_), channel_id=1, source_target_pairs={{0,32},{32,64},{64,96},{96,0},{1,33},{33,65},{65,97},{97,1},{2,34}... | collective-permute-start | bytes 1658888 | tf_op jit(solution)/shard_map/ppermute | solution.py:268
  66.7 15.7 %collective-permute-start.8 = (bf16[720,384]{1,0:T(8,128)(2,1)}, bf16[720,384]{1,0:T(8,128)(2,1)S(1)}, u32[]{:S(2)}, u32[]{:S(2)}) collective-permute-start(bf16[720,384]{1,0:T(8,128)(2,1)} %collective-permute-done.6.refs_4_), channel_id=1, source_target_pairs={{0,96},{32,0},{64,32},{96,64},{1,97},{33,1},{65,33},{97,65},{2,98}... | collective-permute-start | bytes 1658888 | tf_op jit(solution)/shard_map/ppermute | solution.py:268
  69.2 25.0 %collective-permute-start.1 = (bf16[720,384]{1,0:T(8,128)(2,1)S(1)}, bf16[720,384]{1,0:T(8,128)(2,1)S(1)}, u32[]{:S(2)}, u32[]{:S(2)}) collective-permute-start(bf16[720,384]{1,0:T(8,128)(2,1)S(1)} %get-tuple-element.41.refs_3_), channel_id=1, source_target_pairs={{0,96},{32,0},{64,32},{96,64},{1,97},{33,1},{65,33},{97,65},{2,98}... | collective-permute-start | bytes 1658888 | tf_op jit(solution)/shard_map/ppermute | solution.py:268
  70.4 27.4 %collective-permute-start.2 = (bf16[720,384]{1,0:T(8,128)(2,1)S(1)}, bf16[720,384]{1,0:T(8,128)(2,1)S(1)}, u32[]{:S(2)}, u32[]{:S(2)}) collective-permute-start(bf16[720,384]{1,0:T(8,128)(2,1)S(1)} %collective-permute-done.refs_4_), channel_id=1, source_target_pairs={{0,32},{32,64},{64,96},{96,0},{1,33},{33,65},{65,97},{97,1},{2,34}... | collective-permute-start | bytes 1658888 | tf_op jit(solution)/shard_map/ppermute | solution.py:268
  71.2 2.3 %copy-start = (bf16[4,720,720]{2,1,0:T(8,128)(2,1)S(1)}, bf16[4,720,720]{2,1,0:T(8,128)(2,1)}, u32[]{:S(2)}) copy-start(bf16[4,720,720]{2,1,0:T(8,128)(2,1)} %get-tuple-element.38.refs_1_) | copy-start | bytes 12441604
  73.5 2.3 %copy-start.1 = (bf16[4,720,720]{2,1,0:T(8,128)(2,1)S(1)}, bf16[4,720,720]{2,1,0:T(8,128)(2,1)}, u32[]{:S(2)}) copy-start(bf16[4,720,720]{2,1,0:T(8,128)(2,1)} %get-tuple-element.39.refs_2_) | copy-start | bytes 12441604
  75.7 6.7 %slice-start.3 = ((s8[4423680]{0:T(1024)(128)(4,1)}), s8[4194304]{0:T(1024)(128)(4,1)S(1)}, s32[]{:S(2)}) async-start(s8[4423680]{0:T(1024)(128)(4,1)} %bitcast.17), calls=%async_computation.5 | async-start | bytes 8388608
  82.4 11.8 %slice-start = ((s8[4423680]{0:T(1024)(128)(4,1)}), s8[4194304]{0:T(1024)(128)(4,1)S(1)}, s32[]{:S(2)}) async-start(s8[4423680]{0:T(1024)(128)(4,1)} %bitcast.15), calls=%async_computation.2 | async-start | bytes 8388608
  82.4 11.8 %slice-start.1 = ((s8[4423680]{0:T(1024)(128)(4,1)}), s8[229376]{0:T(1024)(128)(4,1)S(1)}, s32[]{:S(2)}) async-start(s8[4423680]{0:T(1024)(128)(4,1)} %bitcast.15), calls=%async_computation.3 | async-start | bytes 458752
  85.6 22.0 %collective-permute-start.10 = (bf16[720,384]{1,0:T(8,128)(2,1)S(1)}, bf16[720,384]{1,0:T(8,128)(2,1)S(1)}, u32[]{:S(2)}, u32[]{:S(2)}) collective-permute-start(bf16[720,384]{1,0:T(8,128)(2,1)S(1)} %get-tuple-element.56), channel_id=1, source_target_pairs={{0,96},{32,0},{64,32},{96,64},{1,97},{33,1},{65,33},{97,65},{2,98}... | collective-permute-start | bytes 1658888 | tf_op jit(solution)/shard_map/ppermute | solution.py:268
  99.8 17.1 %collective-permute-start.3 = (bf16[720,384]{1,0:T(8,128)(2,1)S(1)}, bf16[720,384]{1,0:T(8,128)(2,1)S(1)}, u32[]{:S(2)}, u32[]{:S(2)}) collective-permute-start(bf16[720,384]{1,0:T(8,128)(2,1)S(1)} %get-tuple-element.47), channel_id=1, source_target_pairs={{0,32},{32,64},{64,96},{96,0},{1,33},{33,65},{65,97},{97,1},{2,34}... | collective-permute-start | bytes 1658888 | tf_op jit(solution)/shard_map/ppermute | solution.py:268
  102.3 26.5 %collective-permute-start.9 = (bf16[720,384]{1,0:T(8,128)(2,1)S(1)}, bf16[720,384]{1,0:T(8,128)(2,1)S(1)}, u32[]{:S(2)}, u32[]{:S(2)}) collective-permute-start(bf16[720,384]{1,0:T(8,128)(2,1)S(1)} %get-tuple-element.54), channel_id=1, source_target_pairs={{0,32},{32,64},{64,96},{96,0},{1,33},{33,65},{65,97},{97,1},{2,34}... | collective-permute-start | bytes 1658888 | tf_op jit(solution)/shard_map/ppermute | solution.py:268
  105.6 23.2 %collective-permute-start.5 = (bf16[720,384]{1,0:T(8,128)(2,1)S(1)}, bf16[720,384]{1,0:T(8,128)(2,1)S(1)}, u32[]{:S(2)}, u32[]{:S(2)}) collective-permute-start(bf16[720,384]{1,0:T(8,128)(2,1)S(1)} %get-tuple-element.48), channel_id=1, source_target_pairs={{0,96},{32,0},{64,32},{96,64},{1,97},{33,1},{65,33},{97,65},{2,98}... | collective-permute-start | bytes 1658888 | tf_op jit(solution)/shard_map/ppermute | solution.py:268
  107.7 21.1 %collective-permute-start.11 = (bf16[720,384]{1,0:T(8,128)(2,1)S(1)}, bf16[720,384]{1,0:T(8,128)(2,1)S(1)}, u32[]{:S(2)}, u32[]{:S(2)}) collective-permute-start(bf16[720,384]{1,0:T(8,128)(2,1)S(1)} %add_convert_fusion), channel_id=1, source_target_pairs={{0,96},{32,0},{64,32},{96,64},{1,97},{33,1},{65,33},{97,65},{2,98}... | collective-permute-start | bytes 1658888 | tf_op jit(solution)/shard_map/ppermute | solution.py:268
  116.9 18.2 %copy-start.3 = (f32[1024,8]{1,0:T(8,128)S(1)}, f32[1024,8]{1,0:T(8,128)}, u32[]{:S(2)}) copy-start(f32[1024,8]{1,0:T(8,128)} %copy-done.2) | copy-start | bytes 98308
  117.1 18.1 %collective-permute-start.4 = (bf16[720,384]{1,0:T(8,128)(2,1)S(1)}, bf16[720,384]{1,0:T(8,128)(2,1)S(1)}, u32[]{:S(2)}, u32[]{:S(2)}) collective-permute-start(bf16[720,384]{1,0:T(8,128)(2,1)S(1)} %add_convert_fusion.1), channel_id=1, source_target_pairs={{0,32},{32,64},{64,96},{96,0},{1,33},{33,65},{65,97},{97,1},{2,34}... | collective-permute-start | bytes 1658888 | tf_op jit(solution)/shard_map/ppermute | solution.py:268
  138.4 41.3 %copy-start.4 = (s32[32,4]{0,1:T(4,128)S(1)}, s32[32,4]{0,1:T(4,128)}, u32[]{:S(2)}) copy-start(s32[32,4]{0,1:T(4,128)} %param.9) | copy-start | bytes 1540
  138.4 41.3 %copy-start.5 = (f32[32,4]{0,1:T(4,128)S(1)}, f32[32,4]{0,1:T(4,128)}, u32[]{:S(2)}) copy-start(f32[32,4]{0,1:T(4,128)} %param.10) | copy-start | bytes 1540

commit v3 on v2

--- a/solution.py
+++ b/solution.py
@@ -27,37 +27,43 @@
     return jnp.where(places == at, 1.0, 0.0)
 
 
-def send_kernel(lay, x_ref, id_ref, s_ref, seen_ref):
+def send_kernel(lay, blocks, x_ref, id_ref, s_ref, seen_ref, hot_ref, flag_ref):
     tok, experts, seats = x_ref.shape[0], lay.experts, lay.seats
-    seen_ref[...] = jnp.zeros_like(seen_ref)
-    ids = id_ref[...].astype(F32)
-    expert = iota((experts, tok), 0).astype(F32)
-    hits = jnp.zeros((experts, tok), F32)
-    for k in range(ids.shape[0]):
-        hits += jnp.where(ids[k : k + 1] == expert, 1.0, 0.0)
-    earlier = (iota((tok, tok), 0) < iota((tok, tok), 1)).astype(BF)
-    order = dot(hits.astype(BF), earlier)
-    order = jnp.where(hits > 0.5, order, -1.0).astype(BF)
-    rows = experts * seats
-    spread = (iota((rows, experts), 0) // seats == iota((rows, experts), 1)).astype(BF)
-    order = dot(spread, order)
-    seat = iota((rows, tok), 0) % seats
-    over = (seats + seat // 2).astype(F32)
-    full = jnp.where(order == seat.astype(F32), 1.0, 0.0).astype(BF)
-    part = jnp.where(order == over, 1.0, 0.0)
-    even = jnp.where(seat % 2 == 0, part, 0.0).astype(BF)
-    odd = jnp.where(seat % 2 == 1, part, 0.0).astype(BF)
     one, none = jnp.ones((tok, 1), BF), lambda n: jnp.zeros((tok, n), BF)
-    second = jnp.concatenate([none(lay.width + 1), one, none(lay.low - lay.width - 2)], axis=1)
-    flags = dot(part.astype(BF), second)
-    for b in range(x_ref.shape[1] // lay.width):
-        first = b * lay.width
-        x = x_ref[:, first : first + lay.width]
-        at = slice(b * rows, (b + 1) * rows)
-        wide = jnp.concatenate([x, one, none(lay.low - lay.width - 1)], axis=1)
-        s_ref[at, : lay.low] = (dot(full, wide) + flags).astype(BF)
-        tail = jnp.concatenate([x[:, lay.point :], none(lay.short)], axis=1)
-        s_ref[at, lay.low :] = (dot(even, x[:, : lay.point]) + dot(odd, tail)).astype(BF)
+
+    @pl.when(pl.program_id(0) == 0)
+    def _():
+        seen_ref[...] = jnp.zeros_like(seen_ref)
+        ids = id_ref[...].astype(F32)
+        expert = iota((experts, tok), 0).astype(F32)
+        hits = jnp.zeros((experts, tok), F32)
+        for k in range(ids.shape[0]):
+            hits += jnp.where(ids[k : k + 1] == expert, 1.0, 0.0)
+        earlier = (iota((tok, tok), 0) < iota((tok, tok), 1)).astype(BF)
+        order = dot(hits.astype(BF), earlier)
+        order = jnp.where(hits > 0.5, order, -1.0).astype(BF)
+        rows = experts * seats
+        spread = (iota((rows, experts), 0) // seats == iota((rows, experts), 1)).astype(BF)
+        order = dot(spread, order)
+        seat = iota((rows, tok), 0) % seats
+        over = (seats + seat // 2).astype(F32)
+        part = jnp.where(order == over, 1.0, 0.0)
+        hot_ref[0] = jnp.where(order == seat.astype(F32), 1.0, 0.0).astype(BF)
+        hot_ref[1] = jnp.where(seat % 2 == 0, part, 0.0).astype(BF)
+        hot_ref[2] = jnp.where(seat % 2 == 1, part, 0.0).astype(BF)
+        second = jnp.concatenate([none(lay.width + 1), one, none(lay.low - lay.width - 2)], axis=1)
+        flag_ref[...] = dot(part.astype(BF), second)
+
+    for b in range(blocks):
+
+        @pl.when(pl.program_id(0) == b)
+        def _(b=b):
+            x = x_ref[:, b * lay.width : (b + 1) * lay.width]
+            wide = jnp.concatenate([x, one, none(lay.low - lay.width - 1)], axis=1)
+            s_ref[:, : lay.low] = (dot(hot_ref[0], wide) + flag_ref[...]).astype(BF)
+            tail = jnp.concatenate([x[:, lay.point :], none(lay.short)], axis=1)
+            rest = dot(hot_ref[1], x[:, : lay.point]) + dot(hot_ref[2], tail)
+            s_ref[:, lay.low :] = rest.astype(BF)
 
 
 def gather_slots(lay, rows, x_ref, first, out):
@@ -75,7 +81,7 @@
     gather_slots(lay, [row_ref[k : k + 1] for k in range(3)], x_ref, first, out)
 
 
-def pick_kernel(lay, x_ref, par_ref, row_ref, col_ref, out):
+def pick_kernel(lay, x_ref, par_ref, row_ref, out):
     came, seats = x_ref.shape[0], lay.seats
     sources = came // seats
     bound = par_ref[0].astype(F32)
@@ -99,9 +105,7 @@
     over = jnp.where(jnp.logical_and(part > 0.5, over < bound), over, -1.0)
     evens, odds = jnp.where(even, over, -1.0), jnp.where(even, -1.0, over)
     nothing = jnp.full((5, came), -1.0, F32)
-    every = jnp.concatenate([rank, evens, odds, nothing], axis=0)
-    row_ref[...] = every
-    col_ref[...] = every.T
+    row_ref[...] = jnp.concatenate([rank, evens, odds, nothing], axis=0)
     gather_slots(lay, (rank, evens, odds), x_ref, 0, out)
 
 
@@ -147,25 +151,30 @@
         out[...] = dot(wd_ref[block], hidden).astype(out.dtype)
 
 
-def place_kernel(lay, slot_ref, *refs):
+def spots_kernel(row_ref, *outs):
+    places = row_ref[...].T
+    for k, out in enumerate(outs):
+        out[...] = hot(places[:, k : k + 1], out.shape[1]).astype(BF)
+
+
+def place_kernel(lay, whole_ref, even_ref, odd_ref, *refs):
     ins, z_ref = refs[:-1], refs[-1]
     columns = []
     for own, left, right in (ins[:3], ins[3:]):
         total = own[...] + left[...].astype(F32) + right[...].astype(F32)
         columns.append(total.astype(BF))
     y = jnp.concatenate(columns, axis=1)
-    slots, came = y.shape[1], z_ref.shape[0]
-    at = lambda k: hot(slot_ref[:, k : k + 1], slots).astype(BF)
+    came = z_ref.shape[0]
     none = lambda n: jnp.zeros((came, n), BF)
-    rows = dot(at(0), y, ((1,), (1,))).astype(BF)
+    rows = dot(whole_ref[...], y, ((1,), (1,))).astype(BF)
     z_ref[:, : lay.low] = jnp.concatenate([rows, none(lay.low - lay.width)], axis=1)
-    left = dot(at(1), y[: lay.point], ((1,), (1,))).astype(BF)
-    right = dot(at(2), y[lay.point :], ((1,), (1,))).astype(BF)
+    left = dot(even_ref[...], y[: lay.point], ((1,), (1,))).astype(BF)
+    right = dot(odd_ref[...], y[lay.point :], ((1,), (1,))).astype(BF)
     z_ref[:, lay.low :] = left + jnp.concatenate([right, none(lay.short)], axis=1)
 
 
-def mix_kernel(lay, b_ref, id_ref, p_ref, o_ref):
-    tok, seats = o_ref.shape[0], lay.seats
+def router_kernel(lay, id_ref, p_ref, w_ref):
+    tok, seats = id_ref.shape[1], lay.seats
     ids, prob = id_ref[...].astype(F32).T, p_ref[...].T
     top = ids.shape[1]
     lane = iota((tok, lay.experts), 1).astype(F32)
@@ -185,16 +194,19 @@
         odd = jnp.where(seat < seats, -1.0, over + 1.0)
         for n, place in enumerate((full, over, odd)):
             kinds[n] += hot(place, rows) * prob[:, k : k + 1]
-    weights = []
-    for kind in kinds:
+    for n, kind in enumerate(kinds):
         high = kind.astype(BF)
         rest = kind - high.astype(F32)
         middle = rest.astype(BF)
         low = (rest - middle.astype(F32)).astype(BF)
-        weights.append(jnp.concatenate([high, middle, low], axis=0))
+        w_ref[n] = jnp.concatenate([high, middle, low], axis=0)
+
+
+def mix_kernel(lay, b_ref, w_ref, o_ref):
+    tok, rows = o_ref.shape[0], w_ref.shape[2]
 
     def weighted(n, block):
-        three = dot(weights[n], block)
+        three = dot(w_ref[n], block)
         return three[:tok] + three[tok : 2 * tok] + three[2 * tok :]
 
     for b in range(o_ref.shape[1] // lay.width):
@@ -275,12 +287,26 @@
         return moved.reshape(came, lay.lanes)
 
     packed = shape((came, lay.lanes), BF)
-    outgoing, seen = run(
-        lambda *refs: send_kernel(lay, *refs),
-        [VMEM] * 2,
-        (packed, shape((8, 128), F32)),
-        (2 * tok * came * width, 2 * came * width),
-        mebibytes=60,
+    block_rows = experts * lay.seats
+    outgoing, seen = pl.pallas_call(
+        lambda *refs: send_kernel(lay, groups, *refs),
+        grid=(groups,),
+        out_shape=(packed, shape((8, 128), F32)),
+        in_specs=[
+            pl.BlockSpec((tok, model), lambda i: (0, 0)),
+            pl.BlockSpec((top, tok), lambda i: (0, 0)),
+        ],
+        out_specs=(
+            pl.BlockSpec((block_rows, lay.lanes), lambda i: (i, 0)),
+            pl.BlockSpec((8, 128), lambda i: (0, 0)),
+        ),
+        scratch_shapes=[
+            pltpu.VMEM((3, block_rows, tok), BF),
+            pltpu.VMEM((block_rows, lay.low), F32),
+        ],
+        cost_estimate=cost(2 * tok * came * width, 2 * came * width),
+        compiler_params=grant(60),
+        name="send",
     )(tokens, expert_ids.T)
     arrived = exchange(outgoing)
     relaid = shape((groups, units, width), BF)
@@ -299,18 +325,26 @@
     )(seen, gate_weight[0].T, up_weight[0].T, down_weight[0])
     arrived, wg, wu, wd = lax.optimization_barrier((arrived, wg, wu, wd))
 
+    weights = run(
+        lambda *refs: router_kernel(lay, *refs),
+        [VMEM] * 2,
+        shape((3, 3 * tok, block_rows), BF),
+        (12 * tok * block_rows, 18 * tok * block_rows),
+    )(expert_ids.T, gate_probs.T)
     part = slots // 2
     columns = shape((width, part), BF)
     gather_work = (2 * slots * came * width, 2 * came * width)
-    places, slot, own_a = run(
+    places, own_a = run(
         lambda *refs: pick_kernel(lay, *refs),
         [VMEM, SMEM],
-        (shape((8, came), F32), shape((came, 8), F32), columns),
+        (shape((8, came), F32), columns),
         gather_work,
     )(arrived, par)
     own_b = run(
         lambda *refs: pick_more_kernel(lay, part, *refs), [VMEM] * 2, columns, gather_work
     )(arrived, places)
+    spot = shape((came, slots), BF)
+    spots = run(spots_kernel, [VMEM], (spot,) * 3, (6 * came * slots, 6 * came * slots))(places)
     before, after, across = groups - 1, 1, groups // 2
     area = width * units
     rows = lambda n, kind: shape((n, part), kind)
@@ -363,14 +397,14 @@
     from_right_b = left(added_b)
     sums = (mine_a, from_left_a, from_right_a, mine_b, from_left_b, from_right_b)
     answers = run(
-        lambda *refs: place_kernel(lay, *refs), [VMEM] * 7, packed, gather_work
-    )(slot, *sums)
+        lambda *refs: place_kernel(lay, *refs), [VMEM] * 9, packed, gather_work
+    )(*spots, *sums)
     return run(
         lambda *refs: mix_kernel(lay, *refs),
-        [VMEM] * 3,
+        [VMEM] * 2,
         shape((tok, model), BF),
         (6 * tok * came * width, 2 * came * width),
-    )(exchange(answers), expert_ids.T, gate_probs.T)
+    )(exchange(answers), weights)
 
 
 def solution(mesh):

time: 182 us -> 184 us (1.011)
  blocking collectives: 41.3 us -> 0 us
  waiting for transfers between devices: 61.1 us -> 92.8 us
  starting transfers between devices: 26.9 us -> 35.1 us
    all_to_all x1 -> x0, blocking collectives: 41.3 us -> none  [exchange(): lax.all_to_all(blocks, ATTN_EXPERT, split_axis=0, concat_axis=0, tiled=True)]
    all_to_all x1 -> x2, waiting for transfers between devices: 15.6 us -> 48.2 us  [exchange(): lax.all_to_all(blocks, ATTN_EXPERT, split_axis=0, concat_axis=0, tiled=True)]
    all_to_all x1 -> x2, starting transfers between devices: 11.2 us -> 19.4 us  [exchange(): lax.all_to_all(blocks, ATTN_EXPERT, split_axis=0, concat_axis=0, tiled=True)]
    pallas_call x3 -> x5, Pallas kernels: 8.74 us -> 10.2 us  [the longest x1 4.12 us: on_device(): pl.pallas_call(lambda *refs: send_kernel(lay, groups, *refs), grid=(group...]
    unnamed x24 -> x22, local copies, waits for them, and re-layouts: 4.55 us -> 5.95 us
  transfers between devices with their start and end apart: 13 -> 14, of which waited for: 9 -> 10; matrix products, arithmetic and copies ran while one was open for 1% -> 1% of each run, Pallas kernels for 16% -> 17%
where the time goes in v3:
time: 184 us; the launch traced here: 183 us
  waiting for transfers between devices  92.8 us (50%)
  Pallas kernels  44.4 us (24%)
  starting transfers between devices  35.1 us (19%)
  local copies, waits for them, and re-layouts  7.19 us (4%)
  between operations  3.32 us (2%)
    all_to_all x2, waiting for transfers between devices, exchange(): lax.all_to_all(blocks, ATTN_EXPERT, split_axis=0, concat_axis=0, tiled=True)  48.2 us
    ppermute x12, waiting for transfers between devices, shifted(): return lambda array: lax.ppermute(array, 'attn', pairs)  44.5 us
    all_to_all x2, starting transfers between devices, exchange(): lax.all_to_all(blocks, ATTN_EXPERT, split_axis=0, concat_axis=0, tiled=True)  19.4 us
    ppermute x12, starting transfers between devices, shifted(): return lambda array: lax.ppermute(array, 'attn', pairs)  15.7 us
    pallas_call x1, Pallas kernels, on_device(): pl.pallas_call(relay_kernel, grid=(pl.cdiv(units, step),), out_shape=(rel...  13.3 us
    pallas_call x2, Pallas kernels, mid(): run(lambda *refs: mid_kernel(ahead, *refs), [SMEM] + [VMEM] * (2 + len(bl...  7.45 us
    unnamed x22, local copies, waits for them, and re-layouts  5.95 us
    pallas_call x2, Pallas kernels, far(): run(lambda *refs: far_kernel(ahead, *refs), [SMEM] + [VMEM] * (5 + len(bl...  5.11 us
  transfers between devices with their start and end apart: 14, of which 10 were waited for; matrix products, arithmetic and copies ran while one was open for 1% of the time, Pallas kernels for 17%

profile of v3, /device:TPU:0, one launch (start us, length us, event | category | flops | bytes accessed | tf_op | source)
XLA Modules:
  0.0 183.1 jit_solution(730197121869856951)
XLA Ops:
  0.0 4.1 %send.1 = (bf16[1024,1152]{1,0:T(8,128)(2,1)}, f32[8,128]{1,0:T(8,128)}) custom-call(bf16[32,2880]{1,0:T(8,128)(2,1)} %refs_0_.1, s32[4,32]{1,0:T(4,128)} %bitcast.23), custom_call_target="tpu_custom_call" | custom-call | flops 47185920 | bytes 1474560 | tf_op jit(solution)/shard_map/send/pallas_call | solution.py:291
  4.1 0.0 copy-start.6
  4.1 0.0 copy-start.5
  4.1 11.2 %all-to-all-start = ((bf16[128,8,1152]{2,1,0:T(8,128)(2,1)}), bf16[128,8,1152]{2,1,0:T(8,128)(2,1)S(1)}, u32[]{:S(2)}, u32[]{:S(2)}) async-start(bf16[128,8,1152]{2,1,0:T(8,128)(2,1)} %bitcast.26), calls=%async_computation | async-start | bytes 4718592 | tf_op jit(solution)/shard_map/all_to_all | solution.py:286
  15.3 0.0 copy-done.6
  15.3 0.6 dynamic_slice.9
  17.8 0.0 copy-done.5
  17.9 0.6 fusion
  19.7 13.3 %relay.1 = (bf16[4,720,720]{2,1,0:T(8,128)(2,1)}, bf16[4,720,720]{2,1,0:T(8,128)(2,1)}, bf16[4,720,720]{2,1,0:T(8,128)(2,1)}) custom-call(f32[8,128]{1,0:T(8,128)} %get-tuple-element.34.seen_ref, bf16[720,2880]{1,0:T(8,128)(2,1)} %bitcast.27, bf16[720,2880]{1,0:T(8,128)(2,1)} %bitcast.28, bf16[720,2880]{1,0:T(8,128)(2,1)} %bitcast.29), custom_call_target="tpu_custom_call" | custom-call | flops 4777574400 | bytes 24883200 | tf_op jit(solution)/shard_map/relay/pallas_call | solution.py:316
  33.0 15.6 %all-to-all-done = bf16[128,8,1152]{2,1,0:T(8,128)(2,1)S(1)} async-done(((bf16[128,8,1152]{2,1,0:T(8,128)(2,1)}), bf16[128,8,1152]{2,1,0:T(8,128)(2,1)S(1)}, u32[]{:S(2)}, u32[]{:S(2)}) %all-to-all-start) | async-done | bytes 2359328 | tf_op jit(solution)/shard_map/all_to_all | solution.py:286
  48.5 2.2 %shard_map.82 = (f32[8,1024]{1,0:T(8,128)S(1)}, bf16[720,384]{1,0:T(8,128)(2,1)S(1)}) custom-call(bf16[1024,1152]{1,0:T(8,128)(2,1)S(1)} %bitcast.21, s32[1]{0:T(128)S(6)} %add.27.refs_1_), custom_call_target="tpu_custom_call" | custom-call | flops 1132462080 | bytes 1474560 | tf_op jit(solution)/shard_map/pallas_call | solution.py:337
  50.7 0.0 slice-start.2
  50.7 2.5 %shard_map.87.refs_3_ = bf16[720,384]{1,0:T(8,128)(2,1)} custom-call(bf16[1024,1152]{1,0:T(8,128)(2,1)S(1)} %bitcast.22, f32[8,1024]{1,0:T(8,128)S(1)} %get-tuple-element.39.row_ref.refs_1_), custom_call_target="tpu_custom_call" | custom-call | flops 1132462080 | bytes 1474560 | tf_op jit(solution)/shard_map/pallas_call | solution.py:343
  53.2 1.1 collective-permute-start.6
  54.3 0.9 collective-permute-start
  55.2 0.5 collective-permute-start.7
  55.8 11.5 %collective-permute-done.6.refs_4_ = bf16[720,384]{1,0:T(8,128)(2,1)} collective-permute-done((bf16[720,384]{1,0:T(8,128)(2,1)}, bf16[720,384]{1,0:T(8,128)(2,1)}, u32[]{:S(2)}, u32[]{:S(2)}) %collective-permute-start.6) | collective-permute-done | bytes 552992 | tf_op jit(solution)/shard_map/ppermute | solution.py:280
  67.2 2.4 %collective-permute-start.8 = (bf16[720,384]{1,0:T(8,128)(2,1)}, bf16[720,384]{1,0:T(8,128)(2,1)S(1)}, u32[]{:S(2)}, u32[]{:S(2)}) collective-permute-start(bf16[720,384]{1,0:T(8,128)(2,1)} %collective-permute-done.6.refs_4_), channel_id=1, source_target_pairs={{0,96},{32,0},{64,32},{96,64},{1,97},{33,1},{65,33},{97,65},{2,98}... | collective-permute-start | bytes 1658888 | tf_op jit(solution)/shard_map/ppermute | solution.py:280
  69.7 0.0 collective-permute-start.1
  69.7 1.3 collective-permute-done.refs_4_
  70.9 0.8 collective-permute-start.2
  71.7 0.0 copy-start
  71.7 2.3 %copy-done = bf16[4,720,720]{2,1,0:T(8,128)(2,1)S(1)} copy-done((bf16[4,720,720]{2,1,0:T(8,128)(2,1)S(1)}, bf16[4,720,720]{2,1,0:T(8,128)(2,1)}, u32[]{:S(2)}) %copy-start) | copy-done | bytes 4147224
  73.9 0.0 copy-start.1
  73.9 2.3 %copy-done.1 = bf16[4,720,720]{2,1,0:T(8,128)(2,1)S(1)} copy-done((bf16[4,720,720]{2,1,0:T(8,128)(2,1)S(1)}, bf16[4,720,720]{2,1,0:T(8,128)(2,1)}, u32[]{:S(2)}) %copy-start.1) | copy-done | bytes 4147224
  76.2 0.0 slice-start.3
  76.2 3.8 %shard_map.88 = (f32[720,384]{1,0:T(8,128)S(1)}, f32[720,384]{1,0:T(8,128)S(1)}) custom-call(s32[1]{0:T(128)} %bitcast.9.refs_0_.at_ref, bf16[4,720,720]{2,1,0:T(8,128)(2,1)S(1)} %copy-done, bf16[4,720,720]{2,1,0:T(8,128)(2,1)S(1)} %copy-done.1, bf16[720,384]{1,0:T(8,128)(2,1)} %shard_map.87.refs_3_, bf16[720,384]{1,0:T(8,128)(2,1)} %collective-permute-done.6.refs_4_), custom_call_target="tpu_custom_call" | custom-call | flops 1592524800 | bytes 4147200 | tf_op jit(solution)/shard_map/pallas_call | solution.py:353
  80.0 2.8 %collective-permute-done.7.refs_6_ = bf16[720,384]{1,0:T(8,128)(2,1)S(1)} collective-permute-done((bf16[720,384]{1,0:T(8,128)(2,1)}, bf16[720,384]{1,0:T(8,128)(2,1)S(1)}, u32[]{:S(2)}, u32[]{:S(2)}) %collective-permute-start.7) | collective-permute-done | bytes 552992 | tf_op jit(solution)/shard_map/ppermute | solution.py:280
  82.8 0.1 collective-permute-done.8.refs_7_
  82.9 0.0 slice-done.2
  82.9 0.0 slice-done.3
  82.9 3.2 %shard_map.89 = (bf16[720,384]{1,0:T(8,128)(2,1)S(1)}, bf16[720,384]{1,0:T(8,128)(2,1)S(1)}) custom-call(s32[1]{0:T(128)} %bitcast.9.refs_0_.at_ref, bf16[4,720,720]{2,1,0:T(8,128)(2,1)S(1)} %copy-done, bf16[4,720,720]{2,1,0:T(8,128)(2,1)S(1)} %copy-done.1, bf16[4,720,720]{2,1,0:T(8,128)(2,1)S(1)} %bitcast.18, f32[720,384]{1,0:T(8,128)S(1)} %get-tuple-element.54.refs_4_, ...), custom_call_target="tpu_custom_call" | custom-call | flops 1990656000 | bytes 5184000 | tf_op jit(solution)/shard_map/pallas_call | solution.py:362
  86.1 3.6 %collective-permute-start.10 = (bf16[720,384]{1,0:T(8,128)(2,1)S(1)}, bf16[720,384]{1,0:T(8,128)(2,1)S(1)}, u32[]{:S(2)}, u32[]{:S(2)}) collective-permute-start(bf16[720,384]{1,0:T(8,128)(2,1)S(1)} %get-tuple-element.60), channel_id=1, source_target_pairs={{0,96},{32,0},{64,32},{96,64},{1,97},{33,1},{65,33},{97,65},{2,98}... | collective-permute-start | bytes 1658888 | tf_op jit(solution)/shard_map/ppermute | solution.py:280
  89.7 5.0 %collective-permute-done.1.refs_5_ = bf16[720,384]{1,0:T(8,128)(2,1)S(1)} collective-permute-done((bf16[720,384]{1,0:T(8,128)(2,1)S(1)}, bf16[720,384]{1,0:T(8,128)(2,1)S(1)}, u32[]{:S(2)}, u32[]{:S(2)}) %collective-permute-start.1) | collective-permute-done | bytes 552992 | tf_op jit(solution)/shard_map/ppermute | solution.py:280
  94.7 0.0 slice-done
  94.7 0.0 slice-done.1
  94.7 3.6 %shard_map.84 = (f32[720,384]{1,0:T(8,128)S(1)}, f32[720,384]{1,0:T(8,128)S(1)}) custom-call(s32[1]{0:T(128)} %bitcast.9.refs_0_.at_ref, bf16[4,720,720]{2,1,0:T(8,128)(2,1)S(1)} %bitcast.16, bf16[4,720,720]{2,1,0:T(8,128)(2,1)S(1)} %copy-done.1, bf16[720,384]{1,0:T(8,128)(2,1)S(1)} %get-tuple-element.46.refs_3_, ...), custom_call_target="tpu_custom_call" | custom-call | flops 2388787200 | bytes 6220800 | tf_op jit(solution)/shard_map/pallas_call | solution.py:353
  98.3 0.0 collective-permute-done.2.refs_6_
  98.4 1.9 %shard_map.85 = (bf16[720,384]{1,0:T(8,128)(2,1)S(1)}, bf16[720,384]{1,0:T(8,128)(2,1)S(1)}) custom-call(s32[1]{0:T(128)} %bitcast.9.refs_0_.at_ref, bf16[4,720,720]{2,1,0:T(8,128)(2,1)S(1)} %bitcast.16, bf16[4,720,720]{2,1,0:T(8,128)(2,1)S(1)} %copy-done.1, bf16[4,720,720]{2,1,0:T(8,128)(2,1)S(1)} %bitcast.18, f32[720,384]{1,0:T(8,128)S(1)} %get-tuple-element.47.refs_4_, ...), custom_call_target="tpu_custom_call" | custom-call | flops 1194393600 | bytes 3110400 | tf_op jit(solution)/shard_map/pallas_call | solution.py:362
  100.3 0.6 collective-permute-start.3
  100.9 1.9 %shard_map.90 = (f32[720,384]{1,0:T(8,128)S(1)}, f32[720,384]{1,0:T(8,128)S(1)}, bf16[720,384]{1,0:T(8,128)(2,1)S(1)}) custom-call(s32[1]{0:T(128)} %bitcast.9.refs_0_.at_ref, bf16[720,384]{1,0:T(8,128)(2,1)S(1)} %get-tuple-element.56.h_ref, bf16[4,720,720]{2,1,0:T(8,128)(2,1)S(1)} %bitcast.18), custom_call_target="tpu_custom_call" | custom-call | flops 1194393600 | bytes 3110400 | tf_op jit(solution)/shard_map/pallas_call | solution.py:370
  102.8 1.4 collective-permute-start.9
  104.2 1.9 %shard_map.86 = (f32[720,384]{1,0:T(8,128)S(1)}, bf16[720,384]{1,0:T(8,128)(2,1)S(1)}, f32[720,384]{1,0:T(8,128)S(1)}) custom-call(s32[1]{0:T(128)} %bitcast.9.refs_0_.at_ref, bf16[720,384]{1,0:T(8,128)(2,1)S(1)} %get-tuple-element.49.h_ref, bf16[4,720,720]{2,1,0:T(8,128)(2,1)S(1)} %bitcast.18), custom_call_target="tpu_custom_call" | custom-call | flops 1194393600 | bytes 3110400 | tf_op jit(solution)/shard_map/pallas_call | solution.py:370
  106.0 2.0 %collective-permute-start.5 = (bf16[720,384]{1,0:T(8,128)(2,1)S(1)}, bf16[720,384]{1,0:T(8,128)(2,1)S(1)}, u32[]{:S(2)}, u32[]{:S(2)}) collective-permute-start(bf16[720,384]{1,0:T(8,128)(2,1)S(1)} %get-tuple-element.53), channel_id=1, source_target_pairs={{0,96},{32,0},{64,32},{96,64},{1,97},{33,1},{65,33},{97,65},{2,98}... | collective-permute-start | bytes 1658888 | tf_op jit(solution)/shard_map/ppermute | solution.py:280
  108.1 0.0 collective-permute-done.10
  108.1 0.1 add_convert_fusion
  108.2 2.2 %collective-permute-start.11 = (bf16[720,384]{1,0:T(8,128)(2,1)S(1)}, bf16[720,384]{1,0:T(8,128)(2,1)S(1)}, u32[]{:S(2)}, u32[]{:S(2)}) collective-permute-start(bf16[720,384]{1,0:T(8,128)(2,1)S(1)} %add_convert_fusion), channel_id=1, source_target_pairs={{0,96},{32,0},{64,32},{96,64},{1,97},{33,1},{65,33},{97,65},{2,98}... | collective-permute-start | bytes 1658888 | tf_op jit(solution)/shard_map/ppermute | solution.py:280
  110.4 7.0 %collective-permute-done.3 = bf16[720,384]{1,0:T(8,128)(2,1)S(1)} collective-permute-done((bf16[720,384]{1,0:T(8,128)(2,1)S(1)}, bf16[720,384]{1,0:T(8,128)(2,1)S(1)}, u32[]{:S(2)}, u32[]{:S(2)}) %collective-permute-start.3) | collective-permute-done | bytes 552992 | tf_op jit(solution)/shard_map/ppermute | solution.py:280
  117.4 0.1 add_convert_fusion.1
  117.5 0.1 collective-permute-start.4
  117.6 1.0 shard_map.83
  118.6 10.6 %collective-permute-done.9.refs_7_ = bf16[720,384]{1,0:T(8,128)(2,1)S(1)} collective-permute-done((bf16[720,384]{1,0:T(8,128)(2,1)S(1)}, bf16[720,384]{1,0:T(8,128)(2,1)S(1)}, u32[]{:S(2)}, u32[]{:S(2)}) %collective-permute-start.9) | collective-permute-done | bytes 552992 | tf_op jit(solution)/shard_map/ppermute | solution.py:280
  129.3 0.0 collective-permute-done.5.refs_5_
  129.3 0.0 collective-permute-done.11.refs_8_
  129.3 6.4 %collective-permute-done.4.refs_4_ = bf16[720,384]{1,0:T(8,128)(2,1)S(1)} collective-permute-done((bf16[720,384]{1,0:T(8,128)(2,1)S(1)}, bf16[720,384]{1,0:T(8,128)(2,1)S(1)}, u32[]{:S(2)}, u32[]{:S(2)}) %collective-permute-start.4) | collective-permute-done | bytes 552992 | tf_op jit(solution)/shard_map/ppermute | solution.py:280
  135.6 3.2 %shard_map.91 = bf16[1024,1152]{1,0:T(8,128)(2,1)S(1)} custom-call(bf16[1024,768]{1,0:T(8,128)(2,1)S(1)} %get-tuple-element.40.refs_0_, bf16[1024,768]{1,0:T(8,128)(2,1)S(1)} %get-tuple-element.41.refs_1_, bf16[1024,768]{1,0:T(8,128)(2,1)S(1)} %get-tuple-element.42.refs_2_, f32[720,384]{1,0:T(8,128)S(1)} %get-tuple-element.50.refs_3_, ...), custom_call_target="tpu_custom_call" | custom-call | flops 1132462080 | bytes 1474560 | tf_op jit(solution)/shard_map/pallas_call | solution.py:399
  138.8 0.0 copy-start.2
  138.8 1.4 copy-done.2
  140.3 8.2 %all-to-all-start.1 = ((bf16[128,8,1152]{2,1,0:T(8,128)(2,1)}), bf16[128,8,1152]{2,1,0:T(8,128)(2,1)S(1)}, u32[]{:S(2)}, u32[]{:S(2)}) async-start(bf16[128,8,1152]{2,1,0:T(8,128)(2,1)} %bitcast.20), calls=%async_computation.1 | async-start | bytes 4718592 | tf_op jit(solution)/shard_map/all_to_all | solution.py:286
  148.5 0.0 copy-done.3
  148.5 0.0 copy-done.4
  148.5 0.5 shard_map.92.refs_1_
  149.1 32.7 %all-to-all-done.1 = bf16[128,8,1152]{2,1,0:T(8,128)(2,1)S(1)} async-done(((bf16[128,8,1152]{2,1,0:T(8,128)(2,1)}), bf16[128,8,1152]{2,1,0:T(8,128)(2,1)S(1)}, u32[]{:S(2)}, u32[]{:S(2)}) %all-to-all-start.1) | async-done | bytes 2359328 | tf_op jit(solution)/shard_map/all_to_all | solution.py:286
  181.7 1.4 shard_map.93
  (6 shorter events, 0.0 us)
Async XLA Ops:
  4.1 11.2 %copy-start.6 = (s32[32]{0:T(128)S(1)}, s32[32]{0:T(128)}, u32[]{:S(2)}) copy-start(s32[32]{0:T(128)} %param.12) | copy-start | bytes 388
  4.1 13.7 %copy-start.5 = (s32[32]{0:T(128)S(1)}, s32[32]{0:T(128)}, u32[]{:S(2)}) copy-start(s32[32]{0:T(128)} %param.11) | copy-start | bytes 388
  4.1 44.4 %all-to-all-start = ((bf16[128,8,1152]{2,1,0:T(8,128)(2,1)}), bf16[128,8,1152]{2,1,0:T(8,128)(2,1)S(1)}, u32[]{:S(2)}, u32[]{:S(2)}) async-start(bf16[128,8,1152]{2,1,0:T(8,128)(2,1)} %bitcast.26), calls=%async_computation | async-start | bytes 4718592 | tf_op jit(solution)/shard_map/all_to_all | solution.py:286
  50.7 32.2 %slice-start.2 = ((s8[4423680]{0:T(1024)(128)(4,1)}), s8[229376]{0:T(1024)(128)(4,1)S(1)}, s32[]{:S(2)}) async-start(s8[4423680]{0:T(1024)(128)(4,1)} %bitcast.17), calls=%async_computation.4 | async-start | bytes 458752
  53.2 14.0 %collective-permute-start.6 = (bf16[720,384]{1,0:T(8,128)(2,1)}, bf16[720,384]{1,0:T(8,128)(2,1)}, u32[]{:S(2)}, u32[]{:S(2)}) collective-permute-start(bf16[720,384]{1,0:T(8,128)(2,1)} %shard_map.87.refs_3_), channel_id=1, source_target_pairs={{0,96},{32,0},{64,32},{96,64},{1,97},{33,1},{65,33},{97,65},{2,98}... | collective-permute-start | bytes 1658888 | tf_op jit(solution)/shard_map/ppermute | solution.py:280
  54.3 16.6 %collective-permute-start = (bf16[720,384]{1,0:T(8,128)(2,1)S(1)}, bf16[720,384]{1,0:T(8,128)(2,1)S(1)}, u32[]{:S(2)}, u32[]{:S(2)}) collective-permute-start(bf16[720,384]{1,0:T(8,128)(2,1)S(1)} %get-tuple-element.46.refs_3_), channel_id=1, source_target_pairs={{0,32},{32,64},{64,96},{96,0},{1,33},{33,65},{65,97},{97,1},{2,34}... | collective-permute-start | bytes 1658888 | tf_op jit(solution)/shard_map/ppermute | solution.py:280
  55.2 27.6 %collective-permute-start.7 = (bf16[720,384]{1,0:T(8,128)(2,1)}, bf16[720,384]{1,0:T(8,128)(2,1)S(1)}, u32[]{:S(2)}, u32[]{:S(2)}) collective-permute-start(bf16[720,384]{1,0:T(8,128)(2,1)} %shard_map.87.refs_3_), channel_id=1, source_target_pairs={{0,32},{32,64},{64,96},{96,0},{1,33},{33,65},{65,97},{97,1},{2,34}... | collective-permute-start | bytes 1658888 | tf_op jit(solution)/shard_map/ppermute | solution.py:280
  67.2 15.7 %collective-permute-start.8 = (bf16[720,384]{1,0:T(8,128)(2,1)}, bf16[720,384]{1,0:T(8,128)(2,1)S(1)}, u32[]{:S(2)}, u32[]{:S(2)}) collective-permute-start(bf16[720,384]{1,0:T(8,128)(2,1)} %collective-permute-done.6.refs_4_), channel_id=1, source_target_pairs={{0,96},{32,0},{64,32},{96,64},{1,97},{33,1},{65,33},{97,65},{2,98}... | collective-permute-start | bytes 1658888 | tf_op jit(solution)/shard_map/ppermute | solution.py:280
  69.7 25.0 %collective-permute-start.1 = (bf16[720,384]{1,0:T(8,128)(2,1)S(1)}, bf16[720,384]{1,0:T(8,128)(2,1)S(1)}, u32[]{:S(2)}, u32[]{:S(2)}) collective-permute-start(bf16[720,384]{1,0:T(8,128)(2,1)S(1)} %get-tuple-element.46.refs_3_), channel_id=1, source_target_pairs={{0,96},{32,0},{64,32},{96,64},{1,97},{33,1},{65,33},{97,65},{2,98}... | collective-permute-start | bytes 1658888 | tf_op jit(solution)/shard_map/ppermute | solution.py:280
  70.9 27.4 %collective-permute-start.2 = (bf16[720,384]{1,0:T(8,128)(2,1)S(1)}, bf16[720,384]{1,0:T(8,128)(2,1)S(1)}, u32[]{:S(2)}, u32[]{:S(2)}) collective-permute-start(bf16[720,384]{1,0:T(8,128)(2,1)S(1)} %collective-permute-done.refs_4_), channel_id=1, source_target_pairs={{0,32},{32,64},{64,96},{96,0},{1,33},{33,65},{65,97},{97,1},{2,34}... | collective-permute-start | bytes 1658888 | tf_op jit(solution)/shard_map/ppermute | solution.py:280
  71.7 2.3 %copy-start = (bf16[4,720,720]{2,1,0:T(8,128)(2,1)S(1)}, bf16[4,720,720]{2,1,0:T(8,128)(2,1)}, u32[]{:S(2)}) copy-start(bf16[4,720,720]{2,1,0:T(8,128)(2,1)} %get-tuple-element.43.refs_1_) | copy-start | bytes 12441604
  73.9 2.3 %copy-start.1 = (bf16[4,720,720]{2,1,0:T(8,128)(2,1)S(1)}, bf16[4,720,720]{2,1,0:T(8,128)(2,1)}, u32[]{:S(2)}) copy-start(bf16[4,720,720]{2,1,0:T(8,128)(2,1)} %get-tuple-element.44.refs_2_) | copy-start | bytes 12441604
  76.2 6.7 %slice-start.3 = ((s8[4423680]{0:T(1024)(128)(4,1)}), s8[4194304]{0:T(1024)(128)(4,1)S(1)}, s32[]{:S(2)}) async-start(s8[4423680]{0:T(1024)(128)(4,1)} %bitcast.17), calls=%async_computation.5 | async-start | bytes 8388608
  82.9 11.8 %slice-start = ((s8[4423680]{0:T(1024)(128)(4,1)}), s8[4194304]{0:T(1024)(128)(4,1)S(1)}, s32[]{:S(2)}) async-start(s8[4423680]{0:T(1024)(128)(4,1)} %bitcast.15), calls=%async_computation.2 | async-start | bytes 8388608
  82.9 11.8 %slice-start.1 = ((s8[4423680]{0:T(1024)(128)(4,1)}), s8[229376]{0:T(1024)(128)(4,1)S(1)}, s32[]{:S(2)}) async-start(s8[4423680]{0:T(1024)(128)(4,1)} %bitcast.15), calls=%async_computation.3 | async-start | bytes 458752
  86.1 22.0 %collective-permute-start.10 = (bf16[720,384]{1,0:T(8,128)(2,1)S(1)}, bf16[720,384]{1,0:T(8,128)(2,1)S(1)}, u32[]{:S(2)}, u32[]{:S(2)}) collective-permute-start(bf16[720,384]{1,0:T(8,128)(2,1)S(1)} %get-tuple-element.60), channel_id=1, source_target_pairs={{0,96},{32,0},{64,32},{96,64},{1,97},{33,1},{65,33},{97,65},{2,98}... | collective-permute-start | bytes 1658888 | tf_op jit(solution)/shard_map/ppermute | solution.py:280
  100.3 17.1 %collective-permute-start.3 = (bf16[720,384]{1,0:T(8,128)(2,1)S(1)}, bf16[720,384]{1,0:T(8,128)(2,1)S(1)}, u32[]{:S(2)}, u32[]{:S(2)}) collective-permute-start(bf16[720,384]{1,0:T(8,128)(2,1)S(1)} %get-tuple-element.52), channel_id=1, source_target_pairs={{0,32},{32,64},{64,96},{96,0},{1,33},{33,65},{65,97},{97,1},{2,34}... | collective-permute-start | bytes 1658888 | tf_op jit(solution)/shard_map/ppermute | solution.py:280
  102.8 26.5 %collective-permute-start.9 = (bf16[720,384]{1,0:T(8,128)(2,1)S(1)}, bf16[720,384]{1,0:T(8,128)(2,1)S(1)}, u32[]{:S(2)}, u32[]{:S(2)}) collective-permute-start(bf16[720,384]{1,0:T(8,128)(2,1)S(1)} %get-tuple-element.58), channel_id=1, source_target_pairs={{0,32},{32,64},{64,96},{96,0},{1,33},{33,65},{65,97},{97,1},{2,34}... | collective-permute-start | bytes 1658888 | tf_op jit(solution)/shard_map/ppermute | solution.py:280
  106.0 23.2 %collective-permute-start.5 = (bf16[720,384]{1,0:T(8,128)(2,1)S(1)}, bf16[720,384]{1,0:T(8,128)(2,1)S(1)}, u32[]{:S(2)}, u32[]{:S(2)}) collective-permute-start(bf16[720,384]{1,0:T(8,128)(2,1)S(1)} %get-tuple-element.53), channel_id=1, source_target_pairs={{0,96},{32,0},{64,32},{96,64},{1,97},{33,1},{65,33},{97,65},{2,98}... | collective-permute-start | bytes 1658888 | tf_op jit(solution)/shard_map/ppermute | solution.py:280
  108.2 21.0 %collective-permute-start.11 = (bf16[720,384]{1,0:T(8,128)(2,1)S(1)}, bf16[720,384]{1,0:T(8,128)(2,1)S(1)}, u32[]{:S(2)}, u32[]{:S(2)}) collective-permute-start(bf16[720,384]{1,0:T(8,128)(2,1)S(1)} %add_convert_fusion), channel_id=1, source_target_pairs={{0,96},{32,0},{64,32},{96,64},{1,97},{33,1},{65,33},{97,65},{2,98}... | collective-permute-start | bytes 1658888 | tf_op jit(solution)/shard_map/ppermute | solution.py:280
  117.5 18.1 %collective-permute-start.4 = (bf16[720,384]{1,0:T(8,128)(2,1)S(1)}, bf16[720,384]{1,0:T(8,128)(2,1)S(1)}, u32[]{:S(2)}, u32[]{:S(2)}) collective-permute-start(bf16[720,384]{1,0:T(8,128)(2,1)S(1)} %add_convert_fusion.1), channel_id=1, source_target_pairs={{0,32},{32,64},{64,96},{96,0},{1,33},{33,65},{65,97},{97,1},{2,34}... | collective-permute-start | bytes 1658888 | tf_op jit(solution)/shard_map/ppermute | solution.py:280
  138.8 1.4 copy-start.2
  140.2 8.2 %copy-start.3 = (s32[32,4]{0,1:T(4,128)S(1)}, s32[32,4]{0,1:T(4,128)}, u32[]{:S(2)}) copy-start(s32[32,4]{0,1:T(4,128)} %param.9) | copy-start | bytes 1540
  140.3 8.3 %copy-start.4 = (f32[32,4]{0,1:T(4,128)S(1)}, f32[32,4]{0,1:T(4,128)}, u32[]{:S(2)}) copy-start(f32[32,4]{0,1:T(4,128)} %param.10) | copy-start | bytes 1540
  140.3 41.5 %all-to-all-start.1 = ((bf16[128,8,1152]{2,1,0:T(8,128)(2,1)}), bf16[128,8,1152]{2,1,0:T(8,128)(2,1)S(1)}, u32[]{:S(2)}, u32[]{:S(2)}) async-start(bf16[128,8,1152]{2,1,0:T(8,128)(2,1)} %bitcast.20), calls=%async_computation.1 | async-start | bytes 4718592 | tf_op jit(solution)/shard_map/all_to_all | solution.py:286

commit v4 on v2

--- a/solution.py
+++ b/solution.py
@@ -75,7 +75,7 @@
     gather_slots(lay, [row_ref[k : k + 1] for k in range(3)], x_ref, first, out)
 
 
-def pick_kernel(lay, x_ref, par_ref, row_ref, col_ref, out):
+def pick_kernel(lay, x_ref, par_ref, row_ref, out):
     came, seats = x_ref.shape[0], lay.seats
     sources = came // seats
     bound = par_ref[0].astype(F32)
@@ -99,9 +99,7 @@
     over = jnp.where(jnp.logical_and(part > 0.5, over < bound), over, -1.0)
     evens, odds = jnp.where(even, over, -1.0), jnp.where(even, -1.0, over)
     nothing = jnp.full((5, came), -1.0, F32)
-    every = jnp.concatenate([rank, evens, odds, nothing], axis=0)
-    row_ref[...] = every
-    col_ref[...] = every.T
+    row_ref[...] = jnp.concatenate([rank, evens, odds, nothing], axis=0)
     gather_slots(lay, (rank, evens, odds), x_ref, 0, out)
 
 
@@ -147,25 +145,30 @@
         out[...] = dot(wd_ref[block], hidden).astype(out.dtype)
 
 
-def place_kernel(lay, slot_ref, *refs):
+def spots_kernel(row_ref, *outs):
+    places = row_ref[...].T
+    for k, out in enumerate(outs):
+        out[...] = hot(places[:, k : k + 1], out.shape[1]).astype(BF)
+
+
+def place_kernel(lay, whole_ref, even_ref, odd_ref, *refs):
     ins, z_ref = refs[:-1], refs[-1]
     columns = []
     for own, left, right in (ins[:3], ins[3:]):
         total = own[...] + left[...].astype(F32) + right[...].astype(F32)
         columns.append(total.astype(BF))
     y = jnp.concatenate(columns, axis=1)
-    slots, came = y.shape[1], z_ref.shape[0]
-    at = lambda k: hot(slot_ref[:, k : k + 1], slots).astype(BF)
+    came = z_ref.shape[0]
     none = lambda n: jnp.zeros((came, n), BF)
-    rows = dot(at(0), y, ((1,), (1,))).astype(BF)
+    rows = dot(whole_ref[...], y, ((1,), (1,))).astype(BF)
     z_ref[:, : lay.low] = jnp.concatenate([rows, none(lay.low - lay.width)], axis=1)
-    left = dot(at(1), y[: lay.point], ((1,), (1,))).astype(BF)
-    right = dot(at(2), y[lay.point :], ((1,), (1,))).astype(BF)
+    left = dot(even_ref[...], y[: lay.point], ((1,), (1,))).astype(BF)
+    right = dot(odd_ref[...], y[lay.point :], ((1,), (1,))).astype(BF)
     z_ref[:, lay.low :] = left + jnp.concatenate([right, none(lay.short)], axis=1)
 
 
-def mix_kernel(lay, b_ref, id_ref, p_ref, o_ref):
-    tok, seats = o_ref.shape[0], lay.seats
+def router_kernel(lay, id_ref, p_ref, w_ref):
+    tok, seats = id_ref.shape[1], lay.seats
     ids, prob = id_ref[...].astype(F32).T, p_ref[...].T
     top = ids.shape[1]
     lane = iota((tok, lay.experts), 1).astype(F32)
@@ -185,16 +188,19 @@
         odd = jnp.where(seat < seats, -1.0, over + 1.0)
         for n, place in enumerate((full, over, odd)):
             kinds[n] += hot(place, rows) * prob[:, k : k + 1]
-    weights = []
-    for kind in kinds:
+    for n, kind in enumerate(kinds):
         high = kind.astype(BF)
         rest = kind - high.astype(F32)
         middle = rest.astype(BF)
         low = (rest - middle.astype(F32)).astype(BF)
-        weights.append(jnp.concatenate([high, middle, low], axis=0))
+        w_ref[n] = jnp.concatenate([high, middle, low], axis=0)
+
+
+def mix_kernel(lay, b_ref, w_ref, o_ref):
+    tok, rows = o_ref.shape[0], w_ref.shape[2]
 
     def weighted(n, block):
-        three = dot(weights[n], block)
+        three = dot(w_ref[n], block)
         return three[:tok] + three[tok : 2 * tok] + three[2 * tok :]
 
     for b in range(o_ref.shape[1] // lay.width):
@@ -275,6 +281,8 @@
         return moved.reshape(came, lay.lanes)
 
     packed = shape((came, lay.lanes), BF)
+    block_rows = experts * lay.seats
+    block_rows = experts * lay.seats
     outgoing, seen = run(
         lambda *refs: send_kernel(lay, *refs),
         [VMEM] * 2,
@@ -299,18 +307,26 @@
     )(seen, gate_weight[0].T, up_weight[0].T, down_weight[0])
     arrived, wg, wu, wd = lax.optimization_barrier((arrived, wg, wu, wd))
 
+    weights = run(
+        lambda *refs: router_kernel(lay, *refs),
+        [VMEM] * 2,
+        shape((3, 3 * tok, block_rows), BF),
+        (12 * tok * block_rows, 18 * tok * block_rows),
+    )(expert_ids.T, gate_probs.T)
     part = slots // 2
     columns = shape((width, part), BF)
     gather_work = (2 * slots * came * width, 2 * came * width)
-    places, slot, own_a = run(
+    places, own_a = run(
         lambda *refs: pick_kernel(lay, *refs),
         [VMEM, SMEM],
-        (shape((8, came), F32), shape((came, 8), F32), columns),
+        (shape((8, came), F32), columns),
         gather_work,
     )(arrived, par)
     own_b = run(
         lambda *refs: pick_more_kernel(lay, part, *refs), [VMEM] * 2, columns, gather_work
     )(arrived, places)
+    spot = shape((came, slots), BF)
+    spots = run(spots_kernel, [VMEM], (spot,) * 3, (6 * came * slots, 6 * came * slots))(places)
     before, after, across = groups - 1, 1, groups // 2
     area = width * units
     rows = lambda n, kind: shape((n, part), kind)
@@ -343,34 +359,35 @@
     def add(mine, came):
         return (mine + came.astype(F32)).astype(BF)
 
-    below_a, above_a = right(own_a), left(own_a)
+    above_a = left(own_a)
+    below_b = right(own_b)
     above_b = left(own_b)
-    far_a = right(below_a)
-    below_b = right(own_b)
-    far_b = left(above_b)
+    below_a = right(own_a)
+    far_a = left(above_a)
+    far_b = right(below_b)
     sums_a = mid((own_a, below_a, above_a), (0, before, after))
+    sums_b = mid((own_b, below_b, above_b), (0, before, after))
     hidden_a, share_a = far(sums_a, (far_a,), (across,))
     crossed_a = right(share_a)
-    mine_a, left_a, right_a = near(hidden_a, (F32, BF, F32))
-    from_right_a = left(left_a)
-    sums_b = mid((own_b, above_b), (0, after))
-    hidden_b, share_b = far(sums_b, (below_b, far_b), (before, across))
+    hidden_b, share_b = far(sums_b, (far_b,), (across,))
     crossed_b = left(share_b)
     mine_b, left_b, right_b = near(hidden_b, (F32, F32, BF))
     from_left_b = right(right_b)
+    mine_a, left_a, right_a = near(hidden_a, (F32, BF, F32))
+    from_right_a = left(left_a)
     added_a, added_b = add(right_a, crossed_a), add(left_b, crossed_b)
     from_left_a = right(added_a)
     from_right_b = left(added_b)
     sums = (mine_a, from_left_a, from_right_a, mine_b, from_left_b, from_right_b)
     answers = run(
-        lambda *refs: place_kernel(lay, *refs), [VMEM] * 7, packed, gather_work
-    )(slot, *sums)
+        lambda *refs: place_kernel(lay, *refs), [VMEM] * 9, packed, gather_work
+    )(*spots, *sums)
     return run(
         lambda *refs: mix_kernel(lay, *refs),
-        [VMEM] * 3,
+        [VMEM] * 2,
         shape((tok, model), BF),
         (6 * tok * came * width, 2 * came * width),
-    )(exchange(answers), expert_ids.T, gate_probs.T)
+    )(exchange(answers), weights)
 
 
 def solution(mesh):

time: 182 us -> 183 us (level)
  blocking collectives: 41.3 us -> 0 us
  waiting for transfers between devices: 61.1 us -> 93.4 us
  starting transfers between devices: 26.9 us -> 34.2 us
    all_to_all x1 -> x0, blocking collectives: 41.3 us -> none  [exchange(): lax.all_to_all(blocks, ATTN_EXPERT, split_axis=0, concat_axis=0, tiled=True)]
    all_to_all x1 -> x2, waiting for transfers between devices: 15.6 us -> 48.2 us  [exchange(): lax.all_to_all(blocks, ATTN_EXPERT, split_axis=0, concat_axis=0, tiled=True)]
    all_to_all x1 -> x2, starting transfers between devices: 11.2 us -> 17.1 us  [exchange(): lax.all_to_all(blocks, ATTN_EXPERT, split_axis=0, concat_axis=0, tiled=True)]
    unnamed x24 -> x22, local copies, waits for them, and re-layouts: 4.55 us -> 5.96 us
    pallas_call x2 -> x4, Pallas kernels: 5.13 us -> 6.08 us  [the longest x1 3.17 us: on_device(): run(lambda *refs: place_kernel(lay, *refs), [VMEM] * 9, packed, gather_work)]
  transfers between devices with their start and end apart: 13 -> 14, of which waited for: 9 -> 8; matrix products, arithmetic and copies ran while one was open for 1% -> 1% of each run, Pallas kernels for 16% -> 17%
where the time goes in v4:
time: 183 us; the launch traced here: 182 us
  waiting for transfers between devices  93.4 us (51%)
  Pallas kernels  43.9 us (24%)
  starting transfers between devices  34.2 us (19%)
  local copies, waits for them, and re-layouts  7.19 us (4%)
  between operations  3.39 us (2%)
    all_to_all x2, waiting for transfers between devices, exchange(): lax.all_to_all(blocks, ATTN_EXPERT, split_axis=0, concat_axis=0, tiled=True)  48.2 us
    ppermute x12, waiting for transfers between devices, shifted(): return lambda array: lax.ppermute(array, 'attn', pairs)  45.2 us
    all_to_all x2, starting transfers between devices, exchange(): lax.all_to_all(blocks, ATTN_EXPERT, split_axis=0, concat_axis=0, tiled=True)  17.1 us
    ppermute x12, starting transfers between devices, shifted(): return lambda array: lax.ppermute(array, 'attn', pairs)  17.1 us
    pallas_call x1, Pallas kernels, on_device(): pl.pallas_call(relay_kernel, grid=(pl.cdiv(units, step),), out_shape=(rel...  13.3 us
    pallas_call x2, Pallas kernels, mid(): run(lambda *refs: mid_kernel(ahead, *refs), [SMEM] + [VMEM] * (2 + len(bl...  8.61 us
    unnamed x22, local copies, waits for them, and re-layouts  5.96 us
    pallas_call x2, Pallas kernels, far(): run(lambda *refs: far_kernel(ahead, *refs), [SMEM] + [VMEM] * (5 + len(bl...  3.9 us
  transfers between devices with their start and end apart: 14, of which 8 were waited for; matrix products, arithmetic and copies ran while one was open for 1% of the time, Pallas kernels for 17%

profile of v4, /device:TPU:0, one launch (start us, length us, event | category | flops | bytes accessed | tf_op | source)
XLA Modules:
  0.0 182.4 jit_solution(6472967086030714866)
XLA Ops:
  0.0 3.6 %shard_map.82 = (bf16[1024,1152]{1,0:T(8,128)(2,1)}, f32[8,128]{1,0:T(8,128)}) custom-call(bf16[32,2880]{1,0:T(8,128)(2,1)} %refs_0_.1, s32[4,32]{1,0:T(4,128)} %bitcast.23), custom_call_target="tpu_custom_call" | custom-call | flops 47185920 | bytes 1474560 | tf_op jit(solution)/shard_map/pallas_call | solution.py:286
  3.6 0.0 copy-start.6
  3.6 0.0 copy-start.5
  3.6 11.2 %all-to-all-start = ((bf16[128,8,1152]{2,1,0:T(8,128)(2,1)}), bf16[128,8,1152]{2,1,0:T(8,128)(2,1)S(1)}, u32[]{:S(2)}, u32[]{:S(2)}) async-start(bf16[128,8,1152]{2,1,0:T(8,128)(2,1)} %bitcast.26), calls=%async_computation | async-start | bytes 4718592 | tf_op jit(solution)/shard_map/all_to_all | solution.py:280
  14.8 0.0 copy-done.6
  14.8 0.6 dynamic_slice.9
  17.3 0.0 copy-done.5
  17.3 0.6 fusion
  19.2 13.3 %relay.1 = (bf16[4,720,720]{2,1,0:T(8,128)(2,1)}, bf16[4,720,720]{2,1,0:T(8,128)(2,1)}, bf16[4,720,720]{2,1,0:T(8,128)(2,1)}) custom-call(f32[8,128]{1,0:T(8,128)} %get-tuple-element.34.seen_ref, bf16[720,2880]{1,0:T(8,128)(2,1)} %bitcast.27, bf16[720,2880]{1,0:T(8,128)(2,1)} %bitcast.28, bf16[720,2880]{1,0:T(8,128)(2,1)} %bitcast.29), custom_call_target="tpu_custom_call" | custom-call | flops 4777574400 | bytes 24883200 | tf_op jit(solution)/shard_map/relay/pallas_call | solution.py:298
  32.4 15.6 %all-to-all-done = bf16[128,8,1152]{2,1,0:T(8,128)(2,1)S(1)} async-done(((bf16[128,8,1152]{2,1,0:T(8,128)(2,1)}), bf16[128,8,1152]{2,1,0:T(8,128)(2,1)S(1)}, u32[]{:S(2)}, u32[]{:S(2)}) %all-to-all-start) | async-done | bytes 2359328 | tf_op jit(solution)/shard_map/all_to_all | solution.py:280
  48.0 2.2 %shard_map.83 = (f32[8,1024]{1,0:T(8,128)S(1)}, bf16[720,384]{1,0:T(8,128)(2,1)S(1)}) custom-call(bf16[1024,1152]{1,0:T(8,128)(2,1)S(1)} %bitcast.21, s32[1]{0:T(128)S(6)} %add.27.refs_1_), custom_call_target="tpu_custom_call" | custom-call | flops 1132462080 | bytes 1474560 | tf_op jit(solution)/shard_map/pallas_call | solution.py:319
  50.2 0.0 slice-start.2
  50.2 2.5 %shard_map.88.refs_3_ = bf16[720,384]{1,0:T(8,128)(2,1)} custom-call(bf16[1024,1152]{1,0:T(8,128)(2,1)S(1)} %bitcast.22, f32[8,1024]{1,0:T(8,128)S(1)} %get-tuple-element.39.row_ref.refs_1_), custom_call_target="tpu_custom_call" | custom-call | flops 1132462080 | bytes 1474560 | tf_op jit(solution)/shard_map/pallas_call | solution.py:325
  52.7 0.5 collective-permute-start.6
  53.2 2.7 %collective-permute-start.1 = (bf16[720,384]{1,0:T(8,128)(2,1)S(1)}, bf16[720,384]{1,0:T(8,128)(2,1)S(1)}, u32[]{:S(2)}, u32[]{:S(2)}) collective-permute-start(bf16[720,384]{1,0:T(8,128)(2,1)S(1)} %get-tuple-element.46.refs_3_), channel_id=1, source_target_pairs={{0,96},{32,0},{64,32},{96,64},{1,97},{33,1},{65,33},{97,65},{2,98}... | collective-permute-start | bytes 1658888 | tf_op jit(solution)/shard_map/ppermute | solution.py:274
  55.9 0.0 collective-permute-start.7
  55.9 11.9 %collective-permute-done.6.refs_4_ = bf16[720,384]{1,0:T(8,128)(2,1)S(1)} collective-permute-done((bf16[720,384]{1,0:T(8,128)(2,1)}, bf16[720,384]{1,0:T(8,128)(2,1)S(1)}, u32[]{:S(2)}, u32[]{:S(2)}) %collective-permute-start.6) | collective-permute-done | bytes 552992 | tf_op jit(solution)/shard_map/ppermute | solution.py:274
  67.8 0.0 collective-permute-start.8
  67.8 0.5 collective-permute-start
  68.3 0.5 collective-permute-done.1.refs_5_
  68.8 3.7 %collective-permute-start.2 = (bf16[720,384]{1,0:T(8,128)(2,1)S(1)}, bf16[720,384]{1,0:T(8,128)(2,1)S(1)}, u32[]{:S(2)}, u32[]{:S(2)}) collective-permute-start(bf16[720,384]{1,0:T(8,128)(2,1)S(1)} %collective-permute-done.1.refs_5_), channel_id=1, source_target_pairs={{0,96},{32,0},{64,32},{96,64},{1,97},{33,1},{65,33},{97,65},{2,98}... | collective-permute-start | bytes 1658888 | tf_op jit(solution)/shard_map/ppermute | solution.py:274
  72.5 8.3 %collective-permute-done.7.refs_5_ = bf16[720,384]{1,0:T(8,128)(2,1)} collective-permute-done((bf16[720,384]{1,0:T(8,128)(2,1)}, bf16[720,384]{1,0:T(8,128)(2,1)}, u32[]{:S(2)}, u32[]{:S(2)}) %collective-permute-start.7) | collective-permute-done | bytes 552992 | tf_op jit(solution)/shard_map/ppermute | solution.py:274
  80.8 0.0 copy-start
  80.8 2.3 %copy-done = bf16[4,720,720]{2,1,0:T(8,128)(2,1)S(1)} copy-done((bf16[4,720,720]{2,1,0:T(8,128)(2,1)S(1)}, bf16[4,720,720]{2,1,0:T(8,128)(2,1)}, u32[]{:S(2)}) %copy-start) | copy-done | bytes 4147224
  83.1 2.3 %copy-done.1 = bf16[4,720,720]{2,1,0:T(8,128)(2,1)S(1)} copy-done((bf16[4,720,720]{2,1,0:T(8,128)(2,1)S(1)}, bf16[4,720,720]{2,1,0:T(8,128)(2,1)}, u32[]{:S(2)}) %copy-start.1) | copy-done | bytes 4147224
  85.3 5.0 %shard_map.89 = (f32[720,384]{1,0:T(8,128)S(1)}, f32[720,384]{1,0:T(8,128)S(1)}) custom-call(s32[1]{0:T(128)} %bitcast.9.refs_0_.at_ref, bf16[4,720,720]{2,1,0:T(8,128)(2,1)S(1)} %copy-done, bf16[4,720,720]{2,1,0:T(8,128)(2,1)S(1)} %copy-done.1, bf16[720,384]{1,0:T(8,128)(2,1)} %shard_map.88.refs_3_, bf16[720,384]{1,0:T(8,128)(2,1)S(1)} %collective-permute-done.6.refs_4_, ...), custom_call_target="tpu_custom_call" | custom-call | flops 2388787200 | bytes 6220800 | tf_op jit(solution)/shard_map/pallas_call | solution.py:335
  90.3 0.0 collective-permute-done.8.refs_6_
  90.3 0.0 slice-start
  90.3 0.0 slice-done.2
  90.3 0.0 slice-done.3
  90.3 0.0 slice-start.1
  90.3 1.9 %shard_map.90 = (bf16[720,384]{1,0:T(8,128)(2,1)S(1)}, bf16[720,384]{1,0:T(8,128)(2,1)S(1)}) custom-call(s32[1]{0:T(128)} %bitcast.9.refs_0_.at_ref, bf16[4,720,720]{2,1,0:T(8,128)(2,1)S(1)} %copy-done, bf16[4,720,720]{2,1,0:T(8,128)(2,1)S(1)} %copy-done.1, bf16[4,720,720]{2,1,0:T(8,128)(2,1)S(1)} %bitcast.18, f32[720,384]{1,0:T(8,128)S(1)} %get-tuple-element.54.refs_4_, ...), custom_call_target="tpu_custom_call" | custom-call | flops 1194393600 | bytes 3110400 | tf_op jit(solution)/shard_map/pallas_call | solution.py:344
  92.3 4.0 %collective-permute-start.10 = (bf16[720,384]{1,0:T(8,128)(2,1)S(1)}, bf16[720,384]{1,0:T(8,128)(2,1)S(1)}, u32[]{:S(2)}, u32[]{:S(2)}) collective-permute-start(bf16[720,384]{1,0:T(8,128)(2,1)S(1)} %get-tuple-element.60), channel_id=1, source_target_pairs={{0,96},{32,0},{64,32},{96,64},{1,97},{33,1},{65,33},{97,65},{2,98}... | collective-permute-start | bytes 1658888 | tf_op jit(solution)/shard_map/ppermute | solution.py:274
  96.3 0.0 collective-permute-done.refs_4_
  96.3 0.0 slice-done
  96.3 0.0 slice-done.1
  96.3 3.6 %shard_map.85 = (f32[720,384]{1,0:T(8,128)S(1)}, f32[720,384]{1,0:T(8,128)S(1)}) custom-call(s32[1]{0:T(128)} %bitcast.9.refs_0_.at_ref, bf16[4,720,720]{2,1,0:T(8,128)(2,1)S(1)} %bitcast.16, bf16[4,720,720]{2,1,0:T(8,128)(2,1)S(1)} %copy-done.1, bf16[720,384]{1,0:T(8,128)(2,1)S(1)} %get-tuple-element.46.refs_3_, ...), custom_call_target="tpu_custom_call" | custom-call | flops 2388787200 | bytes 6220800 | tf_op jit(solution)/shard_map/pallas_call | solution.py:335
  99.9 0.0 collective-permute-done.2.refs_6_
  100.0 1.9 %shard_map.86 = (bf16[720,384]{1,0:T(8,128)(2,1)S(1)}, bf16[720,384]{1,0:T(8,128)(2,1)S(1)}) custom-call(s32[1]{0:T(128)} %bitcast.9.refs_0_.at_ref, bf16[4,720,720]{2,1,0:T(8,128)(2,1)S(1)} %bitcast.16, bf16[4,720,720]{2,1,0:T(8,128)(2,1)S(1)} %copy-done.1, bf16[4,720,720]{2,1,0:T(8,128)(2,1)S(1)} %bitcast.18, f32[720,384]{1,0:T(8,128)S(1)} %get-tuple-element.47.refs_4_, ...), custom_call_target="tpu_custom_call" | custom-call | flops 1194393600 | bytes 3110400 | tf_op jit(solution)/shard_map/pallas_call | solution.py:344
  101.9 0.1 collective-permute-start.3
  102.0 1.9 %shard_map.91 = (f32[720,384]{1,0:T(8,128)S(1)}, f32[720,384]{1,0:T(8,128)S(1)}, bf16[720,384]{1,0:T(8,128)(2,1)S(1)}) custom-call(s32[1]{0:T(128)} %bitcast.9.refs_0_.at_ref, bf16[720,384]{1,0:T(8,128)(2,1)S(1)} %get-tuple-element.56.h_ref, bf16[4,720,720]{2,1,0:T(8,128)(2,1)S(1)} %bitcast.18), custom_call_target="tpu_custom_call" | custom-call | flops 1194393600 | bytes 3110400 | tf_op jit(solution)/shard_map/pallas_call | solution.py:352
  103.9 0.1 collective-permute-start.9
  104.0 1.9 %shard_map.87 = (f32[720,384]{1,0:T(8,128)S(1)}, bf16[720,384]{1,0:T(8,128)(2,1)S(1)}, f32[720,384]{1,0:T(8,128)S(1)}) custom-call(s32[1]{0:T(128)} %bitcast.9.refs_0_.at_ref, bf16[720,384]{1,0:T(8,128)(2,1)S(1)} %get-tuple-element.49.h_ref, bf16[4,720,720]{2,1,0:T(8,128)(2,1)S(1)} %bitcast.18), custom_call_target="tpu_custom_call" | custom-call | flops 1194393600 | bytes 3110400 | tf_op jit(solution)/shard_map/pallas_call | solution.py:352
  105.9 3.3 %collective-permute-start.5 = (bf16[720,384]{1,0:T(8,128)(2,1)S(1)}, bf16[720,384]{1,0:T(8,128)(2,1)S(1)}, u32[]{:S(2)}, u32[]{:S(2)}) collective-permute-start(bf16[720,384]{1,0:T(8,128)(2,1)S(1)} %get-tuple-element.53), channel_id=1, source_target_pairs={{0,96},{32,0},{64,32},{96,64},{1,97},{33,1},{65,33},{97,65},{2,98}... | collective-permute-start | bytes 1658888 | tf_op jit(solution)/shard_map/ppermute | solution.py:274
  109.2 0.0 collective-permute-done.10
  109.2 0.1 add_convert_fusion
  109.3 2.1 %collective-permute-start.11 = (bf16[720,384]{1,0:T(8,128)(2,1)S(1)}, bf16[720,384]{1,0:T(8,128)(2,1)S(1)}, u32[]{:S(2)}, u32[]{:S(2)}) collective-permute-start(bf16[720,384]{1,0:T(8,128)(2,1)S(1)} %add_convert_fusion), channel_id=1, source_target_pairs={{0,96},{32,0},{64,32},{96,64},{1,97},{33,1},{65,33},{97,65},{2,98}... | collective-permute-start | bytes 1658888 | tf_op jit(solution)/shard_map/ppermute | solution.py:274
  111.4 7.2 %collective-permute-done.3 = bf16[720,384]{1,0:T(8,128)(2,1)S(1)} collective-permute-done((bf16[720,384]{1,0:T(8,128)(2,1)S(1)}, bf16[720,384]{1,0:T(8,128)(2,1)S(1)}, u32[]{:S(2)}, u32[]{:S(2)}) %collective-permute-start.3) | collective-permute-done | bytes 552992 | tf_op jit(solution)/shard_map/ppermute | solution.py:274
  118.6 0.1 add_convert_fusion.1
  118.7 0.1 collective-permute-start.4
  118.8 1.0 shard_map.84
  119.8 10.6 %collective-permute-done.9.refs_7_ = bf16[720,384]{1,0:T(8,128)(2,1)S(1)} collective-permute-done((bf16[720,384]{1,0:T(8,128)(2,1)S(1)}, bf16[720,384]{1,0:T(8,128)(2,1)S(1)}, u32[]{:S(2)}, u32[]{:S(2)}) %collective-permute-start.9) | collective-permute-done | bytes 552992 | tf_op jit(solution)/shard_map/ppermute | solution.py:274
  130.4 0.0 collective-permute-done.5.refs_5_
  130.5 0.0 collective-permute-done.11.refs_8_
  130.5 6.7 %collective-permute-done.4.refs_4_ = bf16[720,384]{1,0:T(8,128)(2,1)S(1)} collective-permute-done((bf16[720,384]{1,0:T(8,128)(2,1)S(1)}, bf16[720,384]{1,0:T(8,128)(2,1)S(1)}, u32[]{:S(2)}, u32[]{:S(2)}) %collective-permute-start.4) | collective-permute-done | bytes 552992 | tf_op jit(solution)/shard_map/ppermute | solution.py:274
  137.2 3.2 %shard_map.92 = bf16[1024,1152]{1,0:T(8,128)(2,1)S(1)} custom-call(bf16[1024,768]{1,0:T(8,128)(2,1)S(1)} %get-tuple-element.40.refs_0_, bf16[1024,768]{1,0:T(8,128)(2,1)S(1)} %get-tuple-element.41.refs_1_, bf16[1024,768]{1,0:T(8,128)(2,1)S(1)} %get-tuple-element.42.refs_2_, f32[720,384]{1,0:T(8,128)S(1)} %get-tuple-element.50.refs_3_, ...), custom_call_target="tpu_custom_call" | custom-call | flops 1132462080 | bytes 1474560 | tf_op jit(solution)/shard_map/pallas_call | solution.py:382
  140.4 0.0 copy-start.2
  140.4 1.4 copy-done.2
  141.8 6.0 %all-to-all-start.1 = ((bf16[128,8,1152]{2,1,0:T(8,128)(2,1)}), bf16[128,8,1152]{2,1,0:T(8,128)(2,1)S(1)}, u32[]{:S(2)}, u32[]{:S(2)}) async-start(bf16[128,8,1152]{2,1,0:T(8,128)(2,1)} %bitcast.20), calls=%async_computation.1 | async-start | bytes 4718592 | tf_op jit(solution)/shard_map/all_to_all | solution.py:280
  147.8 0.0 copy-done.3
  147.8 0.0 copy-done.4
  147.8 0.5 shard_map.93.refs_1_
  148.3 32.7 %all-to-all-done.1 = bf16[128,8,1152]{2,1,0:T(8,128)(2,1)S(1)} async-done(((bf16[128,8,1152]{2,1,0:T(8,128)(2,1)}), bf16[128,8,1152]{2,1,0:T(8,128)(2,1)S(1)}, u32[]{:S(2)}, u32[]{:S(2)}) %all-to-all-start.1) | async-done | bytes 2359328 | tf_op jit(solution)/shard_map/all_to_all | solution.py:280
  181.0 1.4 shard_map.94
  (6 shorter events, 0.0 us)
Async XLA Ops:
  3.6 11.2 %copy-start.6 = (s32[32]{0:T(128)S(1)}, s32[32]{0:T(128)}, u32[]{:S(2)}) copy-start(s32[32]{0:T(128)} %param.12) | copy-start | bytes 388
  3.6 13.7 %copy-start.5 = (s32[32]{0:T(128)S(1)}, s32[32]{0:T(128)}, u32[]{:S(2)}) copy-start(s32[32]{0:T(128)} %param.11) | copy-start | bytes 388
  3.6 44.4 %all-to-all-start = ((bf16[128,8,1152]{2,1,0:T(8,128)(2,1)}), bf16[128,8,1152]{2,1,0:T(8,128)(2,1)S(1)}, u32[]{:S(2)}, u32[]{:S(2)}) async-start(bf16[128,8,1152]{2,1,0:T(8,128)(2,1)} %bitcast.26), calls=%async_computation | async-start | bytes 4718592 | tf_op jit(solution)/shard_map/all_to_all | solution.py:280
  50.2 40.1 %slice-start.2 = ((s8[4423680]{0:T(1024)(128)(4,1)}), s8[229376]{0:T(1024)(128)(4,1)S(1)}, s32[]{:S(2)}) async-start(s8[4423680]{0:T(1024)(128)(4,1)} %bitcast.17), calls=%async_computation.4 | async-start | bytes 458752
  52.7 15.1 %collective-permute-start.6 = (bf16[720,384]{1,0:T(8,128)(2,1)}, bf16[720,384]{1,0:T(8,128)(2,1)S(1)}, u32[]{:S(2)}, u32[]{:S(2)}) collective-permute-start(bf16[720,384]{1,0:T(8,128)(2,1)} %shard_map.88.refs_3_), channel_id=1, source_target_pairs={{0,32},{32,64},{64,96},{96,0},{1,33},{33,65},{65,97},{97,1},{2,34}... | collective-permute-start | bytes 1658888 | tf_op jit(solution)/shard_map/ppermute | solution.py:274
  53.2 15.6 %collective-permute-start.1 = (bf16[720,384]{1,0:T(8,128)(2,1)S(1)}, bf16[720,384]{1,0:T(8,128)(2,1)S(1)}, u32[]{:S(2)}, u32[]{:S(2)}) collective-permute-start(bf16[720,384]{1,0:T(8,128)(2,1)S(1)} %get-tuple-element.46.refs_3_), channel_id=1, source_target_pairs={{0,96},{32,0},{64,32},{96,64},{1,97},{33,1},{65,33},{97,65},{2,98}... | collective-permute-start | bytes 1658888 | tf_op jit(solution)/shard_map/ppermute | solution.py:274
  55.9 24.9 %collective-permute-start.7 = (bf16[720,384]{1,0:T(8,128)(2,1)}, bf16[720,384]{1,0:T(8,128)(2,1)}, u32[]{:S(2)}, u32[]{:S(2)}) collective-permute-start(bf16[720,384]{1,0:T(8,128)(2,1)} %shard_map.88.refs_3_), channel_id=1, source_target_pairs={{0,96},{32,0},{64,32},{96,64},{1,97},{33,1},{65,33},{97,65},{2,98}... | collective-permute-start | bytes 1658888 | tf_op jit(solution)/shard_map/ppermute | solution.py:274
  67.8 22.5 %collective-permute-start.8 = (bf16[720,384]{1,0:T(8,128)(2,1)S(1)}, bf16[720,384]{1,0:T(8,128)(2,1)S(1)}, u32[]{:S(2)}, u32[]{:S(2)}) collective-permute-start(bf16[720,384]{1,0:T(8,128)(2,1)S(1)} %collective-permute-done.6.refs_4_), channel_id=1, source_target_pairs={{0,32},{32,64},{64,96},{96,0},{1,33},{33,65},{65,97},{97,1},{2,34}... | collective-permute-start | bytes 1658888 | tf_op jit(solution)/shard_map/ppermute | solution.py:274
  67.8 28.5 %collective-permute-start = (bf16[720,384]{1,0:T(8,128)(2,1)S(1)}, bf16[720,384]{1,0:T(8,128)(2,1)S(1)}, u32[]{:S(2)}, u32[]{:S(2)}) collective-permute-start(bf16[720,384]{1,0:T(8,128)(2,1)S(1)} %get-tuple-element.46.refs_3_), channel_id=1, source_target_pairs={{0,32},{32,64},{64,96},{96,0},{1,33},{33,65},{65,97},{97,1},{2,34}... | collective-permute-start | bytes 1658888 | tf_op jit(solution)/shard_map/ppermute | solution.py:274
  68.8 31.1 %collective-permute-start.2 = (bf16[720,384]{1,0:T(8,128)(2,1)S(1)}, bf16[720,384]{1,0:T(8,128)(2,1)S(1)}, u32[]{:S(2)}, u32[]{:S(2)}) collective-permute-start(bf16[720,384]{1,0:T(8,128)(2,1)S(1)} %collective-permute-done.1.refs_5_), channel_id=1, source_target_pairs={{0,96},{32,0},{64,32},{96,64},{1,97},{33,1},{65,33},{97,65},{2,98}... | collective-permute-start | bytes 1658888 | tf_op jit(solution)/shard_map/ppermute | solution.py:274
  80.8 2.3 %copy-start = (bf16[4,720,720]{2,1,0:T(8,128)(2,1)S(1)}, bf16[4,720,720]{2,1,0:T(8,128)(2,1)}, u32[]{:S(2)}) copy-start(bf16[4,720,720]{2,1,0:T(8,128)(2,1)} %get-tuple-element.43.refs_1_) | copy-start | bytes 12441604
  83.1 2.3 %copy-start.1 = (bf16[4,720,720]{2,1,0:T(8,128)(2,1)S(1)}, bf16[4,720,720]{2,1,0:T(8,128)(2,1)}, u32[]{:S(2)}) copy-start(bf16[4,720,720]{2,1,0:T(8,128)(2,1)} %get-tuple-element.44.refs_2_) | copy-start | bytes 12441604
  85.3 5.0 %slice-start.3 = ((s8[4423680]{0:T(1024)(128)(4,1)}), s8[4194304]{0:T(1024)(128)(4,1)S(1)}, s32[]{:S(2)}) async-start(s8[4423680]{0:T(1024)(128)(4,1)} %bitcast.17), calls=%async_computation.5 | async-start | bytes 8388608
  90.3 6.0 %slice-start = ((s8[4423680]{0:T(1024)(128)(4,1)}), s8[4194304]{0:T(1024)(128)(4,1)S(1)}, s32[]{:S(2)}) async-start(s8[4423680]{0:T(1024)(128)(4,1)} %bitcast.15), calls=%async_computation.2 | async-start | bytes 8388608
  90.3 6.0 %slice-start.1 = ((s8[4423680]{0:T(1024)(128)(4,1)}), s8[229376]{0:T(1024)(128)(4,1)S(1)}, s32[]{:S(2)}) async-start(s8[4423680]{0:T(1024)(128)(4,1)} %bitcast.15), calls=%async_computation.3 | async-start | bytes 458752
  92.3 16.9 %collective-permute-start.10 = (bf16[720,384]{1,0:T(8,128)(2,1)S(1)}, bf16[720,384]{1,0:T(8,128)(2,1)S(1)}, u32[]{:S(2)}, u32[]{:S(2)}) collective-permute-start(bf16[720,384]{1,0:T(8,128)(2,1)S(1)} %get-tuple-element.60), channel_id=1, source_target_pairs={{0,96},{32,0},{64,32},{96,64},{1,97},{33,1},{65,33},{97,65},{2,98}... | collective-permute-start | bytes 1658888 | tf_op jit(solution)/shard_map/ppermute | solution.py:274
  101.9 16.7 %collective-permute-start.3 = (bf16[720,384]{1,0:T(8,128)(2,1)S(1)}, bf16[720,384]{1,0:T(8,128)(2,1)S(1)}, u32[]{:S(2)}, u32[]{:S(2)}) collective-permute-start(bf16[720,384]{1,0:T(8,128)(2,1)S(1)} %get-tuple-element.52), channel_id=1, source_target_pairs={{0,32},{32,64},{64,96},{96,0},{1,33},{33,65},{65,97},{97,1},{2,34}... | collective-permute-start | bytes 1658888 | tf_op jit(solution)/shard_map/ppermute | solution.py:274
  103.9 26.6 %collective-permute-start.9 = (bf16[720,384]{1,0:T(8,128)(2,1)S(1)}, bf16[720,384]{1,0:T(8,128)(2,1)S(1)}, u32[]{:S(2)}, u32[]{:S(2)}) collective-permute-start(bf16[720,384]{1,0:T(8,128)(2,1)S(1)} %get-tuple-element.58), channel_id=1, source_target_pairs={{0,32},{32,64},{64,96},{96,0},{1,33},{33,65},{65,97},{97,1},{2,34}... | collective-permute-start | bytes 1658888 | tf_op jit(solution)/shard_map/ppermute | solution.py:274
  105.9 24.6 %collective-permute-start.5 = (bf16[720,384]{1,0:T(8,128)(2,1)S(1)}, bf16[720,384]{1,0:T(8,128)(2,1)S(1)}, u32[]{:S(2)}, u32[]{:S(2)}) collective-permute-start(bf16[720,384]{1,0:T(8,128)(2,1)S(1)} %get-tuple-element.53), channel_id=1, source_target_pairs={{0,96},{32,0},{64,32},{96,64},{1,97},{33,1},{65,33},{97,65},{2,98}... | collective-permute-start | bytes 1658888 | tf_op jit(solution)/shard_map/ppermute | solution.py:274
  109.3 21.1 %collective-permute-start.11 = (bf16[720,384]{1,0:T(8,128)(2,1)S(1)}, bf16[720,384]{1,0:T(8,128)(2,1)S(1)}, u32[]{:S(2)}, u32[]{:S(2)}) collective-permute-start(bf16[720,384]{1,0:T(8,128)(2,1)S(1)} %add_convert_fusion), channel_id=1, source_target_pairs={{0,96},{32,0},{64,32},{96,64},{1,97},{33,1},{65,33},{97,65},{2,98}... | collective-permute-start | bytes 1658888 | tf_op jit(solution)/shard_map/ppermute | solution.py:274
  118.7 18.5 %collective-permute-start.4 = (bf16[720,384]{1,0:T(8,128)(2,1)S(1)}, bf16[720,384]{1,0:T(8,128)(2,1)S(1)}, u32[]{:S(2)}, u32[]{:S(2)}) collective-permute-start(bf16[720,384]{1,0:T(8,128)(2,1)S(1)} %add_convert_fusion.1), channel_id=1, source_target_pairs={{0,32},{32,64},{64,96},{96,0},{1,33},{33,65},{65,97},{97,1},{2,34}... | collective-permute-start | bytes 1658888 | tf_op jit(solution)/shard_map/ppermute | solution.py:274
  140.4 1.4 copy-start.2
  141.8 6.0 %copy-start.3 = (s32[32,4]{0,1:T(4,128)S(1)}, s32[32,4]{0,1:T(4,128)}, u32[]{:S(2)}) copy-start(s32[32,4]{0,1:T(4,128)} %param.9) | copy-start | bytes 1540
  141.8 6.0 %copy-start.4 = (f32[32,4]{0,1:T(4,128)S(1)}, f32[32,4]{0,1:T(4,128)}, u32[]{:S(2)}) copy-start(f32[32,4]{0,1:T(4,128)} %param.10) | copy-start | bytes 1540
  141.8 39.2 %all-to-all-start.1 = ((bf16[128,8,1152]{2,1,0:T(8,128)(2,1)}), bf16[128,8,1152]{2,1,0:T(8,128)(2,1)S(1)}, u32[]{:S(2)}, u32[]{:S(2)}) async-start(bf16[128,8,1152]{2,1,0:T(8,128)(2,1)} %bitcast.20), calls=%async_computation.1 | async-start | bytes 4718592 | tf_op jit(solution)/shard_map/all_to_all | solution.py:280

commit v5 on v4

--- a/solution.py
+++ b/solution.py
@@ -359,22 +359,21 @@
     def add(mine, came):
         return (mine + came.astype(F32)).astype(BF)
 
-    above_a = left(own_a)
+    below_a, above_a = right(own_a), left(own_a)
+    above_b = left(own_b)
+    far_a = right(below_a)
     below_b = right(own_b)
-    above_b = left(own_b)
-    below_a = right(own_a)
-    far_a = left(above_a)
-    far_b = right(below_b)
+    far_b = left(above_b)
     sums_a = mid((own_a, below_a, above_a), (0, before, after))
-    sums_b = mid((own_b, below_b, above_b), (0, before, after))
     hidden_a, share_a = far(sums_a, (far_a,), (across,))
     crossed_a = right(share_a)
-    hidden_b, share_b = far(sums_b, (far_b,), (across,))
+    mine_a, left_a, right_a = near(hidden_a, (F32, BF, F32))
+    from_right_a = left(left_a)
+    sums_b = mid((own_b, above_b), (0, after))
+    hidden_b, share_b = far(sums_b, (below_b, far_b), (before, across))
     crossed_b = left(share_b)
     mine_b, left_b, right_b = near(hidden_b, (F32, F32, BF))
     from_left_b = right(right_b)
-    mine_a, left_a, right_a = near(hidden_a, (F32, BF, F32))
-    from_right_a = left(left_a)
     added_a, added_b = add(right_a, crossed_a), add(left_b, crossed_b)
     from_left_a = right(added_a)
     from_right_b = left(added_b)

time: 183 us -> 183 us (level)
    all_to_all x2, starting transfers between devices: 17.1 us -> 19.4 us  [exchange(): lax.all_to_all(blocks, ATTN_EXPERT, split_axis=0, concat_axis=0, tiled=True)]
  transfers between devices with their start and end apart: 14 -> 14, of which waited for: 8 -> 10; matrix products, arithmetic and copies ran while one was open for 1% -> 1% of each run, Pallas kernels for 17% -> 17%
where the time goes in v5:
time: 183 us
  waiting for transfers between devices  92.7 us (51%)
  Pallas kernels  43.9 us (24%)
  starting transfers between devices  35.1 us (19%)
  local copies, waits for them, and re-layouts  7.19 us (4%)
  between operations  3.32 us (2%)
    all_to_all x2, waiting for transfers between devices, exchange(): lax.all_to_all(blocks, ATTN_EXPERT, split_axis=0, concat_axis=0, tiled=True)  48.2 us
    ppermute x12, waiting for transfers between devices, shifted(): return lambda array: lax.ppermute(array, 'attn', pairs)  44.5 us
    all_to_all x2, starting transfers between devices, exchange(): lax.all_to_all(blocks, ATTN_EXPERT, split_axis=0, concat_axis=0, tiled=True)  19.4 us
    ppermute x12, starting transfers between devices, shifted(): return lambda array: lax.ppermute(array, 'attn', pairs)  15.7 us
    pallas_call x1, Pallas kernels, on_device(): pl.pallas_call(relay_kernel, grid=(pl.cdiv(units, step),), out_shape=(rel...  13.3 us
    pallas_call x2, Pallas kernels, mid(): run(lambda *refs: mid_kernel(ahead, *refs), [SMEM] + [VMEM] * (2 + len(bl...  7.45 us
    unnamed x22, local copies, waits for them, and re-layouts  5.95 us
    pallas_call x2, Pallas kernels, far(): run(lambda *refs: far_kernel(ahead, *refs), [SMEM] + [VMEM] * (5 + len(bl...  5.11 us
  transfers between devices with their start and end apart: 14, of which 10 were waited for; matrix products, arithmetic and copies ran while one was open for 1% of the time, Pallas kernels for 17%

profile of v5, /device:TPU:0, one launch (start us, length us, event | category | flops | bytes accessed | tf_op | source)
XLA Modules:
  0.0 182.6 jit_solution(14455657030794602621)
XLA Ops:
  0.0 3.6 %shard_map.82 = (bf16[1024,1152]{1,0:T(8,128)(2,1)}, f32[8,128]{1,0:T(8,128)}) custom-call(bf16[32,2880]{1,0:T(8,128)(2,1)} %refs_0_.1, s32[4,32]{1,0:T(4,128)} %bitcast.23), custom_call_target="tpu_custom_call" | custom-call | flops 47185920 | bytes 1474560 | tf_op jit(solution)/shard_map/pallas_call | solution.py:286
  3.6 0.0 copy-start.6
  3.6 0.0 copy-start.5
  3.6 11.2 %all-to-all-start = ((bf16[128,8,1152]{2,1,0:T(8,128)(2,1)}), bf16[128,8,1152]{2,1,0:T(8,128)(2,1)S(1)}, u32[]{:S(2)}, u32[]{:S(2)}) async-start(bf16[128,8,1152]{2,1,0:T(8,128)(2,1)} %bitcast.26), calls=%async_computation | async-start | bytes 4718592 | tf_op jit(solution)/shard_map/all_to_all | solution.py:280
  14.8 0.0 copy-done.6
  14.8 0.6 dynamic_slice.9
  17.3 0.0 copy-done.5
  17.3 0.6 fusion
  19.2 13.3 %relay.1 = (bf16[4,720,720]{2,1,0:T(8,128)(2,1)}, bf16[4,720,720]{2,1,0:T(8,128)(2,1)}, bf16[4,720,720]{2,1,0:T(8,128)(2,1)}) custom-call(f32[8,128]{1,0:T(8,128)} %get-tuple-element.34.seen_ref, bf16[720,2880]{1,0:T(8,128)(2,1)} %bitcast.27, bf16[720,2880]{1,0:T(8,128)(2,1)} %bitcast.28, bf16[720,2880]{1,0:T(8,128)(2,1)} %bitcast.29), custom_call_target="tpu_custom_call" | custom-call | flops 4777574400 | bytes 24883200 | tf_op jit(solution)/shard_map/relay/pallas_call | solution.py:298
  32.4 15.6 %all-to-all-done = bf16[128,8,1152]{2,1,0:T(8,128)(2,1)S(1)} async-done(((bf16[128,8,1152]{2,1,0:T(8,128)(2,1)}), bf16[128,8,1152]{2,1,0:T(8,128)(2,1)S(1)}, u32[]{:S(2)}, u32[]{:S(2)}) %all-to-all-start) | async-done | bytes 2359328 | tf_op jit(solution)/shard_map/all_to_all | solution.py:280
  48.0 2.2 %shard_map.83 = (f32[8,1024]{1,0:T(8,128)S(1)}, bf16[720,384]{1,0:T(8,128)(2,1)S(1)}) custom-call(bf16[1024,1152]{1,0:T(8,128)(2,1)S(1)} %bitcast.21, s32[1]{0:T(128)S(6)} %add.27.refs_1_), custom_call_target="tpu_custom_call" | custom-call | flops 1132462080 | bytes 1474560 | tf_op jit(solution)/shard_map/pallas_call | solution.py:319
  50.2 0.0 slice-start.2
  50.2 2.5 %shard_map.88.refs_3_ = bf16[720,384]{1,0:T(8,128)(2,1)} custom-call(bf16[1024,1152]{1,0:T(8,128)(2,1)S(1)} %bitcast.22, f32[8,1024]{1,0:T(8,128)S(1)} %get-tuple-element.39.row_ref.refs_1_), custom_call_target="tpu_custom_call" | custom-call | flops 1132462080 | bytes 1474560 | tf_op jit(solution)/shard_map/pallas_call | solution.py:325
  52.7 1.1 collective-permute-start.6
  53.8 0.9 collective-permute-start
  54.7 0.5 collective-permute-start.7
  55.3 11.4 %collective-permute-done.6.refs_4_ = bf16[720,384]{1,0:T(8,128)(2,1)} collective-permute-done((bf16[720,384]{1,0:T(8,128)(2,1)}, bf16[720,384]{1,0:T(8,128)(2,1)}, u32[]{:S(2)}, u32[]{:S(2)}) %collective-permute-start.6) | collective-permute-done | bytes 552992 | tf_op jit(solution)/shard_map/ppermute | solution.py:274
  66.7 2.4 %collective-permute-start.8 = (bf16[720,384]{1,0:T(8,128)(2,1)}, bf16[720,384]{1,0:T(8,128)(2,1)S(1)}, u32[]{:S(2)}, u32[]{:S(2)}) collective-permute-start(bf16[720,384]{1,0:T(8,128)(2,1)} %collective-permute-done.6.refs_4_), channel_id=1, source_target_pairs={{0,96},{32,0},{64,32},{96,64},{1,97},{33,1},{65,33},{97,65},{2,98}... | collective-permute-start | bytes 1658888 | tf_op jit(solution)/shard_map/ppermute | solution.py:274
  69.1 0.0 collective-permute-start.1
  69.2 1.3 collective-permute-done.refs_4_
  70.4 0.7 collective-permute-start.2
  71.2 0.0 copy-start
  71.2 2.3 %copy-done = bf16[4,720,720]{2,1,0:T(8,128)(2,1)S(1)} copy-done((bf16[4,720,720]{2,1,0:T(8,128)(2,1)S(1)}, bf16[4,720,720]{2,1,0:T(8,128)(2,1)}, u32[]{:S(2)}) %copy-start) | copy-done | bytes 4147224
  73.4 0.0 copy-start.1
  73.4 2.3 %copy-done.1 = bf16[4,720,720]{2,1,0:T(8,128)(2,1)S(1)} copy-done((bf16[4,720,720]{2,1,0:T(8,128)(2,1)S(1)}, bf16[4,720,720]{2,1,0:T(8,128)(2,1)}, u32[]{:S(2)}) %copy-start.1) | copy-done | bytes 4147224
  75.7 0.0 slice-start.3
  75.7 3.8 %shard_map.89 = (f32[720,384]{1,0:T(8,128)S(1)}, f32[720,384]{1,0:T(8,128)S(1)}) custom-call(s32[1]{0:T(128)} %bitcast.9.refs_0_.at_ref, bf16[4,720,720]{2,1,0:T(8,128)(2,1)S(1)} %copy-done, bf16[4,720,720]{2,1,0:T(8,128)(2,1)S(1)} %copy-done.1, bf16[720,384]{1,0:T(8,128)(2,1)} %shard_map.88.refs_3_, bf16[720,384]{1,0:T(8,128)(2,1)} %collective-permute-done.6.refs_4_), custom_call_target="tpu_custom_call" | custom-call | flops 1592524800 | bytes 4147200 | tf_op jit(solution)/shard_map/pallas_call | solution.py:335
  79.5 2.8 %collective-permute-done.7.refs_6_ = bf16[720,384]{1,0:T(8,128)(2,1)S(1)} collective-permute-done((bf16[720,384]{1,0:T(8,128)(2,1)}, bf16[720,384]{1,0:T(8,128)(2,1)S(1)}, u32[]{:S(2)}, u32[]{:S(2)}) %collective-permute-start.7) | collective-permute-done | bytes 552992 | tf_op jit(solution)/shard_map/ppermute | solution.py:274
  82.3 0.1 collective-permute-done.8.refs_7_
  82.4 0.0 slice-done.2
  82.4 0.0 slice-done.3
  82.4 3.2 %shard_map.90 = (bf16[720,384]{1,0:T(8,128)(2,1)S(1)}, bf16[720,384]{1,0:T(8,128)(2,1)S(1)}) custom-call(s32[1]{0:T(128)} %bitcast.9.refs_0_.at_ref, bf16[4,720,720]{2,1,0:T(8,128)(2,1)S(1)} %copy-done, bf16[4,720,720]{2,1,0:T(8,128)(2,1)S(1)} %copy-done.1, bf16[4,720,720]{2,1,0:T(8,128)(2,1)S(1)} %bitcast.18, f32[720,384]{1,0:T(8,128)S(1)} %get-tuple-element.54.refs_4_, ...), custom_call_target="tpu_custom_call" | custom-call | flops 1990656000 | bytes 5184000 | tf_op jit(solution)/shard_map/pallas_call | solution.py:344
  85.6 3.6 %collective-permute-start.10 = (bf16[720,384]{1,0:T(8,128)(2,1)S(1)}, bf16[720,384]{1,0:T(8,128)(2,1)S(1)}, u32[]{:S(2)}, u32[]{:S(2)}) collective-permute-start(bf16[720,384]{1,0:T(8,128)(2,1)S(1)} %get-tuple-element.60), channel_id=1, source_target_pairs={{0,96},{32,0},{64,32},{96,64},{1,97},{33,1},{65,33},{97,65},{2,98}... | collective-permute-start | bytes 1658888 | tf_op jit(solution)/shard_map/ppermute | solution.py:274
  89.2 5.0 %collective-permute-done.1.refs_5_ = bf16[720,384]{1,0:T(8,128)(2,1)S(1)} collective-permute-done((bf16[720,384]{1,0:T(8,128)(2,1)S(1)}, bf16[720,384]{1,0:T(8,128)(2,1)S(1)}, u32[]{:S(2)}, u32[]{:S(2)}) %collective-permute-start.1) | collective-permute-done | bytes 552992 | tf_op jit(solution)/shard_map/ppermute | solution.py:274
  94.2 0.0 slice-done
  94.2 0.0 slice-done.1
  94.2 3.6 %shard_map.85 = (f32[720,384]{1,0:T(8,128)S(1)}, f32[720,384]{1,0:T(8,128)S(1)}) custom-call(s32[1]{0:T(128)} %bitcast.9.refs_0_.at_ref, bf16[4,720,720]{2,1,0:T(8,128)(2,1)S(1)} %bitcast.16, bf16[4,720,720]{2,1,0:T(8,128)(2,1)S(1)} %copy-done.1, bf16[720,384]{1,0:T(8,128)(2,1)S(1)} %get-tuple-element.46.refs_3_, ...), custom_call_target="tpu_custom_call" | custom-call | flops 2388787200 | bytes 6220800 | tf_op jit(solution)/shard_map/pallas_call | solution.py:335
  97.8 0.0 collective-permute-done.2.refs_6_
  97.8 1.9 %shard_map.86 = (bf16[720,384]{1,0:T(8,128)(2,1)S(1)}, bf16[720,384]{1,0:T(8,128)(2,1)S(1)}) custom-call(s32[1]{0:T(128)} %bitcast.9.refs_0_.at_ref, bf16[4,720,720]{2,1,0:T(8,128)(2,1)S(1)} %bitcast.16, bf16[4,720,720]{2,1,0:T(8,128)(2,1)S(1)} %copy-done.1, bf16[4,720,720]{2,1,0:T(8,128)(2,1)S(1)} %bitcast.18, f32[720,384]{1,0:T(8,128)S(1)} %get-tuple-element.47.refs_4_, ...), custom_call_target="tpu_custom_call" | custom-call | flops 1194393600 | bytes 3110400 | tf_op jit(solution)/shard_map/pallas_call | solution.py:344
  99.8 0.6 collective-permute-start.3
  100.4 1.9 %shard_map.91 = (f32[720,384]{1,0:T(8,128)S(1)}, f32[720,384]{1,0:T(8,128)S(1)}, bf16[720,384]{1,0:T(8,128)(2,1)S(1)}) custom-call(s32[1]{0:T(128)} %bitcast.9.refs_0_.at_ref, bf16[720,384]{1,0:T(8,128)(2,1)S(1)} %get-tuple-element.56.h_ref, bf16[4,720,720]{2,1,0:T(8,128)(2,1)S(1)} %bitcast.18), custom_call_target="tpu_custom_call" | custom-call | flops 1194393600 | bytes 3110400 | tf_op jit(solution)/shard_map/pallas_call | solution.py:352
  102.3 1.4 collective-permute-start.9
  103.6 1.9 %shard_map.87 = (f32[720,384]{1,0:T(8,128)S(1)}, bf16[720,384]{1,0:T(8,128)(2,1)S(1)}, f32[720,384]{1,0:T(8,128)S(1)}) custom-call(s32[1]{0:T(128)} %bitcast.9.refs_0_.at_ref, bf16[720,384]{1,0:T(8,128)(2,1)S(1)} %get-tuple-element.49.h_ref, bf16[4,720,720]{2,1,0:T(8,128)(2,1)S(1)} %bitcast.18), custom_call_target="tpu_custom_call" | custom-call | flops 1194393600 | bytes 3110400 | tf_op jit(solution)/shard_map/pallas_call | solution.py:352
  105.5 2.0 %collective-permute-start.5 = (bf16[720,384]{1,0:T(8,128)(2,1)S(1)}, bf16[720,384]{1,0:T(8,128)(2,1)S(1)}, u32[]{:S(2)}, u32[]{:S(2)}) collective-permute-start(bf16[720,384]{1,0:T(8,128)(2,1)S(1)} %get-tuple-element.53), channel_id=1, source_target_pairs={{0,96},{32,0},{64,32},{96,64},{1,97},{33,1},{65,33},{97,65},{2,98}... | collective-permute-start | bytes 1658888 | tf_op jit(solution)/shard_map/ppermute | solution.py:274
  107.5 0.0 collective-permute-done.10
  107.6 0.1 add_convert_fusion
  107.7 2.2 %collective-permute-start.11 = (bf16[720,384]{1,0:T(8,128)(2,1)S(1)}, bf16[720,384]{1,0:T(8,128)(2,1)S(1)}, u32[]{:S(2)}, u32[]{:S(2)}) collective-permute-start(bf16[720,384]{1,0:T(8,128)(2,1)S(1)} %add_convert_fusion), channel_id=1, source_target_pairs={{0,96},{32,0},{64,32},{96,64},{1,97},{33,1},{65,33},{97,65},{2,98}... | collective-permute-start | bytes 1658888 | tf_op jit(solution)/shard_map/ppermute | solution.py:274
  109.9 7.0 %collective-permute-done.3 = bf16[720,384]{1,0:T(8,128)(2,1)S(1)} collective-permute-done((bf16[720,384]{1,0:T(8,128)(2,1)S(1)}, bf16[720,384]{1,0:T(8,128)(2,1)S(1)}, u32[]{:S(2)}, u32[]{:S(2)}) %collective-permute-start.3) | collective-permute-done | bytes 552992 | tf_op jit(solution)/shard_map/ppermute | solution.py:274
  116.9 0.1 add_convert_fusion.1
  117.0 0.1 collective-permute-start.4
  117.1 1.0 shard_map.84
  118.1 10.6 %collective-permute-done.9.refs_7_ = bf16[720,384]{1,0:T(8,128)(2,1)S(1)} collective-permute-done((bf16[720,384]{1,0:T(8,128)(2,1)S(1)}, bf16[720,384]{1,0:T(8,128)(2,1)S(1)}, u32[]{:S(2)}, u32[]{:S(2)}) %collective-permute-start.9) | collective-permute-done | bytes 552992 | tf_op jit(solution)/shard_map/ppermute | solution.py:274
  128.7 0.0 collective-permute-done.5.refs_5_
  128.7 0.0 collective-permute-done.11.refs_8_
  128.8 6.3 %collective-permute-done.4.refs_4_ = bf16[720,384]{1,0:T(8,128)(2,1)S(1)} collective-permute-done((bf16[720,384]{1,0:T(8,128)(2,1)S(1)}, bf16[720,384]{1,0:T(8,128)(2,1)S(1)}, u32[]{:S(2)}, u32[]{:S(2)}) %collective-permute-start.4) | collective-permute-done | bytes 552992 | tf_op jit(solution)/shard_map/ppermute | solution.py:274
  135.1 3.2 %shard_map.92 = bf16[1024,1152]{1,0:T(8,128)(2,1)S(1)} custom-call(bf16[1024,768]{1,0:T(8,128)(2,1)S(1)} %get-tuple-element.40.refs_0_, bf16[1024,768]{1,0:T(8,128)(2,1)S(1)} %get-tuple-element.41.refs_1_, bf16[1024,768]{1,0:T(8,128)(2,1)S(1)} %get-tuple-element.42.refs_2_, f32[720,384]{1,0:T(8,128)S(1)} %get-tuple-element.50.refs_3_, ...), custom_call_target="tpu_custom_call" | custom-call | flops 1132462080 | bytes 1474560 | tf_op jit(solution)/shard_map/pallas_call | solution.py:381
  138.3 0.0 copy-start.2
  138.3 1.4 copy-done.2
  139.7 8.3 %all-to-all-start.1 = ((bf16[128,8,1152]{2,1,0:T(8,128)(2,1)}), bf16[128,8,1152]{2,1,0:T(8,128)(2,1)S(1)}, u32[]{:S(2)}, u32[]{:S(2)}) async-start(bf16[128,8,1152]{2,1,0:T(8,128)(2,1)} %bitcast.20), calls=%async_computation.1 | async-start | bytes 4718592 | tf_op jit(solution)/shard_map/all_to_all | solution.py:280
  148.0 0.0 copy-done.3
  148.0 0.0 copy-done.4
  148.0 0.5 shard_map.93.refs_1_
  148.5 32.7 %all-to-all-done.1 = bf16[128,8,1152]{2,1,0:T(8,128)(2,1)S(1)} async-done(((bf16[128,8,1152]{2,1,0:T(8,128)(2,1)}), bf16[128,8,1152]{2,1,0:T(8,128)(2,1)S(1)}, u32[]{:S(2)}, u32[]{:S(2)}) %all-to-all-start.1) | async-done | bytes 2359328 | tf_op jit(solution)/shard_map/all_to_all | solution.py:280
  181.2 1.4 shard_map.94
  (6 shorter events, 0.0 us)
Async XLA Ops:
  3.6 11.2 %copy-start.6 = (s32[32]{0:T(128)S(1)}, s32[32]{0:T(128)}, u32[]{:S(2)}) copy-start(s32[32]{0:T(128)} %param.12) | copy-start | bytes 388
  3.6 13.7 %copy-start.5 = (s32[32]{0:T(128)S(1)}, s32[32]{0:T(128)}, u32[]{:S(2)}) copy-start(s32[32]{0:T(128)} %param.11) | copy-start | bytes 388
  3.6 44.4 %all-to-all-start = ((bf16[128,8,1152]{2,1,0:T(8,128)(2,1)}), bf16[128,8,1152]{2,1,0:T(8,128)(2,1)S(1)}, u32[]{:S(2)}, u32[]{:S(2)}) async-start(bf16[128,8,1152]{2,1,0:T(8,128)(2,1)} %bitcast.26), calls=%async_computation | async-start | bytes 4718592 | tf_op jit(solution)/shard_map/all_to_all | solution.py:280
  50.2 32.2 %slice-start.2 = ((s8[4423680]{0:T(1024)(128)(4,1)}), s8[229376]{0:T(1024)(128)(4,1)S(1)}, s32[]{:S(2)}) async-start(s8[4423680]{0:T(1024)(128)(4,1)} %bitcast.17), calls=%async_computation.4 | async-start | bytes 458752
  52.7 14.0 %collective-permute-start.6 = (bf16[720,384]{1,0:T(8,128)(2,1)}, bf16[720,384]{1,0:T(8,128)(2,1)}, u32[]{:S(2)}, u32[]{:S(2)}) collective-permute-start(bf16[720,384]{1,0:T(8,128)(2,1)} %shard_map.88.refs_3_), channel_id=1, source_target_pairs={{0,96},{32,0},{64,32},{96,64},{1,97},{33,1},{65,33},{97,65},{2,98}... | collective-permute-start | bytes 1658888 | tf_op jit(solution)/shard_map/ppermute | solution.py:274
  53.8 16.6 %collective-permute-start = (bf16[720,384]{1,0:T(8,128)(2,1)S(1)}, bf16[720,384]{1,0:T(8,128)(2,1)S(1)}, u32[]{:S(2)}, u32[]{:S(2)}) collective-permute-start(bf16[720,384]{1,0:T(8,128)(2,1)S(1)} %get-tuple-element.46.refs_3_), channel_id=1, source_target_pairs={{0,32},{32,64},{64,96},{96,0},{1,33},{33,65},{65,97},{97,1},{2,34}... | collective-permute-start | bytes 1658888 | tf_op jit(solution)/shard_map/ppermute | solution.py:274
  54.7 27.6 %collective-permute-start.7 = (bf16[720,384]{1,0:T(8,128)(2,1)}, bf16[720,384]{1,0:T(8,128)(2,1)S(1)}, u32[]{:S(2)}, u32[]{:S(2)}) collective-permute-start(bf16[720,384]{1,0:T(8,128)(2,1)} %shard_map.88.refs_3_), channel_id=1, source_target_pairs={{0,32},{32,64},{64,96},{96,0},{1,33},{33,65},{65,97},{97,1},{2,34}... | collective-permute-start | bytes 1658888 | tf_op jit(solution)/shard_map/ppermute | solution.py:274
  66.7 15.7 %collective-permute-start.8 = (bf16[720,384]{1,0:T(8,128)(2,1)}, bf16[720,384]{1,0:T(8,128)(2,1)S(1)}, u32[]{:S(2)}, u32[]{:S(2)}) collective-permute-start(bf16[720,384]{1,0:T(8,128)(2,1)} %collective-permute-done.6.refs_4_), channel_id=1, source_target_pairs={{0,96},{32,0},{64,32},{96,64},{1,97},{33,1},{65,33},{97,65},{2,98}... | collective-permute-start | bytes 1658888 | tf_op jit(solution)/shard_map/ppermute | solution.py:274
  69.1 25.0 %collective-permute-start.1 = (bf16[720,384]{1,0:T(8,128)(2,1)S(1)}, bf16[720,384]{1,0:T(8,128)(2,1)S(1)}, u32[]{:S(2)}, u32[]{:S(2)}) collective-permute-start(bf16[720,384]{1,0:T(8,128)(2,1)S(1)} %get-tuple-element.46.refs_3_), channel_id=1, source_target_pairs={{0,96},{32,0},{64,32},{96,64},{1,97},{33,1},{65,33},{97,65},{2,98}... | collective-permute-start | bytes 1658888 | tf_op jit(solution)/shard_map/ppermute | solution.py:274
  70.4 27.4 %collective-permute-start.2 = (bf16[720,384]{1,0:T(8,128)(2,1)S(1)}, bf16[720,384]{1,0:T(8,128)(2,1)S(1)}, u32[]{:S(2)}, u32[]{:S(2)}) collective-permute-start(bf16[720,384]{1,0:T(8,128)(2,1)S(1)} %collective-permute-done.refs_4_), channel_id=1, source_target_pairs={{0,32},{32,64},{64,96},{96,0},{1,33},{33,65},{65,97},{97,1},{2,34}... | collective-permute-start | bytes 1658888 | tf_op jit(solution)/shard_map/ppermute | solution.py:274
  71.2 2.3 %copy-start = (bf16[4,720,720]{2,1,0:T(8,128)(2,1)S(1)}, bf16[4,720,720]{2,1,0:T(8,128)(2,1)}, u32[]{:S(2)}) copy-start(bf16[4,720,720]{2,1,0:T(8,128)(2,1)} %get-tuple-element.43.refs_1_) | copy-start | bytes 12441604
  73.4 2.3 %copy-start.1 = (bf16[4,720,720]{2,1,0:T(8,128)(2,1)S(1)}, bf16[4,720,720]{2,1,0:T(8,128)(2,1)}, u32[]{:S(2)}) copy-start(bf16[4,720,720]{2,1,0:T(8,128)(2,1)} %get-tuple-element.44.refs_2_) | copy-start | bytes 12441604
  75.7 6.7 %slice-start.3 = ((s8[4423680]{0:T(1024)(128)(4,1)}), s8[4194304]{0:T(1024)(128)(4,1)S(1)}, s32[]{:S(2)}) async-start(s8[4423680]{0:T(1024)(128)(4,1)} %bitcast.17), calls=%async_computation.5 | async-start | bytes 8388608
  82.4 11.8 %slice-start = ((s8[4423680]{0:T(1024)(128)(4,1)}), s8[4194304]{0:T(1024)(128)(4,1)S(1)}, s32[]{:S(2)}) async-start(s8[4423680]{0:T(1024)(128)(4,1)} %bitcast.15), calls=%async_computation.2 | async-start | bytes 8388608
  82.4 11.8 %slice-start.1 = ((s8[4423680]{0:T(1024)(128)(4,1)}), s8[229376]{0:T(1024)(128)(4,1)S(1)}, s32[]{:S(2)}) async-start(s8[4423680]{0:T(1024)(128)(4,1)} %bitcast.15), calls=%async_computation.3 | async-start | bytes 458752
  85.6 22.0 %collective-permute-start.10 = (bf16[720,384]{1,0:T(8,128)(2,1)S(1)}, bf16[720,384]{1,0:T(8,128)(2,1)S(1)}, u32[]{:S(2)}, u32[]{:S(2)}) collective-permute-start(bf16[720,384]{1,0:T(8,128)(2,1)S(1)} %get-tuple-element.60), channel_id=1, source_target_pairs={{0,96},{32,0},{64,32},{96,64},{1,97},{33,1},{65,33},{97,65},{2,98}... | collective-permute-start | bytes 1658888 | tf_op jit(solution)/shard_map/ppermute | solution.py:274
  99.8 17.1 %collective-permute-start.3 = (bf16[720,384]{1,0:T(8,128)(2,1)S(1)}, bf16[720,384]{1,0:T(8,128)(2,1)S(1)}, u32[]{:S(2)}, u32[]{:S(2)}) collective-permute-start(bf16[720,384]{1,0:T(8,128)(2,1)S(1)} %get-tuple-element.52), channel_id=1, source_target_pairs={{0,32},{32,64},{64,96},{96,0},{1,33},{33,65},{65,97},{97,1},{2,34}... | collective-permute-start | bytes 1658888 | tf_op jit(solution)/shard_map/ppermute | solution.py:274
  102.3 26.5 %collective-permute-start.9 = (bf16[720,384]{1,0:T(8,128)(2,1)S(1)}, bf16[720,384]{1,0:T(8,128)(2,1)S(1)}, u32[]{:S(2)}, u32[]{:S(2)}) collective-permute-start(bf16[720,384]{1,0:T(8,128)(2,1)S(1)} %get-tuple-element.58), channel_id=1, source_target_pairs={{0,32},{32,64},{64,96},{96,0},{1,33},{33,65},{65,97},{97,1},{2,34}... | collective-permute-start | bytes 1658888 | tf_op jit(solution)/shard_map/ppermute | solution.py:274
  105.5 23.2 %collective-permute-start.5 = (bf16[720,384]{1,0:T(8,128)(2,1)S(1)}, bf16[720,384]{1,0:T(8,128)(2,1)S(1)}, u32[]{:S(2)}, u32[]{:S(2)}) collective-permute-start(bf16[720,384]{1,0:T(8,128)(2,1)S(1)} %get-tuple-element.53), channel_id=1, source_target_pairs={{0,96},{32,0},{64,32},{96,64},{1,97},{33,1},{65,33},{97,65},{2,98}... | collective-permute-start | bytes 1658888 | tf_op jit(solution)/shard_map/ppermute | solution.py:274
  107.7 21.0 %collective-permute-start.11 = (bf16[720,384]{1,0:T(8,128)(2,1)S(1)}, bf16[720,384]{1,0:T(8,128)(2,1)S(1)}, u32[]{:S(2)}, u32[]{:S(2)}) collective-permute-start(bf16[720,384]{1,0:T(8,128)(2,1)S(1)} %add_convert_fusion), channel_id=1, source_target_pairs={{0,96},{32,0},{64,32},{96,64},{1,97},{33,1},{65,33},{97,65},{2,98}... | collective-permute-start | bytes 1658888 | tf_op jit(solution)/shard_map/ppermute | solution.py:274
  117.0 18.1 %collective-permute-start.4 = (bf16[720,384]{1,0:T(8,128)(2,1)S(1)}, bf16[720,384]{1,0:T(8,128)(2,1)S(1)}, u32[]{:S(2)}, u32[]{:S(2)}) collective-permute-start(bf16[720,384]{1,0:T(8,128)(2,1)S(1)} %add_convert_fusion.1), channel_id=1, source_target_pairs={{0,32},{32,64},{64,96},{96,0},{1,33},{33,65},{65,97},{97,1},{2,34}... | collective-permute-start | bytes 1658888 | tf_op jit(solution)/shard_map/ppermute | solution.py:274
  138.3 1.4 copy-start.2
  139.7 8.3 %copy-start.3 = (s32[32,4]{0,1:T(4,128)S(1)}, s32[32,4]{0,1:T(4,128)}, u32[]{:S(2)}) copy-start(s32[32,4]{0,1:T(4,128)} %param.9) | copy-start | bytes 1540
  139.7 8.3 %copy-start.4 = (f32[32,4]{0,1:T(4,128)S(1)}, f32[32,4]{0,1:T(4,128)}, u32[]{:S(2)}) copy-start(f32[32,4]{0,1:T(4,128)} %param.10) | copy-start | bytes 1540
  139.7 41.5 %all-to-all-start.1 = ((bf16[128,8,1152]{2,1,0:T(8,128)(2,1)}), bf16[128,8,1152]{2,1,0:T(8,128)(2,1)S(1)}, u32[]{:S(2)}, u32[]{:S(2)}) async-start(bf16[128,8,1152]{2,1,0:T(8,128)(2,1)} %bitcast.20), calls=%async_computation.1 | async-start | bytes 4718592 | tf_op jit(solution)/shard_map/all_to_all | solution.py:280

commit v6 on v5

--- a/solution.py
+++ b/solution.py
@@ -71,8 +71,21 @@
     out[...] = (got + extra).astype(BF).T
 
 
-def pick_more_kernel(lay, first, x_ref, row_ref, out):
-    gather_slots(lay, [row_ref[k : k + 1] for k in range(3)], x_ref, first, out)
+def pick_more_kernel(lay, first, x_ref, row_ref, *outs):
+    for out in outs:
+        gather_slots(lay, [row_ref[k : k + 1] for k in range(3)], x_ref, first, out)
+        first += out.shape[1]
+
+
+def joined(refs):
+    return jnp.concatenate([ref[...] for ref in refs], axis=1)
+
+
+def spread_out(values, refs):
+    first = 0
+    for ref in refs:
+        ref[...] = values[:, first : first + ref.shape[1]].astype(ref.dtype)
+        first += ref.shape[1]
 
 
 def pick_kernel(lay, x_ref, par_ref, row_ref, out):
@@ -113,11 +126,13 @@
         do_ref[b] = d_ref[:, at].T
 
 
-def gate_up(at, ahead, wg_ref, wu_ref, blocks):
+def gate_up(at, ahead, wg_ref, wu_ref, refs):
     gate = up = None
-    for distance, x in zip(ahead, blocks):
+    pieces = len(refs) // len(ahead)
+    for n, distance in enumerate(ahead):
         block = lax.rem(at + distance, wg_ref.shape[0])
-        g, u = dot(wg_ref[block], x[...]), dot(wu_ref[block], x[...])
+        x = joined(refs[n * pieces : (n + 1) * pieces])
+        g, u = dot(wg_ref[block], x), dot(wu_ref[block], x)
         gate, up = (g, u) if gate is None else (gate + g, up + u)
     return gate, up
 
@@ -126,23 +141,24 @@
     refs[-2][...], refs[-1][...] = gate_up(at_ref[0], ahead, wg_ref, wu_ref, refs[:-2])
 
 
-def far_kernel(ahead, at_ref, wg_ref, wu_ref, wd_ref, g_ref, u_ref, *refs):
-    gate, up = gate_up(at_ref[0], ahead, wg_ref, wu_ref, refs[:-2])
-    h_ref, o_ref = refs[-2:]
+def far_kernel(ahead, pieces, at_ref, wg_ref, wu_ref, wd_ref, g_ref, u_ref, *refs):
+    ins, h_ref, outs = refs[: -pieces - 1], refs[-pieces - 1], refs[-pieces:]
+    gate, up = gate_up(at_ref[0], ahead, wg_ref, wu_ref, ins)
     gate, up = gate + g_ref[...], up + u_ref[...]
     hidden = (gate * jax.nn.sigmoid(SWISH_SCALE * gate) * (up + 1.0)).astype(BF)
     h_ref[...] = hidden
     groups = wd_ref.shape[0]
     across = lax.rem(at_ref[0] + groups // 2, groups)
-    o_ref[...] = dot(wd_ref[across], hidden).astype(BF)
-
-
-def near_kernel(at_ref, h_ref, wd_ref, *outs):
+    spread_out(dot(wd_ref[across], hidden), outs)
+
+
+def near_kernel(pieces, at_ref, h_ref, wd_ref, own_ref, *outs):
     hidden = h_ref[...]
     groups = wd_ref.shape[0]
-    for distance, out in zip((0, groups - 1, 1), outs):
+    targets = ((0, (own_ref,)), (groups - 1, outs[:pieces]), (1, outs[pieces:]))
+    for distance, refs in targets:
         block = lax.rem(at_ref[0] + distance, groups)
-        out[...] = dot(wd_ref[block], hidden).astype(out.dtype)
+        spread_out(dot(wd_ref[block], hidden), refs)
 
 
 def spots_kernel(row_ref, *outs):
@@ -151,11 +167,13 @@
         out[...] = hot(places[:, k : k + 1], out.shape[1]).astype(BF)
 
 
-def place_kernel(lay, whole_ref, even_ref, odd_ref, *refs):
+def place_kernel(lay, pieces, whole_ref, even_ref, odd_ref, *refs):
     ins, z_ref = refs[:-1], refs[-1]
     columns = []
-    for own, left, right in (ins[:3], ins[3:]):
-        total = own[...] + left[...].astype(F32) + right[...].astype(F32)
+    for count in pieces:
+        own, left, right = ins[0], ins[1 : 1 + count], ins[1 + count : 1 + 2 * count]
+        ins = ins[1 + 2 * count :]
+        total = own[...] + joined(left).astype(F32) + joined(right).astype(F32)
         columns.append(total.astype(BF))
     y = jnp.concatenate(columns, axis=1)
     came = z_ref.shape[0]
@@ -315,6 +333,7 @@
     )(expert_ids.T, gate_probs.T)
     part = slots // 2
     columns = shape((width, part), BF)
+    cuts = (part // 3, part - part // 3)
     gather_work = (2 * slots * came * width, 2 * came * width)
     places, own_a = run(
         lambda *refs: pick_kernel(lay, *refs),
@@ -323,7 +342,10 @@
         gather_work,
     )(arrived, par)
     own_b = run(
-        lambda *refs: pick_more_kernel(lay, part, *refs), [VMEM] * 2, columns, gather_work
+        lambda *refs: pick_more_kernel(lay, part, *refs),
+        [VMEM] * 2,
+        tuple(shape((width, n), BF) for n in cuts),
+        gather_work,
     )(arrived, places)
     spot = shape((came, slots), BF)
     spots = run(spots_kernel, [VMEM], (spot,) * 3, (6 * came * slots, 6 * came * slots))(places)
@@ -336,50 +358,55 @@
             lambda *refs: mid_kernel(ahead, *refs),
             [SMEM] + [VMEM] * (2 + len(blocks)),
             (rows(units, F32), rows(units, F32)),
-            (4 * len(blocks) * part * area, 4 * len(blocks) * area),
+            (4 * len(ahead) * part * area, 4 * len(ahead) * area),
         )(at, wg, wu, *blocks)
 
-    def far(sums, blocks, ahead):
-        count = 4 * len(blocks) + 2
-        return run(
-            lambda *refs: far_kernel(ahead, *refs),
+    def far(sums, blocks, ahead, sizes):
+        count = 4 * len(ahead) + 2
+        hidden, *shares = run(
+            lambda *refs: far_kernel(ahead, len(sizes), *refs),
             [SMEM] + [VMEM] * (5 + len(blocks)),
-            (rows(units, BF), rows(width, BF)),
+            (rows(units, BF), *(shape((width, n), BF) for n in sizes)),
             (count * part * area, count * area),
         )(at, wg, wu, wd, *sums, *blocks)
-
-    def near(hidden, kinds):
-        return run(
-            near_kernel,
+        return hidden, shares
+
+    def near(hidden, kinds, sizes):
+        own, *shares = run(
+            lambda *refs: near_kernel(len(sizes), *refs),
             [SMEM] + [VMEM] * 2,
-            tuple(rows(width, kind) for kind in kinds),
+            (rows(width, F32), *(shape((width, n), kind) for kind in kinds for n in sizes)),
             (6 * part * area, 6 * area),
         )(at, hidden, wd)
+        return own, shares[: len(sizes)], shares[len(sizes) :]
 
     def add(mine, came):
         return (mine + came.astype(F32)).astype(BF)
 
     below_a, above_a = right(own_a), left(own_a)
-    above_b = left(own_b)
+    above_b = [left(own_b[0])]
+    above_b += [left(own_b[1])]
     far_a = right(below_a)
-    below_b = right(own_b)
-    far_b = left(above_b)
+    below_b = [right(piece) for piece in own_b]
+    far_b = [left(above_b[0])]
+    far_b += [left(above_b[1])]
     sums_a = mid((own_a, below_a, above_a), (0, before, after))
-    hidden_a, share_a = far(sums_a, (far_a,), (across,))
+    hidden_a, (share_a,) = far(sums_a, (far_a,), (across,), (part,))
     crossed_a = right(share_a)
-    mine_a, left_a, right_a = near(hidden_a, (F32, BF, F32))
+    mine_a, (left_a,), (right_a,) = near(hidden_a, (BF, F32), (part,))
     from_right_a = left(left_a)
-    sums_b = mid((own_b, above_b), (0, after))
-    hidden_b, share_b = far(sums_b, (below_b, far_b), (before, across))
-    crossed_b = left(share_b)
-    mine_b, left_b, right_b = near(hidden_b, (F32, F32, BF))
-    from_left_b = right(right_b)
-    added_a, added_b = add(right_a, crossed_a), add(left_b, crossed_b)
+    sums_b = mid((*own_b, *above_b), (0, after))
+    hidden_b, share_b = far(sums_b, (*below_b, *far_b), (before, across), cuts)
+    crossed_b = [left(piece) for piece in share_b]
+    mine_b, left_b, right_b = near(hidden_b, (F32, BF), cuts)
+    from_left_b = [right(piece) for piece in right_b]
+    added_a = add(right_a, crossed_a)
+    added_b = [add(mine, came) for mine, came in zip(left_b, crossed_b)]
     from_left_a = right(added_a)
-    from_right_b = left(added_b)
-    sums = (mine_a, from_left_a, from_right_a, mine_b, from_left_b, from_right_b)
+    from_right_b = [left(piece) for piece in added_b]
+    sums = (mine_a, from_left_a, from_right_a, mine_b, *from_left_b, *from_right_b)
     answers = run(
-        lambda *refs: place_kernel(lay, *refs), [VMEM] * 9, packed, gather_work
+        lambda *refs: place_kernel(lay, (1, len(cuts)), *refs), [VMEM] * (3 + len(sums)), packed, gather_work
     )(*spots, *sums)
     return run(
         lambda *refs: mix_kernel(lay, *refs),

time: 183 us -> 187 us (1.022)
  starting transfers between devices: 35.1 us -> 44.6 us
  waiting for transfers between devices: 92.7 us -> 84.2 us
  local copies, waits for them, and re-layouts: 7.19 us -> 9.42 us
    ppermute x12 -> x18, starting transfers between devices: 15.7 us -> 24.9 us  [shifted(): return lambda array: lax.ppermute(array, 'attn', pairs)]
    ppermute x12 -> x18, waiting for transfers between devices: 44.5 us -> 35.7 us  [shifted(): return lambda array: lax.ppermute(array, 'attn', pairs)]
    unnamed x22, local copies, waits for them, and re-layouts: 5.95 us -> 8.21 us
  transfers between devices with their start and end apart: 14 -> 20, of which waited for: 10 -> 7; matrix products, arithmetic and copies ran while one was open for 1% -> 1% of each run, Pallas kernels for 17% -> 18%
where the time goes in v6:
time: 187 us; the launch traced here: 186 us
  waiting for transfers between devices  84.2 us (45%)
  starting transfers between devices  44.6 us (24%)
  Pallas kernels  44.4 us (24%)
  local copies, waits for them, and re-layouts  9.42 us (5%)
  between operations  3.1 us (2%)
    all_to_all x2, waiting for transfers between devices, exchange(): lax.all_to_all(blocks, ATTN_EXPERT, split_axis=0, concat_axis=0, tiled=True)  48.6 us
    ppermute x18, waiting for transfers between devices, shifted(): return lambda array: lax.ppermute(array, 'attn', pairs)  35.7 us
    ppermute x18, starting transfers between devices, shifted(): return lambda array: lax.ppermute(array, 'attn', pairs)  24.9 us
    all_to_all x2, starting transfers between devices, exchange(): lax.all_to_all(blocks, ATTN_EXPERT, split_axis=0, concat_axis=0, tiled=True)  19.6 us
    pallas_call x1, Pallas kernels, on_device(): pl.pallas_call(relay_kernel, grid=(pl.cdiv(units, step),), out_shape=(rel...  13.3 us
    pallas_call x2, Pallas kernels, mid(): run(lambda *refs: mid_kernel(ahead, *refs), [SMEM] + [VMEM] * (2 + len(bl...  8.36 us
    unnamed x22, local copies, waits for them, and re-layouts  8.21 us
    pallas_call x2, Pallas kernels, far(): run(lambda *refs: far_kernel(ahead, len(sizes), *refs), [SMEM] + [VMEM] *...  5.12 us
  transfers between devices with their start and end apart: 20, of which 7 were waited for; matrix products, arithmetic and copies ran while one was open for 1% of the time, Pallas kernels for 18%

profile of v6, /device:TPU:0, one launch (start us, length us, event | category | flops | bytes accessed | tf_op | source)
XLA Modules:
  0.0 186.1 jit_solution(16742258028443136734)
XLA Ops:
  0.0 3.6 %shard_map.82 = (bf16[1024,1152]{1,0:T(8,128)(2,1)}, f32[8,128]{1,0:T(8,128)}) custom-call(bf16[32,2880]{1,0:T(8,128)(2,1)} %refs_0_.1, s32[4,32]{1,0:T(4,128)} %bitcast.21), custom_call_target="tpu_custom_call" | custom-call | flops 47185920 | bytes 1474560 | tf_op jit(solution)/shard_map/pallas_call | solution.py:304
  3.6 11.2 %all-to-all-start = ((bf16[128,8,1152]{2,1,0:T(8,128)(2,1)}), bf16[128,8,1152]{2,1,0:T(8,128)(2,1)S(1)}, u32[]{:S(2)}, u32[]{:S(2)}) async-start(bf16[128,8,1152]{2,1,0:T(8,128)(2,1)} %bitcast.24), calls=%async_computation | async-start | bytes 4718592 | tf_op jit(solution)/shard_map/all_to_all | solution.py:298
  14.8 0.0 copy-done.8
  14.8 0.6 dynamic_slice.9
  17.0 0.7 fusion
  18.9 13.3 %relay.1 = (bf16[4,720,720]{2,1,0:T(8,128)(2,1)}, bf16[4,720,720]{2,1,0:T(8,128)(2,1)}, bf16[4,720,720]{2,1,0:T(8,128)(2,1)}) custom-call(f32[8,128]{1,0:T(8,128)} %get-tuple-element.39.seen_ref, bf16[720,2880]{1,0:T(8,128)(2,1)} %bitcast.25, bf16[720,2880]{1,0:T(8,128)(2,1)} %bitcast.26, bf16[720,2880]{1,0:T(8,128)(2,1)} %bitcast.27), custom_call_target="tpu_custom_call" | custom-call | flops 4777574400 | bytes 24883200 | tf_op jit(solution)/shard_map/relay/pallas_call | solution.py:316
  32.1 15.9 %all-to-all-done = bf16[128,8,1152]{2,1,0:T(8,128)(2,1)S(1)} async-done(((bf16[128,8,1152]{2,1,0:T(8,128)(2,1)}), bf16[128,8,1152]{2,1,0:T(8,128)(2,1)S(1)}, u32[]{:S(2)}, u32[]{:S(2)}) %all-to-all-start) | async-done | bytes 2359328 | tf_op jit(solution)/shard_map/all_to_all | solution.py:298
  48.0 2.2 %shard_map.83 = (f32[8,1024]{1,0:T(8,128)S(1)}, bf16[720,384]{1,0:T(8,128)(2,1)S(1)}) custom-call(bf16[1024,1152]{1,0:T(8,128)(2,1)S(1)} %bitcast.19, s32[1]{0:T(128)S(6)} %add.30.refs_1_), custom_call_target="tpu_custom_call" | custom-call | flops 1132462080 | bytes 1474560 | tf_op jit(solution)/shard_map/pallas_call | solution.py:338
  50.2 0.6 collective-permute-start
  50.8 2.7 %collective-permute-start.1 = (bf16[720,384]{1,0:T(8,128)(2,1)S(1)}, bf16[720,384]{1,0:T(8,128)(2,1)}, u32[]{:S(2)}, u32[]{:S(2)}) collective-permute-start(bf16[720,384]{1,0:T(8,128)(2,1)S(1)} %get-tuple-element.51.refs_3_), channel_id=1, source_target_pairs={{0,96},{32,0},{64,32},{96,64},{1,97},{33,1},{65,33},{97,65},{2,98}... | collective-permute-start | bytes 1658888 | tf_op jit(solution)/shard_map/ppermute | solution.py:292
  53.5 2.1 %shard_map.88 = (bf16[720,128]{1,0:T(8,128)(2,1)}, bf16[720,256]{1,0:T(8,128)(2,1)S(1)}) custom-call(bf16[1024,1152]{1,0:T(8,128)(2,1)S(1)} %bitcast.20, f32[8,1024]{1,0:T(8,128)S(1)} %get-tuple-element.44.row_ref.refs_1_), custom_call_target="tpu_custom_call" | custom-call | flops 1132462080 | bytes 1474560 | tf_op jit(solution)/shard_map/pallas_call | solution.py:344
  55.6 0.0 collective-permute-start.7
  55.6 9.6 %collective-permute-done.refs_4_ = bf16[720,384]{1,0:T(8,128)(2,1)} collective-permute-done((bf16[720,384]{1,0:T(8,128)(2,1)S(1)}, bf16[720,384]{1,0:T(8,128)(2,1)}, u32[]{:S(2)}, u32[]{:S(2)}) %collective-permute-start) | collective-permute-done | bytes 552992 | tf_op jit(solution)/shard_map/ppermute | solution.py:292
  65.3 0.0 collective-permute-start.2
  65.3 3.2 %collective-permute-start.6 = (bf16[720,128]{1,0:T(8,128)(2,1)}, bf16[720,128]{1,0:T(8,128)(2,1)S(1)}, u32[]{:S(2)}, u32[]{:S(2)}) collective-permute-start(bf16[720,128]{1,0:T(8,128)(2,1)} %get-tuple-element.59.refs_3_), channel_id=1, source_target_pairs={{0,96},{32,0},{64,32},{96,64},{1,97},{33,1},{65,33},{97,65},{2,98}... | collective-permute-start | bytes 552968 | tf_op jit(solution)/shard_map/ppermute | solution.py:292
  68.5 0.0 collective-permute-start.9
  68.5 7.9 %collective-permute-done.6.refs_5_ = bf16[720,128]{1,0:T(8,128)(2,1)S(1)} collective-permute-done((bf16[720,128]{1,0:T(8,128)(2,1)}, bf16[720,128]{1,0:T(8,128)(2,1)S(1)}, u32[]{:S(2)}, u32[]{:S(2)}) %collective-permute-start.6) | collective-permute-done | bytes 184352 | tf_op jit(solution)/shard_map/ppermute | solution.py:292
  76.4 0.9 collective-permute-start.8
  77.3 0.0 collective-permute-done.7.refs_6_
  77.3 2.7 %collective-permute-start.10 = (bf16[720,128]{1,0:T(8,128)(2,1)S(1)}, bf16[720,128]{1,0:T(8,128)(2,1)S(1)}, u32[]{:S(2)}, u32[]{:S(2)}) collective-permute-start(bf16[720,128]{1,0:T(8,128)(2,1)S(1)} %collective-permute-done.6.refs_5_), channel_id=1, source_target_pairs={{0,96},{32,0},{64,32},{96,64},{1,97},{33,1},{65,33},{97,65},{2,98}... | collective-permute-start | bytes 552968 | tf_op jit(solution)/shard_map/ppermute | solution.py:292
  80.0 0.0 collective-permute-done.1.refs_5_
  80.0 2.0 %collective-permute-start.11 = (bf16[720,256]{1,0:T(8,128)(2,1)S(1)}, bf16[720,256]{1,0:T(8,128)(2,1)S(1)}, u32[]{:S(2)}, u32[]{:S(2)}) collective-permute-start(bf16[720,256]{1,0:T(8,128)(2,1)S(1)} %collective-permute-done.7.refs_6_), channel_id=1, source_target_pairs={{0,96},{32,0},{64,32},{96,64},{1,97},{33,1},{65,33},{97,65},{2,98}... | collective-permute-start | bytes 1105928 | tf_op jit(solution)/shard_map/ppermute | solution.py:292
  82.0 2.3 %copy-done = bf16[4,720,720]{2,1,0:T(8,128)(2,1)S(1)} copy-done((bf16[4,720,720]{2,1,0:T(8,128)(2,1)S(1)}, bf16[4,720,720]{2,1,0:T(8,128)(2,1)}, u32[]{:S(2)}) %copy-start) | copy-done | bytes 4147224
  84.3 2.3 %copy-done.1 = bf16[4,720,720]{2,1,0:T(8,128)(2,1)S(1)} copy-done((bf16[4,720,720]{2,1,0:T(8,128)(2,1)S(1)}, bf16[4,720,720]{2,1,0:T(8,128)(2,1)}, u32[]{:S(2)}) %copy-start.1) | copy-done | bytes 4147224
  86.5 5.0 %shard_map.85 = (f32[720,384]{1,0:T(8,128)S(1)}, f32[720,384]{1,0:T(8,128)S(1)}) custom-call(s32[1]{0:T(128)} %bitcast.9.refs_0_, bf16[4,720,720]{2,1,0:T(8,128)(2,1)S(1)} %copy-done, bf16[4,720,720]{2,1,0:T(8,128)(2,1)S(1)} %copy-done.1, bf16[720,384]{1,0:T(8,128)(2,1)S(1)} %get-tuple-element.51.refs_3_, bf16[720,384]{1,0:T(8,128)(2,1)} %collective-permute-done.refs_4_, ...), custom_call_target="tpu_custom_call" | custom-call | flops 2388787200 | bytes 6220800 | tf_op jit(solution)/shard_map/pallas_call | solution.py:357
  91.5 0.0 collective-permute-done.2.refs_6_
  91.6 2.2 %copy-done.3 = bf16[4,720,720]{2,1,0:T(8,128)(2,1)S(1)} copy-done((bf16[4,720,720]{2,1,0:T(8,128)(2,1)S(1)}, bf16[4,720,720]{2,1,0:T(8,128)(2,1)}, u32[]{:S(2)}) %copy-start.3) | copy-done | bytes 4147224
  93.8 1.9 %shard_map.86 = (bf16[720,384]{1,0:T(8,128)(2,1)S(1)}, bf16[720,384]{1,0:T(8,128)(2,1)S(1)}) custom-call(s32[1]{0:T(128)} %bitcast.9.refs_0_, bf16[4,720,720]{2,1,0:T(8,128)(2,1)S(1)} %bitcast.16, bf16[4,720,720]{2,1,0:T(8,128)(2,1)S(1)} %copy-done.2, bf16[4,720,720]{2,1,0:T(8,128)(2,1)S(1)} %copy-done.3, f32[720,384]{1,0:T(8,128)S(1)} %get-tuple-element.52.refs_4_, ...), custom_call_target="tpu_custom_call" | custom-call | flops 1194393600 | bytes 3110400 | tf_op jit(solution)/shard_map/pallas_call | solution.py:366
  95.8 0.1 collective-permute-start.3
  95.9 3.4 %shard_map.89 = (f32[720,384]{1,0:T(8,128)S(1)}, f32[720,384]{1,0:T(8,128)S(1)}) custom-call(s32[1]{0:T(128)} %bitcast.9.refs_0_, bf16[4,720,720]{2,1,0:T(8,128)(2,1)S(1)} %bitcast.16, bf16[4,720,720]{2,1,0:T(8,128)(2,1)S(1)} %copy-done.2, bf16[720,128]{1,0:T(8,128)(2,1)} %get-tuple-element.59.refs_3_, bf16[720,256]{1,0:T(8,128)(2,1)S(1)} %get-tuple-element.60.refs_4_, ...), custom_call_target="tpu_custom_call" | custom-call | flops 1592524800 | bytes 4147200 | tf_op jit(solution)/shard_map/pallas_call | solution.py:357
  99.2 0.0 collective-permute-done.8.refs_6_
  99.3 0.0 collective-permute-done.10.refs_8_
  99.3 0.0 collective-permute-done.9.refs_7_
  99.3 0.0 collective-permute-done.11.refs_9_
  99.3 3.2 %shard_map.90 = (bf16[720,384]{1,0:T(8,128)(2,1)S(1)}, bf16[720,128]{1,0:T(8,128)(2,1)S(1)}, bf16[720,256]{1,0:T(8,128)(2,1)S(1)}) custom-call(s32[1]{0:T(128)} %bitcast.9.refs_0_, bf16[4,720,720]{2,1,0:T(8,128)(2,1)S(1)} %bitcast.16, bf16[4,720,720]{2,1,0:T(8,128)(2,1)S(1)} %copy-done.2, bf16[4,720,720]{2,1,0:T(8,128)(2,1)S(1)} %copy-done.3, ...), custom_call_target="tpu_custom_call" | custom-call | flops 1990656000 | bytes 5184000 | tf_op jit(solution)/shard_map/pallas_call | solution.py:366
  102.5 3.3 %collective-permute-start.16 = (bf16[720,256]{1,0:T(8,128)(2,1)S(1)}, bf16[720,256]{1,0:T(8,128)(2,1)S(1)}, u32[]{:S(2)}, u32[]{:S(2)}) collective-permute-start(bf16[720,256]{1,0:T(8,128)(2,1)S(1)} %get-tuple-element.70), channel_id=1, source_target_pairs={{0,96},{32,0},{64,32},{96,64},{1,97},{33,1},{65,33},{97,65},{2,98}... | collective-permute-start | bytes 1105928 | tf_op jit(solution)/shard_map/ppermute | solution.py:292
  105.7 0.1 collective-permute-start.14
  105.8 1.9 %shard_map.91 = (f32[720,384]{1,0:T(8,128)S(1)}, f32[720,128]{1,0:T(8,128)S(1)}, f32[720,256]{1,0:T(8,128)S(1)}, bf16[720,128]{1,0:T(8,128)(2,1)S(1)}, bf16[720,256]{1,0:T(8,128)(2,1)S(1)}) custom-call(s32[1]{0:T(128)} %bitcast.9.refs_0_, bf16[720,384]{1,0:T(8,128)(2,1)S(1)} %get-tuple-element.63.refs_1_, bf16[4,720,720]{2,1,0:T(8,128)(2,1)S(1)} %copy-done.3), custom_call_target="tpu_custom_call" | custom-call | flops 1194393600 | bytes 3110400 | tf_op jit(solution)/shard_map/pallas_call | solution.py:375
  107.7 2.0 %collective-permute-start.13 = (bf16[720,256]{1,0:T(8,128)(2,1)S(1)}, bf16[720,256]{1,0:T(8,128)(2,1)S(1)}, u32[]{:S(2)}, u32[]{:S(2)}) collective-permute-start(bf16[720,256]{1,0:T(8,128)(2,1)S(1)} %get-tuple-element.66), channel_id=1, source_target_pairs={{0,32},{32,64},{64,96},{96,0},{1,33},{33,65},{65,97},{97,1},{2,34}... | collective-permute-start | bytes 1105928 | tf_op jit(solution)/shard_map/ppermute | solution.py:292
  109.7 0.1 collective-permute-start.12
  109.8 1.9 %shard_map.87 = (f32[720,384]{1,0:T(8,128)S(1)}, bf16[720,384]{1,0:T(8,128)(2,1)S(1)}, f32[720,384]{1,0:T(8,128)S(1)}) custom-call(s32[1]{0:T(128)} %bitcast.9.refs_0_, bf16[720,384]{1,0:T(8,128)(2,1)S(1)} %get-tuple-element.54.refs_1_, bf16[4,720,720]{2,1,0:T(8,128)(2,1)S(1)} %copy-done.3), custom_call_target="tpu_custom_call" | custom-call | flops 1194393600 | bytes 3110400 | tf_op jit(solution)/shard_map/pallas_call | solution.py:375
  111.7 0.0 collective-permute-done.3
  111.7 3.4 %collective-permute-start.5 = (bf16[720,384]{1,0:T(8,128)(2,1)S(1)}, bf16[720,384]{1,0:T(8,128)(2,1)S(1)}, u32[]{:S(2)}, u32[]{:S(2)}) collective-permute-start(bf16[720,384]{1,0:T(8,128)(2,1)S(1)} %get-tuple-element.58), channel_id=1, source_target_pairs={{0,96},{32,0},{64,32},{96,64},{1,97},{33,1},{65,33},{97,65},{2,98}... | collective-permute-start | bytes 1658888 | tf_op jit(solution)/shard_map/ppermute | solution.py:292
  115.1 0.1 add_convert_fusion
  115.3 0.0 collective-permute-done.16
  115.3 0.1 collective-permute-start.4
  115.4 0.1 add_convert_fusion.1
  115.5 2.8 %collective-permute-done.14 = bf16[720,128]{1,0:T(8,128)(2,1)S(1)} collective-permute-done((bf16[720,128]{1,0:T(8,128)(2,1)S(1)}, bf16[720,128]{1,0:T(8,128)(2,1)S(1)}, u32[]{:S(2)}, u32[]{:S(2)}) %collective-permute-start.14) | collective-permute-done | bytes 184352 | tf_op jit(solution)/shard_map/ppermute | solution.py:292
  118.3 3.7 %collective-permute-start.17 = (bf16[720,256]{1,0:T(8,128)(2,1)S(1)}, bf16[720,256]{1,0:T(8,128)(2,1)S(1)}, u32[]{:S(2)}, u32[]{:S(2)}) collective-permute-start(bf16[720,256]{1,0:T(8,128)(2,1)S(1)} %add_convert_fusion.1), channel_id=1, source_target_pairs={{0,96},{32,0},{64,32},{96,64},{1,97},{33,1},{65,33},{97,65},{2,98}... | collective-permute-start | bytes 1105928 | tf_op jit(solution)/shard_map/ppermute | solution.py:292
  122.0 0.1 add_convert_fusion.2
  122.0 2.4 %collective-permute-done.12.refs_7_ = bf16[720,128]{1,0:T(8,128)(2,1)S(1)} collective-permute-done((bf16[720,128]{1,0:T(8,128)(2,1)S(1)}, bf16[720,128]{1,0:T(8,128)(2,1)S(1)}, u32[]{:S(2)}, u32[]{:S(2)}) %collective-permute-start.12) | collective-permute-done | bytes 184352 | tf_op jit(solution)/shard_map/ppermute | solution.py:292
  124.4 0.0 collective-permute-start.15
  124.4 1.0 shard_map.84
  125.4 13.0 %collective-permute-done.15.refs_9_ = bf16[720,128]{1,0:T(8,128)(2,1)S(1)} collective-permute-done((bf16[720,128]{1,0:T(8,128)(2,1)S(1)}, bf16[720,128]{1,0:T(8,128)(2,1)S(1)}, u32[]{:S(2)}, u32[]{:S(2)}) %collective-permute-start.15) | collective-permute-done | bytes 184352 | tf_op jit(solution)/shard_map/ppermute | solution.py:292
  138.4 0.0 collective-permute-done.13.refs_8_
  138.4 0.0 collective-permute-done.17.refs_10_
  138.4 0.0 collective-permute-done.5.refs_5_
  138.4 0.0 collective-permute-done.4.refs_4_
  138.4 3.1 %shard_map.92 = bf16[1024,1152]{1,0:T(8,128)(2,1)S(1)} custom-call(bf16[1024,768]{1,0:T(8,128)(2,1)S(1)} %get-tuple-element.45.refs_0_, bf16[1024,768]{1,0:T(8,128)(2,1)S(1)} %get-tuple-element.46.refs_1_, bf16[1024,768]{1,0:T(8,128)(2,1)S(1)} %get-tuple-element.47.refs_2_, f32[720,384]{1,0:T(8,128)S(1)} %get-tuple-element.55.refs_3_, ...), custom_call_target="tpu_custom_call" | custom-call | flops 1132462080 | bytes 1474560 | tf_op jit(solution)/shard_map/pallas_call | solution.py:408
  141.6 1.4 copy-done.4
  143.0 8.5 %all-to-all-start.1 = ((bf16[128,8,1152]{2,1,0:T(8,128)(2,1)}), bf16[128,8,1152]{2,1,0:T(8,128)(2,1)S(1)}, u32[]{:S(2)}, u32[]{:S(2)}) async-start(bf16[128,8,1152]{2,1,0:T(8,128)(2,1)} %bitcast.18), calls=%async_computation.1 | async-start | bytes 4718592 | tf_op jit(solution)/shard_map/all_to_all | solution.py:298
  151.5 0.5 shard_map.93.refs_1_
  152.0 32.7 %all-to-all-done.1 = bf16[128,8,1152]{2,1,0:T(8,128)(2,1)S(1)} async-done(((bf16[128,8,1152]{2,1,0:T(8,128)(2,1)}), bf16[128,8,1152]{2,1,0:T(8,128)(2,1)S(1)}, u32[]{:S(2)}, u32[]{:S(2)}) %all-to-all-start.1) | async-done | bytes 2359328 | tf_op jit(solution)/shard_map/all_to_all | solution.py:298
  184.7 1.4 shard_map.94
  (18 shorter events, 0.0 us)
Async XLA Ops:
  3.6 11.2 %copy-start.8 = (s32[32]{0:T(128)S(1)}, s32[32]{0:T(128)}, u32[]{:S(2)}) copy-start(s32[32]{0:T(128)} %param.12) | copy-start | bytes 388
  3.6 13.4 %copy-start.7 = (s32[32]{0:T(128)S(1)}, s32[32]{0:T(128)}, u32[]{:S(2)}) copy-start(s32[32]{0:T(128)} %param.11) | copy-start | bytes 388
  3.6 44.4 %all-to-all-start = ((bf16[128,8,1152]{2,1,0:T(8,128)(2,1)}), bf16[128,8,1152]{2,1,0:T(8,128)(2,1)S(1)}, u32[]{:S(2)}, u32[]{:S(2)}) async-start(bf16[128,8,1152]{2,1,0:T(8,128)(2,1)} %bitcast.24), calls=%async_computation | async-start | bytes 4718592 | tf_op jit(solution)/shard_map/all_to_all | solution.py:298
  50.2 15.1 %collective-permute-start = (bf16[720,384]{1,0:T(8,128)(2,1)S(1)}, bf16[720,384]{1,0:T(8,128)(2,1)}, u32[]{:S(2)}, u32[]{:S(2)}) collective-permute-start(bf16[720,384]{1,0:T(8,128)(2,1)S(1)} %get-tuple-element.51.refs_3_), channel_id=1, source_target_pairs={{0,32},{32,64},{64,96},{96,0},{1,33},{33,65},{65,97},{97,1},{2,34}... | collective-permute-start | bytes 1658888 | tf_op jit(solution)/shard_map/ppermute | solution.py:292
  50.8 29.2 %collective-permute-start.1 = (bf16[720,384]{1,0:T(8,128)(2,1)S(1)}, bf16[720,384]{1,0:T(8,128)(2,1)}, u32[]{:S(2)}, u32[]{:S(2)}) collective-permute-start(bf16[720,384]{1,0:T(8,128)(2,1)S(1)} %get-tuple-element.51.refs_3_), channel_id=1, source_target_pairs={{0,96},{32,0},{64,32},{96,64},{1,97},{33,1},{65,33},{97,65},{2,98}... | collective-permute-start | bytes 1658888 | tf_op jit(solution)/shard_map/ppermute | solution.py:292
  53.5 38.0 %slice-start = ((s8[4423680]{0:T(1024)(128)(4,1)}), s8[229376]{0:T(1024)(128)(4,1)S(1)}, s32[]{:S(2)}) async-start(s8[4423680]{0:T(1024)(128)(4,1)} %bitcast.15), calls=%async_computation.2 | async-start | bytes 458752
  55.6 21.7 %collective-permute-start.7 = (bf16[720,256]{1,0:T(8,128)(2,1)S(1)}, bf16[720,256]{1,0:T(8,128)(2,1)S(1)}, u32[]{:S(2)}, u32[]{:S(2)}) collective-permute-start(bf16[720,256]{1,0:T(8,128)(2,1)S(1)} %get-tuple-element.60.refs_4_), channel_id=1, source_target_pairs={{0,96},{32,0},{64,32},{96,64},{1,97},{33,1},{65,33},{97,65},{2,98}... | collective-permute-start | bytes 1105928 | tf_op jit(solution)/shard_map/ppermute | solution.py:292
  65.3 26.2 %collective-permute-start.2 = (bf16[720,384]{1,0:T(8,128)(2,1)}, bf16[720,384]{1,0:T(8,128)(2,1)S(1)}, u32[]{:S(2)}, u32[]{:S(2)}) collective-permute-start(bf16[720,384]{1,0:T(8,128)(2,1)} %collective-permute-done.refs_4_), channel_id=1, source_target_pairs={{0,32},{32,64},{64,96},{96,0},{1,33},{33,65},{65,97},{97,1},{2,34}... | collective-permute-start | bytes 1658888 | tf_op jit(solution)/shard_map/ppermute | solution.py:292
  65.3 11.1 %collective-permute-start.6 = (bf16[720,128]{1,0:T(8,128)(2,1)}, bf16[720,128]{1,0:T(8,128)(2,1)S(1)}, u32[]{:S(2)}, u32[]{:S(2)}) collective-permute-start(bf16[720,128]{1,0:T(8,128)(2,1)} %get-tuple-element.59.refs_3_), channel_id=1, source_target_pairs={{0,96},{32,0},{64,32},{96,64},{1,97},{33,1},{65,33},{97,65},{2,98}... | collective-permute-start | bytes 552968 | tf_op jit(solution)/shard_map/ppermute | solution.py:292
  68.5 30.7 %collective-permute-start.9 = (bf16[720,256]{1,0:T(8,128)(2,1)S(1)}, bf16[720,256]{1,0:T(8,128)(2,1)S(1)}, u32[]{:S(2)}, u32[]{:S(2)}) collective-permute-start(bf16[720,256]{1,0:T(8,128)(2,1)S(1)} %get-tuple-element.60.refs_4_), channel_id=1, source_target_pairs={{0,32},{32,64},{64,96},{96,0},{1,33},{33,65},{65,97},{97,1},{2,34}... | collective-permute-start | bytes 1105928 | tf_op jit(solution)/shard_map/ppermute | solution.py:292
  76.4 22.8 %collective-permute-start.8 = (bf16[720,128]{1,0:T(8,128)(2,1)}, bf16[720,128]{1,0:T(8,128)(2,1)S(1)}, u32[]{:S(2)}, u32[]{:S(2)}) collective-permute-start(bf16[720,128]{1,0:T(8,128)(2,1)} %get-tuple-element.59.refs_3_), channel_id=1, source_target_pairs={{0,32},{32,64},{64,96},{96,0},{1,33},{33,65},{65,97},{97,1},{2,34}... | collective-permute-start | bytes 552968 | tf_op jit(solution)/shard_map/ppermute | solution.py:292
  77.3 22.0 %collective-permute-start.10 = (bf16[720,128]{1,0:T(8,128)(2,1)S(1)}, bf16[720,128]{1,0:T(8,128)(2,1)S(1)}, u32[]{:S(2)}, u32[]{:S(2)}) collective-permute-start(bf16[720,128]{1,0:T(8,128)(2,1)S(1)} %collective-permute-done.6.refs_5_), channel_id=1, source_target_pairs={{0,96},{32,0},{64,32},{96,64},{1,97},{33,1},{65,33},{97,65},{2,98}... | collective-permute-start | bytes 552968 | tf_op jit(solution)/shard_map/ppermute | solution.py:292
  80.0 19.3 %collective-permute-start.11 = (bf16[720,256]{1,0:T(8,128)(2,1)S(1)}, bf16[720,256]{1,0:T(8,128)(2,1)S(1)}, u32[]{:S(2)}, u32[]{:S(2)}) collective-permute-start(bf16[720,256]{1,0:T(8,128)(2,1)S(1)} %collective-permute-done.7.refs_6_), channel_id=1, source_target_pairs={{0,96},{32,0},{64,32},{96,64},{1,97},{33,1},{65,33},{97,65},{2,98}... | collective-permute-start | bytes 1105928 | tf_op jit(solution)/shard_map/ppermute | solution.py:292
  82.0 2.3 %copy-start = (bf16[4,720,720]{2,1,0:T(8,128)(2,1)S(1)}, bf16[4,720,720]{2,1,0:T(8,128)(2,1)}, u32[]{:S(2)}) copy-start(bf16[4,720,720]{2,1,0:T(8,128)(2,1)} %get-tuple-element.48.refs_1_) | copy-start | bytes 12441604
  84.3 2.3 %copy-start.1 = (bf16[4,720,720]{2,1,0:T(8,128)(2,1)S(1)}, bf16[4,720,720]{2,1,0:T(8,128)(2,1)}, u32[]{:S(2)}) copy-start(bf16[4,720,720]{2,1,0:T(8,128)(2,1)} %get-tuple-element.49.refs_2_) | copy-start | bytes 12441604
  86.5 5.0 %slice-start.1 = ((s8[4423680]{0:T(1024)(128)(4,1)}), s8[4194304]{0:T(1024)(128)(4,1)S(1)}, s32[]{:S(2)}) async-start(s8[4423680]{0:T(1024)(128)(4,1)} %bitcast.15), calls=%async_computation.3 | async-start | bytes 8388608
  86.5 5.0 %copy-start.2 = (bf16[4,720,720]{2,1,0:T(8,128)(2,1)S(1)}, bf16[4,720,720]{2,1,0:T(8,128)(2,1)}, u32[]{:S(2)}) copy-start(bf16[4,720,720]{2,1,0:T(8,128)(2,1)} %get-tuple-element.49.refs_2_) | copy-start | bytes 12441604
  91.6 2.3 %copy-start.3 = (bf16[4,720,720]{2,1,0:T(8,128)(2,1)S(1)}, bf16[4,720,720]{2,1,0:T(8,128)(2,1)}, u32[]{:S(2)}) copy-start(bf16[4,720,720]{2,1,0:T(8,128)(2,1)} %get-tuple-element.50.refs_3_.refs_2_) | copy-start | bytes 12441604
  95.8 15.9 %collective-permute-start.3 = (bf16[720,384]{1,0:T(8,128)(2,1)S(1)}, bf16[720,384]{1,0:T(8,128)(2,1)S(1)}, u32[]{:S(2)}, u32[]{:S(2)}) collective-permute-start(bf16[720,384]{1,0:T(8,128)(2,1)S(1)} %get-tuple-element.57), channel_id=1, source_target_pairs={{0,32},{32,64},{64,96},{96,0},{1,33},{33,65},{65,97},{97,1},{2,34}... | collective-permute-start | bytes 1658888 | tf_op jit(solution)/shard_map/ppermute | solution.py:292
  102.5 12.8 %collective-permute-start.16 = (bf16[720,256]{1,0:T(8,128)(2,1)S(1)}, bf16[720,256]{1,0:T(8,128)(2,1)S(1)}, u32[]{:S(2)}, u32[]{:S(2)}) collective-permute-start(bf16[720,256]{1,0:T(8,128)(2,1)S(1)} %get-tuple-element.70), channel_id=1, source_target_pairs={{0,96},{32,0},{64,32},{96,64},{1,97},{33,1},{65,33},{97,65},{2,98}... | collective-permute-start | bytes 1105928 | tf_op jit(solution)/shard_map/ppermute | solution.py:292
  105.7 12.5 %collective-permute-start.14 = (bf16[720,128]{1,0:T(8,128)(2,1)S(1)}, bf16[720,128]{1,0:T(8,128)(2,1)S(1)}, u32[]{:S(2)}, u32[]{:S(2)}) collective-permute-start(bf16[720,128]{1,0:T(8,128)(2,1)S(1)} %get-tuple-element.68), channel_id=1, source_target_pairs={{0,96},{32,0},{64,32},{96,64},{1,97},{33,1},{65,33},{97,65},{2,98}... | collective-permute-start | bytes 552968 | tf_op jit(solution)/shard_map/ppermute | solution.py:292
  107.7 30.7 %collective-permute-start.13 = (bf16[720,256]{1,0:T(8,128)(2,1)S(1)}, bf16[720,256]{1,0:T(8,128)(2,1)S(1)}, u32[]{:S(2)}, u32[]{:S(2)}) collective-permute-start(bf16[720,256]{1,0:T(8,128)(2,1)S(1)} %get-tuple-element.66), channel_id=1, source_target_pairs={{0,32},{32,64},{64,96},{96,0},{1,33},{33,65},{65,97},{97,1},{2,34}... | collective-permute-start | bytes 1105928 | tf_op jit(solution)/shard_map/ppermute | solution.py:292
  109.7 14.7 %collective-permute-start.12 = (bf16[720,128]{1,0:T(8,128)(2,1)S(1)}, bf16[720,128]{1,0:T(8,128)(2,1)S(1)}, u32[]{:S(2)}, u32[]{:S(2)}) collective-permute-start(bf16[720,128]{1,0:T(8,128)(2,1)S(1)} %get-tuple-element.65), channel_id=1, source_target_pairs={{0,32},{32,64},{64,96},{96,0},{1,33},{33,65},{65,97},{97,1},{2,34}... | collective-permute-start | bytes 552968 | tf_op jit(solution)/shard_map/ppermute | solution.py:292
  111.7 26.7 %collective-permute-start.5 = (bf16[720,384]{1,0:T(8,128)(2,1)S(1)}, bf16[720,384]{1,0:T(8,128)(2,1)S(1)}, u32[]{:S(2)}, u32[]{:S(2)}) collective-permute-start(bf16[720,384]{1,0:T(8,128)(2,1)S(1)} %get-tuple-element.58), channel_id=1, source_target_pairs={{0,96},{32,0},{64,32},{96,64},{1,97},{33,1},{65,33},{97,65},{2,98}... | collective-permute-start | bytes 1658888 | tf_op jit(solution)/shard_map/ppermute | solution.py:292
  115.3 23.1 %collective-permute-start.4 = (bf16[720,384]{1,0:T(8,128)(2,1)S(1)}, bf16[720,384]{1,0:T(8,128)(2,1)S(1)}, u32[]{:S(2)}, u32[]{:S(2)}) collective-permute-start(bf16[720,384]{1,0:T(8,128)(2,1)S(1)} %add_convert_fusion), channel_id=1, source_target_pairs={{0,32},{32,64},{64,96},{96,0},{1,33},{33,65},{65,97},{97,1},{2,34}... | collective-permute-start | bytes 1658888 | tf_op jit(solution)/shard_map/ppermute | solution.py:292
  118.3 20.1 %collective-permute-start.17 = (bf16[720,256]{1,0:T(8,128)(2,1)S(1)}, bf16[720,256]{1,0:T(8,128)(2,1)S(1)}, u32[]{:S(2)}, u32[]{:S(2)}) collective-permute-start(bf16[720,256]{1,0:T(8,128)(2,1)S(1)} %add_convert_fusion.1), channel_id=1, source_target_pairs={{0,96},{32,0},{64,32},{96,64},{1,97},{33,1},{65,33},{97,65},{2,98}... | collective-permute-start | bytes 1105928 | tf_op jit(solution)/shard_map/ppermute | solution.py:292
  124.4 14.0 %collective-permute-start.15 = (bf16[720,128]{1,0:T(8,128)(2,1)S(1)}, bf16[720,128]{1,0:T(8,128)(2,1)S(1)}, u32[]{:S(2)}, u32[]{:S(2)}) collective-permute-start(bf16[720,128]{1,0:T(8,128)(2,1)S(1)} %add_convert_fusion.2), channel_id=1, source_target_pairs={{0,96},{32,0},{64,32},{96,64},{1,97},{33,1},{65,33},{97,65},{2,98}... | collective-permute-start | bytes 552968 | tf_op jit(solution)/shard_map/ppermute | solution.py:292
  141.6 1.4 copy-start.4
  143.0 8.5 %copy-start.5 = (s32[32,4]{0,1:T(4,128)S(1)}, s32[32,4]{0,1:T(4,128)}, u32[]{:S(2)}) copy-start(s32[32,4]{0,1:T(4,128)} %param.9) | copy-start | bytes 1540
  143.0 8.5 %copy-start.6 = (f32[32,4]{0,1:T(4,128)S(1)}, f32[32,4]{0,1:T(4,128)}, u32[]{:S(2)}) copy-start(f32[32,4]{0,1:T(4,128)} %param.10) | copy-start | bytes 1540
  143.0 41.7 %all-to-all-start.1 = ((bf16[128,8,1152]{2,1,0:T(8,128)(2,1)}), bf16[128,8,1152]{2,1,0:T(8,128)(2,1)S(1)}, u32[]{:S(2)}, u32[]{:S(2)}) async-start(bf16[128,8,1152]{2,1,0:T(8,128)(2,1)} %bitcast.18), calls=%async_computation.1 | async-start | bytes 4718592 | tf_op jit(solution)/shard_map/all_to_all | solution.py:298
